TPU v7x, 32 devices: a whole 2x2x4 slice. The times are simulated.
32 devices in a mesh: dp: 8 (over y, x, core), tile: 4 (over z).
Axes of the slice: x: 2, y: 2, z: 4, core: 2. Of those that a mesh axis runs over, the one named last changes fastest.
Arguments:
- frames: bfloat16 [4, 3, 16, 16, 1024], P('tile', None, None, None, 'dp'), may hold values from -9 to 9
- weights: bfloat16 [4, 64, 8, 972], P('tile'), may hold values from -0.1875 to 0.1875
- connect: int32 [4, 64, 8, 3], P('tile'), may hold values 0 or 1
Outputs:
- update: bfloat16 [4, 64, 8, 972], P('tile')
- loss_value: float32 [], replicated
All inputs are finite; a program needn't handle non-finite values. No bound on the sum of `connect` on one device may be relied on, other than what follows from the above.
Results may differ from a plain program's by a relative error of at most 0.008.
Values may be sent and summed in bfloat16 or wider, within the bound.
No kernel may reach another device: no remote copies, remote signals or barrier semaphores. Data moves between devices by JAX's collectives and lax.ppermute only.
A program may use at most 64 MiB of HBM per device.

v0:
```python
import math

import jax
import jax.numpy as jnp
from jax import lax
from jax.sharding import PartitionSpec as P

FIELD = 18
MAPS = 8
STRIDE = 2
TILE_PX = 16
INPUTS = 972
HALO = 16
POS = 64


sparsity_weight = 1.0
smooth_eps = 0.01
guard_eps = 1e-06


def from_behind(value, axis, steps):
    count = lax.axis_size(axis)
    pairs = [(source, (source + steps) % count) for source in range(count)]
    return lax.ppermute(value, axis, pairs)


def masked(values, connect):
    blocked = values.reshape(values.shape[0], values.shape[1], MAPS, 3, FIELD * FIELD)
    opened = connect.astype(values.dtype)[..., None]
    return (blocked * opened).reshape(values.shape)


def patch_block(extended, row_index):
    strip_rows = lax.dynamic_slice_in_dim(extended, row_index * STRIDE, FIELD, 1)
    pieces = [
        strip_rows[:, :, column * STRIDE : column * STRIDE + FIELD]
        for column in range(TILE_PX // STRIDE)
    ]
    blocks = jnp.stack(pieces, 0)
    return blocks.reshape(blocks.shape[0], INPUTS, blocks.shape[-1])


def spread(coeffs, span_px):
    shaped = coeffs.reshape(coeffs.shape[0], 3, FIELD, FIELD, coeffs.shape[-1])
    canvas_strip = jnp.zeros((3, FIELD, span_px, coeffs.shape[-1]), jnp.float32)
    for column in range(TILE_PX // STRIDE):
        canvas_strip = canvas_strip.at[:, :, column * STRIDE : column * STRIDE + FIELD].add(
            shaped[column]
        )
    return canvas_strip


def extend(frame_tile, side_tiles):
    from_right = from_behind(frame_tile, "tile", -1)
    wide_tile = jnp.concatenate([frame_tile, from_right], axis=2)
    from_below = from_behind(wide_tile, "tile", -side_tiles)
    return jnp.concatenate([wide_tile, from_below], axis=1)


def fold_spill(canvas_part, side_tiles):
    from_above = from_behind(
        canvas_part[:, TILE_PX:].astype(jnp.bfloat16), "tile", side_tiles
    ).astype(jnp.float32)
    upper_rows = canvas_part[:, :TILE_PX].at[:, :HALO].add(from_above)
    from_left = from_behind(upper_rows[:, :, TILE_PX:], "tile", 1)
    return upper_rows[:, :, :TILE_PX].at[:, :, :HALO].add(from_left)


def local(frames, weights, connect):
    batch_cols = frames.shape[-1]
    side_tiles = math.isqrt(lax.axis_size("tile"))
    rows_out = TILE_PX // STRIDE
    span_px = TILE_PX + HALO
    effective = masked(weights, connect)[0].reshape(rows_out, rows_out, MAPS, INPUTS)
    frame_tile = frames[0]
    ext_frames = extend(frame_tile, side_tiles)

    def encode_row(canvas_part, row_index):
        blocks = patch_block(ext_frames, row_index)
        w_row = effective[row_index]
        coded = jnp.einsum("cmk,ckb->cmb", w_row, blocks, preferred_element_type=jnp.float32)
        rounded = coded.astype(jnp.bfloat16)
        decoded = jnp.einsum("cmk,cmb->ckb", w_row, rounded, preferred_element_type=jnp.float32)
        start = row_index * STRIDE
        window = lax.dynamic_slice_in_dim(canvas_part, start, FIELD, 1)
        canvas_part = lax.dynamic_update_slice_in_dim(
            canvas_part, window + spread(decoded, span_px), start, 1
        )
        return (canvas_part, coded)

    canvas_part, coded_all = lax.scan(
        encode_row,
        jnp.zeros((3, span_px, span_px, batch_cols), jnp.float32),
        jnp.arange(rows_out, dtype=jnp.int32),
    )
    own_recon = fold_spill(canvas_part, side_tiles)
    errors = own_recon - frame_tile.astype(jnp.float32)
    error_sq = jnp.sum(errors * errors)
    sparse = jnp.sum(jnp.sqrt(smooth_eps + coded_all * coded_all))
    ext_errors = extend(errors.astype(jnp.bfloat16), side_tiles)

    def grad_row(inner, pair):
        row_index, coded = pair
        frame_block = patch_block(ext_frames, row_index)
        error_block = patch_block(ext_errors, row_index)
        w_row = effective[row_index]
        encoded_err = jnp.einsum(
            "cmk,ckb->cmb", w_row, error_block, preferred_element_type=jnp.float32
        )
        left_coef = (2.0 * coded).astype(jnp.bfloat16)
        right_coef = (
            2.0 * encoded_err + sparsity_weight * coded / jnp.sqrt(smooth_eps + coded * coded)
        ).astype(jnp.bfloat16)
        result = jnp.einsum(
            "cmb,ckb->cmk", left_coef, error_block, preferred_element_type=jnp.float32
        )
        result = result + jnp.einsum(
            "cmb,ckb->cmk", right_coef, frame_block, preferred_element_type=jnp.float32
        )
        return (inner, result)

    inner, grad_rows = lax.scan(
        grad_row, jnp.zeros((), jnp.float32), (jnp.arange(rows_out, dtype=jnp.int32), coded_all)
    )
    gradients = masked(grad_rows.reshape(1, POS, MAPS, INPUTS), connect)[0]
    entries = lax.axis_size("tile") * POS * MAPS * INPUTS
    error_tot, sparse_tot = lax.psum((error_sq, sparse), ("dp", "tile"))
    summed = lax.psum(gradients, "dp")
    square = jnp.sum(summed * summed)
    square = lax.psum(square, "tile")
    factor = lax.rsqrt(square / entries + guard_eps)
    update = (-(summed * factor)).astype(jnp.bfloat16)
    loss_value = (error_tot + sparsity_weight * sparse_tot) / (batch_cols * lax.axis_size("dp"))
    return (update[None], loss_value)


def solution(mesh):
    placed = (
        P("tile", None, None, None, "dp"),
        P("tile", None, None, None),
        P("tile", None, None, None),
    )
    return jax.shard_map(
        local,
        mesh=mesh,
        in_specs=placed,
        out_specs=(P("tile", None, None, None), P()),
        check_vma=False,
    )
```

profile of v0, /device:TPU:0, one launch (start us, length us, event | category | flops | bytes accessed | tf_op | source)
XLA Modules:
  0.0 976.1 jit_solution(11298144664080681925)
XLA Ops:
  24.6 12.7 %collective-permute-done.1 = bf16[3,16,32,128]{3,2,1,0:T(8,128)(2,1)} collective-permute-done((bf16[3,16,32,128]{3,2,1,0:T(8,128)(2,1)S(1)}, bf16[3,16,32,128]{3,2,1,0:T(8,128)(2,1)}, u32[]{:S(2)}, u32[]{:S(2)}) %collective-permute-start.1) | collective-permute-done | bytes 393248 | tf_op jit(solution)/shard_map/ppermute | solution.py:25
  39.8 477.6 %while.37 = (s32[]{:T(128)}, f32[3,32,32,128]{3,2,1,0:T(8,128)}, f32[8,8,8,128]{3,2,1,0:T(8,128)}, s32[8]{0:T(128)S(1)}, bf16[8,8,8,972]{3,2,1,0:T(8,128)(2,1)},...) while((s32[]{:T(128)}, f32[3,32,32,128]{3,2,1,0:T(8,128)}, ...), condition=%wide.region_1.0_spmd, body=%wide.region_0.1_spmd.sunk | while | flops 32950800 | bytes 56633848 | solution.py:92
  60.0 6.0 scatter-add.57
  67.2 6.0 scatter-add.60
  112.5 6.0 scatter-add.54
  119.7 6.0 scatter-add.57
  126.9 6.0 scatter-add.60
  172.2 6.0 scatter-add.54
  179.4 6.0 scatter-add.57
  231.9 6.0 scatter-add.54
  291.6 6.0 scatter-add.54
  358.5 6.0 scatter-add.57
  365.7 6.0 scatter-add.60
  411.0 6.0 scatter-add.54
  418.2 6.0 scatter-add.57
  425.5 6.0 scatter-add.60
  477.9 6.0 scatter-add.57
  518.7 18.8 %collective-permute-done.2 = bf16[3,16,32,128]{3,2,1,0:T(8,128)(2,1)S(1)} collective-permute-done((bf16[3,16,32,128]{3,2,1,0:T(8,128)(2,1)S(1)}, bf16[3,16,32,128]{3,2,1,0:T(8,128)(2,1)S(1)}, u32[]{:S(2)}, u32[]{:S(2)}) %collective-permute-start.2) | collective-permute-done | bytes 393248 | tf_op jit(solution)/shard_map/ppermute | solution.py:25
  538.9 11.7 %collective-permute-done.3 = f32[3,16,16,128]{3,2,1,0:T(8,128)S(1)} collective-permute-done((f32[3,16,16,128]{3,2,1,0:T(8,128)S(1)}, f32[3,16,16,128]{3,2,1,0:T(8,128)S(1)}, u32[]{:S(2)}, u32[]{:S(2)}) %collective-permute-start.3) | collective-permute-done | bytes 393248 | tf_op jit(solution)/shard_map/ppermute | solution.py:25
  564.1 10.2 %collective-permute-done.5 = bf16[3,16,32,128]{3,2,1,0:T(8,128)(2,1)S(1)} collective-permute-done((bf16[3,16,32,128]{3,2,1,0:T(8,128)(2,1)S(1)}, bf16[3,16,32,128]{3,2,1,0:T(8,128)(2,1)S(1)}, u32[]{:S(2)}, u32[]{:S(2)}) %collective-permute-start.5) | collective-permute-done | bytes 393248 | tf_op jit(solution)/shard_map/ppermute | solution.py:25
  574.3 309.8 %while.38 = (s32[]{:T(128)}, f32[8,8,8,972]{3,2,1,0:T(8,128)}, f32[8,8,8,128]{3,2,1,0:T(8,128)}, s32[8]{0:T(128)S(1)}, bf16[3,32,32,128]{3,2,1,0:T(8,128)(2,1)S(...) while((s32[]{:T(128)}, f32[8,8,8,972]{3,2,1,0:T(8,128)}, ...), condition=%wide.region_3.0_spmd, body=%wide.region_2.0_spmd.sunk | while | flops 47903504 | bytes 60725572 | solution.py:123
  891.1 38.8 %psum.32 = f32[]{:T(128)} all-reduce(f32[]{:T(128)S(6)} %add.178), channel_id=1, replica_groups=mesh['dp'=8,'tile'=4] {'dp','tile'}, use_global_device_ids=true, to_apply=%region_8.0 | all-reduce | flops 1 | bytes 8 | tf_op jit(solution)/shard_map/psum | solution.py:128
  929.9 20.5 %all-reduce.3.cloned.1.call-done = f32[64,8,972]{2,1,0:T(8,128)} async-done(((f32[64,8,972]{2,1,0:T(8,128)}), f32[64,8,972]{2,1,0:T(8,128)}) %all-reduce.3.cloned.1.call-update) | async-done | bytes 1990672 | tf_op jit(solution)/shard_map/psum | solution.py:129
  953.9 12.2 %psum.29 = f32[]{:T(128)} all-reduce(f32[]{:T(128)} %multiply_reduce_fusion), channel_id=1, replica_groups=mesh['dp'=8,'tile'=4] {'tile'}, use_global_device_ids=true, to_apply=%region_6.0 | all-reduce | flops 1 | bytes 8 | tf_op jit(solution)/shard_map/psum | solution.py:131
  (952 shorter events, 697.2 us)
Async XLA Ops:
  7.2 943.2 %all-reduce.3.cloned.1.call-start = ((), (), s32[]{:S(2)}) async-start(), calls=%async_computation | async-start | bytes 4194304 | tf_op jit(solution)/shard_map/psum | solution.py:129
  7.2 9.6 collective-permute-start
  16.8 5.1 copy-start.21
  17.8 19.5 %collective-permute-start.1 = (bf16[3,16,32,128]{3,2,1,0:T(8,128)(2,1)S(1)}, bf16[3,16,32,128]{3,2,1,0:T(8,128)(2,1)}, u32[]{:S(2)}, u32[]{:S(2)}) collective-permute-start(bf16[3,16,32,128]{3,2,1,0:T(8,128)(2,1)S(1)} %pad_maximum_fusion.2), channel_id=1, source_target_pairs={{0,2},{1,3},{2,0},{3,1},{4,6},{5,7},{6,4},{7,5},{8,10},{9,11},{10,... | collective-permute-start | bytes 1179656 | tf_op jit(solution)/shard_map/ppermute | solution.py:25
  22.0 15.4 %copy-start.18 = (bf16[1,3,16,16,128]{4,3,2,1,0:T(8,128)(2,1)S(1)}, bf16[1,3,16,16,128]{4,3,2,1,0:T(8,128)(2,1)}, u32[]{:S(2)}) copy-start(bf16[1,3,16,16,128]{4,3,2,1,0:T(8,128)(2,1)} %param.31) | copy-start | bytes 589828
  22.0 15.4 %copy-start.22 = (bf16[3,16,16,128]{3,2,1,0:T(8,128)(2,1)S(1)}, bf16[3,16,16,128]{3,2,1,0:T(8,128)(2,1)}, u32[]{:S(2)}) copy-start(bf16[3,16,16,128]{3,2,1,0:T(8,128)(2,1)} %copy-done.21) | copy-start | bytes 589828
  517.4 33.2 %copy-start.19 = (bf16[1,3,16,16,128]{4,3,2,1,0:T(8,128)(2,1)S(1)}, bf16[1,3,16,16,128]{4,3,2,1,0:T(8,128)(2,1)}, u32[]{:S(2)}) copy-start(bf16[1,3,16,16,128]{4,3,2,1,0:T(8,128)(2,1)} %param.31) | copy-start | bytes 589828
  518.6 18.9 %collective-permute-start.2 = (bf16[3,16,32,128]{3,2,1,0:T(8,128)(2,1)S(1)}, bf16[3,16,32,128]{3,2,1,0:T(8,128)(2,1)S(1)}, u32[]{:S(2)}, u32[]{:S(2)}) collective-permute-start(bf16[3,16,32,128]{3,2,1,0:T(8,128)(2,1)S(1)} %slice.516), channel_id=1, source_target_pairs={{0,2},{1,3},{2,0},{3,1},{4,6},{5,7},{6,4},{7,5},{8,10},{9,11},{10,... | collective-permute-start | bytes 1179656 | tf_op jit(solution)/shard_map/ppermute | solution.py:25
  538.8 11.8 %collective-permute-start.3 = (f32[3,16,16,128]{3,2,1,0:T(8,128)S(1)}, f32[3,16,16,128]{3,2,1,0:T(8,128)S(1)}, u32[]{:S(2)}, u32[]{:S(2)}) collective-permute-start(f32[3,16,16,128]{3,2,1,0:T(8,128)S(1)} %slice.499), channel_id=1, source_target_pairs={{0,1},{1,2},{2,3},{3,0},{4,5},{5,6},{6,7},{7,4},{8,9},{9,10},{10,1... | collective-permute-start | bytes 1179656 | tf_op jit(solution)/shard_map/ppermute | solution.py:25
  551.3 5.7 collective-permute-start.4
  557.0 17.2 %collective-permute-start.5 = (bf16[3,16,32,128]{3,2,1,0:T(8,128)(2,1)S(1)}, bf16[3,16,32,128]{3,2,1,0:T(8,128)(2,1)S(1)}, u32[]{:S(2)}, u32[]{:S(2)}) collective-permute-start(bf16[3,16,32,128]{3,2,1,0:T(8,128)(2,1)S(1)} %pad_maximum_fusion.3), channel_id=1, source_target_pairs={{0,2},{1,3},{2,0},{3,1},{4,6},{5,7},{6,4},{7,5},{8,10},{9,11},{10,... | collective-permute-start | bytes 1179656 | tf_op jit(solution)/shard_map/ppermute | solution.py:25
  601.0 3.4 copy-start.16
  601.8 2.7 copy-start.14
  639.7 3.4 copy-start.16
  640.5 2.7 copy-start.14
  678.4 3.4 copy-start.16
  679.2 2.7 copy-start.14
  717.1 3.4 copy-start.16
  717.9 2.7 copy-start.14
  755.9 3.4 copy-start.16
  794.6 3.4 copy-start.16
  833.3 3.4 copy-start.16
  872.0 3.4 copy-start.16
  950.4 16.5 %copy-start.17 = (f32[64,8,972]{2,1,0:T(8,128)S(1)}, f32[64,8,972]{2,1,0:T(8,128)}, u32[]{:S(2)}) copy-start(f32[64,8,972]{2,1,0:T(8,128)} %all-reduce.3.cloned.1.call-done) | copy-start | bytes 5971972
  (125 other events, 165.9 us)
Sparse Core Ops, SparseCore 0:
  888.4 61.9 all-reduce.2
where the time goes:
time: 984 us; the launch traced here: 976 us
  local copies, waits for them, and re-layouts  656 us (67%)
  waiting for transfers between devices  83.5 us (8%)
  matrix products  73 us (7%)
  blocking collectives  51.1 us (5%)
  loops' own time  46.2 us (5%)
  other arithmetic  40.9 us (4%)
  between operations  17.9 us (2%)
    scatter-add x64, local copies, waits for them, and re-layouts, spread(): canvas_strip.at[:, :, column * STRIDE:column * STRIDE + FIELD]  306 us
    another operation x216, local copies, waits for them, and re-layouts, patch_block(): blocks = jnp.stack(pieces, 0)  197 us
    ppermute x6, waiting for transfers between devices, from_behind(): return lax.ppermute(value, axis, pairs)  63 us
    another operation x56, local copies, waits for them, and re-layouts  43.8 us
    while x440, local copies, waits for them, and re-layouts  40.9 us
    psum x1, blocking collectives, local(): error_tot, sparse_tot = lax.psum((error_sq, sparse), ('dp', 'tile'))  38.8 us
    slice x16, local copies, waits for them, and re-layouts, patch_block(): strip_rows[:, :, column * STRIDE:column * STRIDE + FIELD]  32.8 us
    dot_general x8, matrix products, grad_row(): jnp.einsum('cmb,ckb->cmk', right_coef, frame_block, preferred_element_typ...  32 us
  transfers between devices with their start and end apart: 7, of which 7 were waited for; matrix products, arithmetic and copies ran while one was open for 1% of the time, Pallas kernels for 0%

commit v1 on v0

v1 whole, which is shorter than its diff:
```python
import math

import jax
import jax.numpy as jnp
from jax import lax
from jax.experimental import pallas as pl
from jax.experimental.pallas import tpu as pltpu
from jax.sharding import PartitionSpec as P

FIELD = 18
MAPS = 8
STRIDE = 2
TILE_PX = 16
INPUTS = 972
HALO = 16
POS = 64
SPAN = TILE_PX + HALO
SIDE_POS = TILE_PX // STRIDE
UNITS = POS * MAPS
PLANE = SPAN * SPAN
PATCH = FIELD * FIELD
LANES = 128
PAD_IN = -(-INPUTS // LANES) * LANES
STRIP = FIELD * SPAN
PAD_STRIP = -(-STRIP // LANES) * LANES
ROLL_W = PAD_STRIP + LANES
GRAB = 512
STEP_IN = 256

sparsity_weight = 1.0
smooth_eps = 0.01
guard_eps = 1e-06

BF = jnp.bfloat16
F32 = jnp.float32
VMEM_CAP = 40 * 1024 * 1024


def shift_by(value, axis, steps):
    count = lax.axis_size(axis)
    return lax.ppermute(value, axis, [(s, (s + steps) % count) for s in range(count)])


def swap_with(value, axis, flip):
    count = lax.axis_size(axis)
    return lax.ppermute(value, axis, [(s, s ^ flip) for s in range(count)])


def kernel_call(body, outs, scratch=(), scalars=0, n_in=0, flops=0, name=None):
    return pl.pallas_call(
        body,
        out_shape=outs,
        in_specs=[pl.BlockSpec(memory_space=pltpu.SMEM)] * scalars
        + [pl.BlockSpec(memory_space=pltpu.VMEM)] * n_in,
        out_specs=jax.tree.map(lambda _: pl.BlockSpec(memory_space=pltpu.VMEM), outs),
        scratch_shapes=list(scratch),
        compiler_params=pltpu.CompilerParams(vmem_limit_bytes=VMEM_CAP),
        cost_estimate=pl.CostEstimate(flops=flops, transcendentals=0, bytes_accessed=flops // 256),
        name=name,
    )


def positions():
    for i in range(SIDE_POS):
        for j in range(0, SIDE_POS, 2):
            lead = (i * STRIDE * SPAN) // LANES * LANES
            rest = i * STRIDE * SPAN - lead
            shifts = [rest + STRIDE * j, rest + STRIDE * (j + 1)]
            yield (i * SIDE_POS + j) * MAPS, lead, shifts


def place(dst, a, b, c, d):
    for ch in range(3):
        dst[ch, :TILE_PX, :TILE_PX] = a[ch]
        dst[ch, :TILE_PX, TILE_PX:] = b[ch]
        dst[ch, TILE_PX:, :TILE_PX] = c[ch]
        dst[ch, TILE_PX:, TILE_PX:] = d[ch]


def expand_body(w_ref, con_ref, wd_ref, wt_ref, wp_ref, v_ref, s_ref):
    wp_ref[:, PAD_IN - LANES :] = jnp.zeros((UNITS, LANES), BF)
    wp_ref[:, :INPUTS] = w_ref[...]
    n = lax.broadcasted_iota(jnp.int32, (1, PAD_STRIP), 1)
    row, col = n // SPAN, n % SPAN
    inside = (col < FIELD) & (row < FIELD)
    k = lax.broadcasted_iota(jnp.int32, (GRAB, PAD_STRIP), 0)
    v_ref[:, PAD_STRIP:] = jnp.zeros((UNITS, LANES), F32)
    for ch in range(3):
        want = jnp.where(inside, row * FIELD + col + ch * (PATCH - STEP_IN), -1)
        s_ref[...] = jnp.where(k == want, 1.0, 0.0).astype(BF)
        v = jnp.dot(
            wp_ref[:, ch * STEP_IN : ch * STEP_IN + GRAB], s_ref[...], preferred_element_type=F32
        )
        v_ref[:, :PAD_STRIP] = v * con_ref[:, ch : ch + 1]
        base = ch * PLANE
        for u, lead, shifts in positions():
            parts = []
            for h, s in enumerate(shifts):
                blk = v_ref[u + h * MAPS : u + (h + 1) * MAPS, :]
                parts.append(pltpu.roll(blk, s, 1) if s else blk)
            both = jnp.concatenate(parts, 0).astype(BF)
            width = min(ROLL_W, PLANE - lead)
            rows = slice(u, u + 2 * MAPS)
            if lead:
                wd_ref[rows, base : base + lead] = jnp.zeros((2 * MAPS, lead), BF)
            wd_ref[rows, base + lead : base + lead + width] = both[:, :width]
            left = PLANE - lead - width
            if left:
                wd_ref[rows, base + PLANE - left : base + PLANE] = jnp.zeros((2 * MAPS, left), BF)
        for kb in range(base, base + PLANE, LANES):
            wt_ref[kb : kb + LANES, :] = wd_ref[:, kb : kb + LANES].T


def encode_body(x0, x1, x2, x3, wd_ref, wt_ref, coded_ref, own_ref, r_ref, b_ref, c_ref, sp_ref, xe):
    place(xe, x0, x1, x2, x3)
    batch = x0.shape[-1]
    coded = jnp.dot(wd_ref[...], xe[...].reshape(3 * PLANE, batch), preferred_element_type=F32)
    coded_ref[...] = coded
    sparse = jnp.sqrt(smooth_eps + coded * coded)
    sp_ref[...] = jnp.sum(sparse.reshape(UNITS // 8, 8, batch), 0)
    rounded = coded.astype(BF)
    half = PLANE // 2
    for ch in range(3):
        for low in range(2):
            at = ch * PLANE + low * half
            part = jnp.dot(wt_ref[at : at + half, :], rounded, preferred_element_type=F32)
            part = part.reshape(TILE_PX, SPAN, batch)
            if low:
                b_ref[ch] = part[:, :TILE_PX].astype(BF)
                c_ref[ch] = part[:, TILE_PX:].astype(BF)
            else:
                own_ref[ch] = part[:, :TILE_PX]
                r_ref[ch] = part[:, TILE_PX:].astype(BF)


def error_body(own, fr, fb, fc, x, sp, e_ref, loss_ref):
    batch = x.shape[-1]
    total = sp[...] * sparsity_weight
    for ch in range(3):
        err = own[ch] + fr[ch].astype(F32) + fb[ch].astype(F32) + fc[ch].astype(F32)
        err = err - x[ch].astype(F32)
        e_ref[ch] = err.astype(BF)
        total = total + jnp.sum((err * err).reshape(TILE_PX * TILE_PX // 8, 8, batch), 0)
    loss_ref[...] = total


def grad_body(
    half_ref, wd_ref, coded_ref, x0, x1, x2, x3, e0, e1, e2, e3, con_ref,
    keep_ref, send_ref, ex, lr, gd, gs, st, out,
):
    batch = x0.shape[-1]
    place(ex.at[:, :, :, :batch], e0, e1, e2, e3)
    place(ex.at[:, :, :, batch:], x0, x1, x2, x3)
    e_all = ex[:, :, :, :batch].reshape(3 * PLANE, batch)
    enc = jnp.dot(wd_ref[...], e_all, preferred_element_type=F32)
    coded = coded_ref[...]
    lr[:, :batch] = (2.0 * coded).astype(BF)
    right = 2.0 * enc + sparsity_weight * coded / jnp.sqrt(smooth_eps + coded * coded)
    lr[:, batch:] = right.astype(BF)
    n = lax.broadcasted_iota(jnp.int32, (PAD_STRIP, 1), 0)
    row, col = n // SPAN, n % SPAN
    inside = (col < FIELD) & (row < FIELD)
    k = lax.broadcasted_iota(jnp.int32, (PAD_STRIP, GRAB), 1)
    out[...] = jnp.zeros((UNITS, PAD_IN), F32)
    for ch in range(3):
        pixels = ex[ch].reshape(PLANE, 2 * batch)
        gd[...] = lax.dot_general(
            lr[...], pixels, (((1,), (1,)), ((), ())), preferred_element_type=F32
        )
        want = jnp.where(inside, row * FIELD + col + ch * (PATCH - STEP_IN), -1)
        st[...] = jnp.where(k == want, 1.0, 0.0).astype(BF)
        for u, lead, shifts in positions():
            width = min(ROLL_W, PLANE - lead)
            parts = []
            for h, s in enumerate(shifts):
                blk = gd[u + h * MAPS : u + (h + 1) * MAPS, lead : lead + width]
                blk = pltpu.roll(blk, width - s, 1) if s else blk
                parts.append(blk[:, :PAD_STRIP])
            gs[u : u + 2 * MAPS, :] = jnp.concatenate(parts, 0).astype(BF)
        cols = slice(ch * STEP_IN, ch * STEP_IN + GRAB)
        out[:, cols] = out[:, cols] + jnp.dot(gs[...], st[...], preferred_element_type=F32)
    lane = lax.broadcasted_iota(jnp.int32, (1, PAD_IN), 1)
    con = con_ref[...]
    opened = jnp.where(
        lane < PATCH, con[:, 0:1], jnp.where(lane < 2 * PATCH, con[:, 1:2], con[:, 2:3])
    )
    out[...] = out[...] * opened
    rows = UNITS // 2
    mine = pl.multiple_of(half_ref[0] * rows, rows)
    other = pl.multiple_of((1 - half_ref[0]) * rows, rows)
    keep_ref[...] = out[pl.ds(mine, rows), :]
    send_ref[...] = out[pl.ds(other, rows), :].astype(BF)


def pair_body(chip_ref, keep, got, *refs):
    own_ref, sends, scr = refs[0], refs[1:-1], refs[-1]
    rows = own_ref.shape[0]
    scr[...] = keep[...] + got[...].astype(F32)
    chip = chip_ref[0]
    own_ref[...] = scr[pl.ds(pl.multiple_of(chip * rows, rows), rows), :]
    for x, ref in enumerate(sends):
        at = pl.multiple_of((chip ^ (x + 1)) * rows, rows)
        ref[...] = scr[pl.ds(at, rows), :].astype(BF)


def shard_body(own, *refs):
    got, loss, shard_ref, tally_ref = refs[:-3], refs[-3], refs[-2], refs[-1]
    total = own[...]
    for ref in got:
        total = total + ref[...].astype(F32)
    shard_ref[...] = total.astype(BF)
    rows, width = total.shape
    sq = jnp.sum((total * total).reshape(rows // 8, 8, width), 0)
    folded = sq[:, :LANES]
    for at in range(LANES, width, LANES):
        folded = folded + sq[:, at : at + LANES]
    tally_ref[:8] = loss[...]
    tally_ref[8:] = folded


def gather_body(chip_ref, own, *refs):
    got, half_ref = refs[:-1], refs[-1]
    rows = own.shape[0]
    chip = chip_ref[0]
    half_ref[pl.ds(pl.multiple_of(chip * rows, rows), rows), :] = own[...]
    for x, ref in enumerate(got):
        at = pl.multiple_of((chip ^ (x + 1)) * rows, rows)
        half_ref[pl.ds(at, rows), :] = ref[...]


def finish_body(entries, frames_total, half_ref, mine, other, ta, tb, up_ref, loss_ref):
    tally = ta[...] + tb[...]
    square = jnp.sum(jnp.sum(tally[8:], 0, keepdims=True), 1, keepdims=True)
    factor = lax.rsqrt(square / entries + guard_eps)
    rows = mine.shape[0]
    at = pl.multiple_of(half_ref[0] * rows, rows)
    up_ref[pl.ds(at, rows), :] = (-(mine[:, :INPUTS].astype(F32) * factor)).astype(BF)
    at = pl.multiple_of((1 - half_ref[0]) * rows, rows)
    up_ref[pl.ds(at, rows), :] = (-(other[:, :INPUTS].astype(F32) * factor)).astype(BF)
    loss = jnp.sum(jnp.sum(tally[:8], 0, keepdims=True), 1, keepdims=True) / frames_total
    loss_ref[...] = jnp.broadcast_to(loss, loss_ref.shape)


def local(frames, weights, connect):
    batch = frames.shape[-1]
    n_tile = lax.axis_size("tile")
    n_dp = lax.axis_size("dp")
    side = math.isqrt(n_tile)
    chips = n_dp // 2
    index = lax.axis_index("dp")
    core = (index % 2).astype(jnp.int32).reshape(1)
    chip = (index // 2).astype(jnp.int32).reshape(1)
    sds = jax.ShapeDtypeStruct
    dense_flops = 2 * UNITS * 3 * PLANE * batch

    x0 = frames[0]
    steps = (1, side, side + 1)
    xs = [shift_by(x0, "tile", -s) for s in steps]

    con = connect.reshape(UNITS, 3).astype(F32)
    wd, wt = kernel_call(
        expand_body,
        (sds((UNITS, 3 * PLANE), BF), sds((3 * PLANE, UNITS), BF)),
        [pltpu.VMEM((UNITS, PAD_IN), BF), pltpu.VMEM((UNITS, ROLL_W), F32), pltpu.VMEM((GRAB, PAD_STRIP), BF)],
        n_in=2, flops=4 * dense_flops, name="expand",
    )(weights.reshape(UNITS, INPUTS), con)

    quad = (3, TILE_PX, TILE_PX, batch)
    coded, own, sr, sb, sc, sparse = kernel_call(
        encode_body,
        (sds((UNITS, batch), F32), sds(quad, F32), sds(quad, BF), sds(quad, BF), sds(quad, BF), sds((8, batch), F32)),
        [pltpu.VMEM((3, SPAN, SPAN, batch), BF)],
        n_in=6, flops=2 * dense_flops, name="encode",
    )(x0, *xs, wd, wt)

    back = [shift_by(v, "tile", s) for v, s in zip((sr, sb, sc), steps)]
    e0, loss_part = kernel_call(
        error_body, (sds(quad, BF), sds((8, batch), F32)), n_in=6, flops=dense_flops // 8, name="errors"
    )(own, *back, x0, sparse)
    es = [shift_by(e0, "tile", -s) for s in steps]

    half = UNITS // 2
    keep, send = kernel_call(
        grad_body,
        (sds((half, PAD_IN), F32), sds((half, PAD_IN), BF)),
        [
            pltpu.VMEM((3, SPAN, SPAN, 2 * batch), BF),
            pltpu.VMEM((UNITS, 2 * batch), BF),
            pltpu.VMEM((UNITS, PLANE), F32),
            pltpu.VMEM((UNITS, PAD_STRIP), BF),
            pltpu.VMEM((PAD_STRIP, GRAB), BF),
            pltpu.VMEM((UNITS, PAD_IN), F32),
        ],
        scalars=1, n_in=11, flops=4 * dense_flops, name="grads",
    )(core, wd, coded, x0, *xs, e0, *es, con)

    got = swap_with(send, "dp", 1)
    rows = half // chips
    shard = sds((rows, PAD_IN), BF)
    split = kernel_call(
        pair_body,
        (sds((rows, PAD_IN), F32),) + (shard,) * (chips - 1),
        [pltpu.VMEM((half, PAD_IN), F32)],
        scalars=1, n_in=2, flops=dense_flops // 8, name="pair",
    )(chip, keep, got)
    arrived = [swap_with(v, "dp", 2 * (x + 1)) for x, v in enumerate(split[1:])]
    mine, tally = kernel_call(
        shard_body, (shard, sds((16, LANES), F32)), n_in=chips + 1, flops=dense_flops // 16, name="shard"
    )(split[0], *arrived, loss_part)

    others = [swap_with(mine, "dp", 2 * x) for x in range(1, chips)]
    tally = tally + sum(shift_by(tally, "tile", s) for s in range(1, n_tile))
    tally = tally + sum(swap_with(tally, "dp", 2 * x) for x in range(1, chips))
    tally_b = swap_with(tally, "dp", 1)
    mine_half = kernel_call(
        gather_body, sds((half, PAD_IN), BF), scalars=1, n_in=chips, flops=dense_flops // 16, name="gather"
    )(chip, mine, *others)
    other_half = swap_with(mine_half, "dp", 1)

    entries = n_tile * POS * MAPS * INPUTS
    update, loss = kernel_call(
        lambda *refs: finish_body(float(entries), float(batch * n_dp), *refs),
        (sds((UNITS, INPUTS), BF), sds((8, LANES), F32)),
        scalars=1, n_in=4, flops=dense_flops // 8, name="finish",
    )(core, mine_half, other_half, tally, tally_b)
    return update.reshape(1, POS, MAPS, INPUTS), loss[0, 0]


def solution(mesh):
    placed = (
        P("tile", None, None, None, "dp"),
        P("tile", None, None, None),
        P("tile", None, None, None),
    )
    return jax.shard_map(
        local,
        mesh=mesh,
        in_specs=placed,
        out_specs=(P("tile", None, None, None), P()),
        check_vma=False,
    )
```

time: 984 us -> 116 us (0.12)
  local copies, waits for them, and re-layouts: 656 us -> 7.65 us
  matrix products: 73 us -> 0 us
  blocking collectives: 51.1 us -> 0 us
  loops' own time: 46.2 us -> 0 us
  other arithmetic: 40.9 us -> 0.72 us
  waiting for transfers between devices: 83.5 us -> 56.5 us
  starting transfers between devices: 7.3 us -> 33.2 us
  between operations: 17.9 us -> 0.73 us
  Pallas kernels: 0 us -> 17.1 us
    scatter-add x64 -> x0, local copies, waits for them, and re-layouts: 306 us -> none  [spread(): canvas_strip.at[:, :, column * STRIDE:column * STRIDE + FIELD]]
    another operation x272 -> x0, local copies, waits for them, and re-layouts: 241 us -> none  [the longest x216 197 us: patch_block(): blocks = jnp.stack(pieces, 0)]
    dot_general x32 -> x0, matrix products: 73 us -> none  [the longest x8 32 us: grad_row(): jnp.einsum('cmb,ckb->cmk', right_coef, frame_block, preferred_element_typ...]
    psum x2 -> x0, blocking collectives: 51.1 us -> none  [the longest x1 38.8 us: local(): error_tot, sparse_tot = lax.psum((error_sq, sparse), ('dp', 'tile'))]
    another operation x2 -> x0, loops' own time: 46.2 us -> none  [the longest x1 23.8 us: local(): lax.scan(grad_row, jnp.zeros((), jnp.float32), (jnp.arange(rows_out, dtyp...]
    slice x26 -> x1, local copies, waits for them, and re-layouts: 46 us -> 0.51 us  [local(): return (update.reshape(1, POS, MAPS, INPUTS), loss[0, 0])]
    while x440 -> x0, local copies, waits for them, and re-layouts: 40.9 us -> none
    ppermute x6 -> x24, starting transfers between devices: 7.27 us -> 33.2 us  [the longest x12 22.5 us: shift_by(): lax.ppermute(value, axis, [(s, (s + steps) % count) for s in range(count)])]
  transfers between devices with their start and end apart: 7 -> 24, of which waited for: 7 -> 16; matrix products, arithmetic and copies ran while one was open for 1% -> 1% of each run, Pallas kernels for 0% -> 2%
where the time goes in v1:
time: 116 us
  waiting for transfers between devices  56.5 us (49%)
  starting transfers between devices  33.2 us (29%)
  Pallas kernels  17.1 us (15%)
  local copies, waits for them, and re-layouts  7.65 us (7%)
    ppermute x12, waiting for transfers between devices, shift_by(): lax.ppermute(value, axis, [(s, (s + steps) % count) for s in range(count)])  39 us
    ppermute x12, starting transfers between devices, shift_by(): lax.ppermute(value, axis, [(s, (s + steps) % count) for s in range(count)])  22.5 us
    ppermute x12, waiting for transfers between devices, swap_with(): return lax.ppermute(value, axis, [(s, s ^ flip) for s in range(count)])  17.5 us
    ppermute x12, starting transfers between devices, swap_with(): return lax.ppermute(value, axis, [(s, s ^ flip) for s in range(count)])  10.7 us
    pallas_call x1, Pallas kernels, local(): kernel_call(grad_body, (sds((half, PAD_IN), F32), sds((half, PAD_IN), BF)...  7.19 us
    unnamed x16, local copies, waits for them, and re-layouts  6.28 us
    pallas_call x1, Pallas kernels, local(): kernel_call(encode_body, (sds((UNITS, batch), F32), sds(quad, F32), sds(q...  4.52 us
    pallas_call x1, Pallas kernels, local(): kernel_call(expand_body, (sds((UNITS, 3 * PLANE), BF), sds((3 * PLANE, UN...  2.85 us
  transfers between devices with their start and end apart: 24, of which 16 were waited for; matrix products, arithmetic and copies ran while one was open for 1% of the time, Pallas kernels for 2%

profile of v1, /device:TPU:0, one launch (start us, length us, event | category | flops | bytes accessed | tf_op | source)
XLA Modules:
  0.0 115.9 jit_solution(10665166522691229527)
XLA Ops:
  0.6 5.1 %collective-permute-start = (bf16[3,16,16,128]{3,2,1,0:T(8,128)(2,1)}, bf16[3,16,16,128]{3,2,1,0:T(8,128)(2,1)S(1)}, u32[]{:S(2)}, u32[]{:S(2)}) collective-permute-start(bf16[3,16,16,128]{3,2,1,0:T(8,128)(2,1)} %bitcast.7), channel_id=1, source_target_pairs={{0,3},{1,0},{2,1},{3,2},{4,7},{5,4},{6,5},{7,6},{8,11},{9,8},{10,9... | collective-permute-start | bytes 589832 | tf_op jit(solution)/shard_map/ppermute | solution.py:41
  10.5 2.8 %expand.1 = (bf16[512,3072]{1,0:T(8,128)(2,1)S(1)}, bf16[3072,512]{1,0:T(8,128)(2,1)S(1)}) custom-call(bf16[512,972]{1,0:T(8,128)(2,1)S(1)} %bitcast.15, f32[512,3]{1,0:T(8,128)S(1)} %bitcast.13), custom_call_target="tpu_custom_call" | custom-call | flops 1610612736 | bytes 6291456 | tf_op jit(solution)/shard_map/expand/pallas_call | solution.py:261
  13.4 9.4 %collective-permute-done.1.x2 = bf16[3,16,16,128]{3,2,1,0:T(8,128)(2,1)} collective-permute-done((bf16[3,16,16,128]{3,2,1,0:T(8,128)(2,1)}, bf16[3,16,16,128]{3,2,1,0:T(8,128)(2,1)}, u32[]{:S(2)}, u32[]{:S(2)}) %collective-permute-start.1) | collective-permute-done | bytes 196640 | tf_op jit(solution)/shard_map/ppermute | solution.py:41
  22.8 4.5 %encode.1 = (f32[512,128]{1,0:T(8,128)S(1)}, f32[3,16,16,128]{3,2,1,0:T(8,128)S(1)}, bf16[3,16,16,128]{3,2,1,0:T(8,128)(2,1)S(1)}, bf16[3,16,16,128]{3,2,1,0:T(8...) custom-call(bf16[3,16,16,128]{3,2,1,0:T(8,128)(2,1)S(1)} %bitcast.10, ...), custom_call_target="tpu_custom_call" | custom-call | flops 805306368 | bytes 3145728 | tf_op jit(solution)/shard_map/encode/pallas_call | solution.py:269
  28.3 2.0 %collective-permute-start.4 = (bf16[3,16,16,128]{3,2,1,0:T(8,128)(2,1)S(1)}, bf16[3,16,16,128]{3,2,1,0:T(8,128)(2,1)S(1)}, u32[]{:S(2)}, u32[]{:S(2)}) collective-permute-start(bf16[3,16,16,128]{3,2,1,0:T(8,128)(2,1)S(1)} %get-tuple-element.27), channel_id=1, source_target_pairs={{0,2},{1,3},{2,0},{3,1},{4,6},{5,7},{6,4},{7,5},{8,10},{9,11},{10,... | collective-permute-start | bytes 589832 | tf_op jit(solution)/shard_map/ppermute | solution.py:41
  30.2 2.8 %collective-permute-start.5 = (bf16[3,16,16,128]{3,2,1,0:T(8,128)(2,1)S(1)}, bf16[3,16,16,128]{3,2,1,0:T(8,128)(2,1)S(1)}, u32[]{:S(2)}, u32[]{:S(2)}) collective-permute-start(bf16[3,16,16,128]{3,2,1,0:T(8,128)(2,1)S(1)} %get-tuple-element.28), channel_id=1, source_target_pairs={{0,3},{1,0},{2,1},{3,2},{4,7},{5,4},{6,5},{7,6},{8,11},{9,8},{10,9... | collective-permute-start | bytes 589832 | tf_op jit(solution)/shard_map/ppermute | solution.py:41
  33.1 3.9 %collective-permute-done.3.fr = bf16[3,16,16,128]{3,2,1,0:T(8,128)(2,1)S(1)} collective-permute-done((bf16[3,16,16,128]{3,2,1,0:T(8,128)(2,1)S(1)}, bf16[3,16,16,128]{3,2,1,0:T(8,128)(2,1)S(1)}, u32[]{:S(2)}, u32[]{:S(2)}) %collective-permute-start.3) | collective-permute-done | bytes 196640 | tf_op jit(solution)/shard_map/ppermute | solution.py:41
  37.0 6.6 %collective-permute-done.4.fb = bf16[3,16,16,128]{3,2,1,0:T(8,128)(2,1)S(1)} collective-permute-done((bf16[3,16,16,128]{3,2,1,0:T(8,128)(2,1)S(1)}, bf16[3,16,16,128]{3,2,1,0:T(8,128)(2,1)S(1)}, u32[]{:S(2)}, u32[]{:S(2)}) %collective-permute-start.4) | collective-permute-done | bytes 196640 | tf_op jit(solution)/shard_map/ppermute | solution.py:41
  44.4 6.2 %collective-permute-start.6 = (bf16[3,16,16,128]{3,2,1,0:T(8,128)(2,1)}, bf16[3,16,16,128]{3,2,1,0:T(8,128)(2,1)}, u32[]{:S(2)}, u32[]{:S(2)}) collective-permute-start(bf16[3,16,16,128]{3,2,1,0:T(8,128)(2,1)} %get-tuple-element.30.e0), channel_id=1, source_target_pairs={{0,3},{1,0},{2,1},{3,2},{4,7},{5,4},{6,5},{7,6},{8,11},{9,8},{10,9... | collective-permute-start | bytes 589832 | tf_op jit(solution)/shard_map/ppermute | solution.py:41
  51.2 5.1 %collective-permute-done.6.e1 = bf16[3,16,16,128]{3,2,1,0:T(8,128)(2,1)} collective-permute-done((bf16[3,16,16,128]{3,2,1,0:T(8,128)(2,1)}, bf16[3,16,16,128]{3,2,1,0:T(8,128)(2,1)}, u32[]{:S(2)}, u32[]{:S(2)}) %collective-permute-start.6) | collective-permute-done | bytes 196640 | tf_op jit(solution)/shard_map/ppermute | solution.py:41
  56.3 11.8 %collective-permute-done.7.e2 = bf16[3,16,16,128]{3,2,1,0:T(8,128)(2,1)} collective-permute-done((bf16[3,16,16,128]{3,2,1,0:T(8,128)(2,1)}, bf16[3,16,16,128]{3,2,1,0:T(8,128)(2,1)}, u32[]{:S(2)}, u32[]{:S(2)}) %collective-permute-start.7) | collective-permute-done | bytes 196640 | tf_op jit(solution)/shard_map/ppermute | solution.py:41
  70.0 7.2 %grads.1 = (f32[256,1024]{1,0:T(8,128)S(1)}, bf16[256,1024]{1,0:T(8,128)(2,1)}) custom-call(s32[1]{0:T(128)} %bitcast.half_ref.refs_0_, bf16[512,3072]{1,0:T(8,128)(2,1)S(1)} %get-tuple-element.22.wd_ref, f32[512,128]{1,0:T(8,128)S(1)} %copy-done.7, bf16[3,16,16,128]{3,2,1,0:T(8,128)(2,1)S(1)} %bitcast.12, ...), custom_call_target="tpu_custom_call" | custom-call | flops 1610612736 | bytes 6291456 | tf_op jit(solution)/shard_map/grads/pallas_call | solution.py:283
  78.2 2.1 %collective-permute-done.9.got = bf16[256,1024]{1,0:T(8,128)(2,1)S(1)} collective-permute-done((bf16[256,1024]{1,0:T(8,128)(2,1)}, bf16[256,1024]{1,0:T(8,128)(2,1)S(1)}, u32[]{:S(2)}, u32[]{:S(2)}) %collective-permute-start.9) | collective-permute-done | bytes 524320 | tf_op jit(solution)/shard_map/ppermute | solution.py:46
  81.7 1.6 %collective-permute-start.10 = (bf16[64,1024]{1,0:T(8,128)(2,1)S(1)}, bf16[64,1024]{1,0:T(8,128)(2,1)S(1)}, u32[]{:S(2)}, u32[]{:S(2)}) collective-permute-start(bf16[64,1024]{1,0:T(8,128)(2,1)S(1)} %get-tuple-element.34), channel_id=1, source_target_pairs={{0,8},{4,12},{8,0},{12,4},{16,24},{20,28},{24,16},{28,20},{1,9},{5... | collective-permute-start | bytes 393224 | tf_op jit(solution)/shard_map/ppermute | solution.py:46
  83.2 1.5 %collective-permute-start.11 = (bf16[64,1024]{1,0:T(8,128)(2,1)S(1)}, bf16[64,1024]{1,0:T(8,128)(2,1)S(1)}, u32[]{:S(2)}, u32[]{:S(2)}) collective-permute-start(bf16[64,1024]{1,0:T(8,128)(2,1)S(1)} %get-tuple-element.35), channel_id=1, source_target_pairs={{0,16},{4,20},{8,24},{12,28},{16,0},{20,4},{24,8},{28,12},{1,17},{... | collective-permute-start | bytes 393224 | tf_op jit(solution)/shard_map/ppermute | solution.py:46
  85.2 2.5 %collective-permute-done.10.refs_0_ = bf16[64,1024]{1,0:T(8,128)(2,1)S(1)} collective-permute-done((bf16[64,1024]{1,0:T(8,128)(2,1)S(1)}, bf16[64,1024]{1,0:T(8,128)(2,1)S(1)}, u32[]{:S(2)}, u32[]{:S(2)}) %collective-permute-start.10) | collective-permute-done | bytes 131104 | tf_op jit(solution)/shard_map/ppermute | solution.py:46
  87.7 3.6 %collective-permute-done.11.refs_1_ = bf16[64,1024]{1,0:T(8,128)(2,1)S(1)} collective-permute-done((bf16[64,1024]{1,0:T(8,128)(2,1)S(1)}, bf16[64,1024]{1,0:T(8,128)(2,1)S(1)}, u32[]{:S(2)}, u32[]{:S(2)}) %collective-permute-start.11) | collective-permute-done | bytes 131104 | tf_op jit(solution)/shard_map/ppermute | solution.py:46
  93.5 1.4 %collective-permute-start.15 = (bf16[64,1024]{1,0:T(8,128)(2,1)S(1)}, bf16[64,1024]{1,0:T(8,128)(2,1)S(1)}, u32[]{:S(2)}, u32[]{:S(2)}) collective-permute-start(bf16[64,1024]{1,0:T(8,128)(2,1)S(1)} %get-tuple-element.38.own), channel_id=1, source_target_pairs={{0,24},{4,28},{8,16},{12,20},{16,8},{20,12},{24,0},{28,4},{1,25},{... | collective-permute-start | bytes 393224 | tf_op jit(solution)/shard_map/ppermute | solution.py:46
  95.0 2.4 %collective-permute-done.13.refs_0_ = bf16[64,1024]{1,0:T(8,128)(2,1)S(1)} collective-permute-done((bf16[64,1024]{1,0:T(8,128)(2,1)S(1)}, bf16[64,1024]{1,0:T(8,128)(2,1)S(1)}, u32[]{:S(2)}, u32[]{:S(2)}) %collective-permute-start.13) | collective-permute-done | bytes 131104 | tf_op jit(solution)/shard_map/ppermute | solution.py:46
  97.4 2.5 %collective-permute-done.14.refs_1_ = bf16[64,1024]{1,0:T(8,128)(2,1)S(1)} collective-permute-done((bf16[64,1024]{1,0:T(8,128)(2,1)S(1)}, bf16[64,1024]{1,0:T(8,128)(2,1)S(1)}, u32[]{:S(2)}, u32[]{:S(2)}) %collective-permute-start.14) | collective-permute-done | bytes 131104 | tf_op jit(solution)/shard_map/ppermute | solution.py:46
  101.0 2.9 %collective-permute-start.19 = (f32[16,128]{1,0:T(8,128)S(1)}, f32[16,128]{1,0:T(8,128)S(1)}, u32[]{:S(2)}, u32[]{:S(2)}) collective-permute-start(f32[16,128]{1,0:T(8,128)S(1)} %get-tuple-element.39), channel_id=1, source_target_pairs={{0,3},{1,0},{2,1},{3,2},{4,7},{5,4},{6,5},{7,6},{8,11},{9,8},{10,9... | collective-permute-start | bytes 24584 | tf_op jit(solution)/shard_map/ppermute | solution.py:41
  103.9 1.6 %collective-permute-done.17 = f32[16,128]{1,0:T(8,128)S(1)} collective-permute-done((f32[16,128]{1,0:T(8,128)S(1)}, f32[16,128]{1,0:T(8,128)S(1)}, u32[]{:S(2)}, u32[]{:S(2)}) %collective-permute-start.17) | collective-permute-done | bytes 8224 | tf_op jit(solution)/shard_map/ppermute | solution.py:41
  111.1 1.8 %collective-permute-done.22 = f32[16,128]{1,0:T(8,128)S(1)} collective-permute-done((f32[16,128]{1,0:T(8,128)S(1)}, f32[16,128]{1,0:T(8,128)S(1)}, u32[]{:S(2)}, u32[]{:S(2)}) %collective-permute-start.22) | collective-permute-done | bytes 8224 | tf_op jit(solution)/shard_map/ppermute | solution.py:46
  114.0 1.4 %finish.1 = (bf16[512,972]{1,0:T(8,128)(2,1)}, f32[8,128]{1,0:T(8,128)S(1)}) custom-call(s32[1]{0:T(128)} %bitcast.half_ref.refs_0_, bf16[256,1024]{1,0:T(8,128)(2,1)S(1)} %gather.1.refs_1_, bf16[256,1024]{1,0:T(8,128)(2,1)S(1)} %collective-permute-done.16.refs_2_, f32[16,128]{1,0:T(8,128)S(1)} %add_add_fusion.refs_3_, ...), custom_call_target="tpu_custom_call" | custom-call | flops 50331648 | bytes 196608 | tf_op jit(solution)/shard_map/finish/pallas_call | solution.py:321
  (53 shorter events, 22.4 us)
Async XLA Ops:
  0.6 12.7 %collective-permute-start = (bf16[3,16,16,128]{3,2,1,0:T(8,128)(2,1)}, bf16[3,16,16,128]{3,2,1,0:T(8,128)(2,1)S(1)}, u32[]{:S(2)}, u32[]{:S(2)}) collective-permute-start(bf16[3,16,16,128]{3,2,1,0:T(8,128)(2,1)} %bitcast.7), channel_id=1, source_target_pairs={{0,3},{1,0},{2,1},{3,2},{4,7},{5,4},{6,5},{7,6},{8,11},{9,8},{10,9... | collective-permute-start | bytes 589832 | tf_op jit(solution)/shard_map/ppermute | solution.py:41
  5.8 17.0 %collective-permute-start.1 = (bf16[3,16,16,128]{3,2,1,0:T(8,128)(2,1)}, bf16[3,16,16,128]{3,2,1,0:T(8,128)(2,1)}, u32[]{:S(2)}, u32[]{:S(2)}) collective-permute-start(bf16[3,16,16,128]{3,2,1,0:T(8,128)(2,1)} %bitcast.8), channel_id=1, source_target_pairs={{0,2},{1,3},{2,0},{3,1},{4,6},{5,7},{6,4},{7,5},{8,10},{9,11},{10,... | collective-permute-start | bytes 589832 | tf_op jit(solution)/shard_map/ppermute | solution.py:41
  5.8 17.0 %collective-permute-start.2 = (bf16[3,16,16,128]{3,2,1,0:T(8,128)(2,1)}, bf16[3,16,16,128]{3,2,1,0:T(8,128)(2,1)}, u32[]{:S(2)}, u32[]{:S(2)}) collective-permute-start(bf16[3,16,16,128]{3,2,1,0:T(8,128)(2,1)} %bitcast.9), channel_id=1, source_target_pairs={{0,1},{1,2},{2,3},{3,0},{4,5},{5,6},{6,7},{7,4},{8,9},{9,10},{10,1... | collective-permute-start | bytes 589832 | tf_op jit(solution)/shard_map/ppermute | solution.py:41
  27.3 9.7 %collective-permute-start.3 = (bf16[3,16,16,128]{3,2,1,0:T(8,128)(2,1)S(1)}, bf16[3,16,16,128]{3,2,1,0:T(8,128)(2,1)S(1)}, u32[]{:S(2)}, u32[]{:S(2)}) collective-permute-start(bf16[3,16,16,128]{3,2,1,0:T(8,128)(2,1)S(1)} %get-tuple-element.26), channel_id=1, source_target_pairs={{0,1},{1,2},{2,3},{3,0},{4,5},{5,6},{6,7},{7,4},{8,9},{9,10},{10,1... | collective-permute-start | bytes 589832 | tf_op jit(solution)/shard_map/ppermute | solution.py:41
  28.3 15.4 %collective-permute-start.4 = (bf16[3,16,16,128]{3,2,1,0:T(8,128)(2,1)S(1)}, bf16[3,16,16,128]{3,2,1,0:T(8,128)(2,1)S(1)}, u32[]{:S(2)}, u32[]{:S(2)}) collective-permute-start(bf16[3,16,16,128]{3,2,1,0:T(8,128)(2,1)S(1)} %get-tuple-element.27), channel_id=1, source_target_pairs={{0,2},{1,3},{2,0},{3,1},{4,6},{5,7},{6,4},{7,5},{8,10},{9,11},{10,... | collective-permute-start | bytes 589832 | tf_op jit(solution)/shard_map/ppermute | solution.py:41
  30.2 13.4 %collective-permute-start.5 = (bf16[3,16,16,128]{3,2,1,0:T(8,128)(2,1)S(1)}, bf16[3,16,16,128]{3,2,1,0:T(8,128)(2,1)S(1)}, u32[]{:S(2)}, u32[]{:S(2)}) collective-permute-start(bf16[3,16,16,128]{3,2,1,0:T(8,128)(2,1)S(1)} %get-tuple-element.28), channel_id=1, source_target_pairs={{0,3},{1,0},{2,1},{3,2},{4,7},{5,4},{6,5},{7,6},{8,11},{9,8},{10,9... | collective-permute-start | bytes 589832 | tf_op jit(solution)/shard_map/ppermute | solution.py:41
  44.4 11.8 %collective-permute-start.6 = (bf16[3,16,16,128]{3,2,1,0:T(8,128)(2,1)}, bf16[3,16,16,128]{3,2,1,0:T(8,128)(2,1)}, u32[]{:S(2)}, u32[]{:S(2)}) collective-permute-start(bf16[3,16,16,128]{3,2,1,0:T(8,128)(2,1)} %get-tuple-element.30.e0), channel_id=1, source_target_pairs={{0,3},{1,0},{2,1},{3,2},{4,7},{5,4},{6,5},{7,6},{8,11},{9,8},{10,9... | collective-permute-start | bytes 589832 | tf_op jit(solution)/shard_map/ppermute | solution.py:41
  50.6 17.5 %collective-permute-start.7 = (bf16[3,16,16,128]{3,2,1,0:T(8,128)(2,1)}, bf16[3,16,16,128]{3,2,1,0:T(8,128)(2,1)}, u32[]{:S(2)}, u32[]{:S(2)}) collective-permute-start(bf16[3,16,16,128]{3,2,1,0:T(8,128)(2,1)} %get-tuple-element.30.e0), channel_id=1, source_target_pairs={{0,2},{1,3},{2,0},{3,1},{4,6},{5,7},{6,4},{7,5},{8,10},{9,11},{10,... | collective-permute-start | bytes 589832 | tf_op jit(solution)/shard_map/ppermute | solution.py:41
  50.6 17.5 %collective-permute-start.8 = (bf16[3,16,16,128]{3,2,1,0:T(8,128)(2,1)}, bf16[3,16,16,128]{3,2,1,0:T(8,128)(2,1)}, u32[]{:S(2)}, u32[]{:S(2)}) collective-permute-start(bf16[3,16,16,128]{3,2,1,0:T(8,128)(2,1)} %get-tuple-element.30.e0), channel_id=1, source_target_pairs={{0,1},{1,2},{2,3},{3,0},{4,5},{5,6},{6,7},{7,4},{8,9},{9,10},{10,1... | collective-permute-start | bytes 589832 | tf_op jit(solution)/shard_map/ppermute | solution.py:41
  78.2 2.1 %collective-permute-start.9 = (bf16[256,1024]{1,0:T(8,128)(2,1)}, bf16[256,1024]{1,0:T(8,128)(2,1)S(1)}, u32[]{:S(2)}, u32[]{:S(2)}) collective-permute-start(bf16[256,1024]{1,0:T(8,128)(2,1)} %get-tuple-element.32), channel_id=1, source_target_pairs={{0,4},{4,0},{8,12},{12,8},{16,20},{20,16},{24,28},{28,24},{1,5},{5... | collective-permute-start | bytes 1572872 | tf_op jit(solution)/shard_map/ppermute | solution.py:46
  81.7 6.0 %collective-permute-start.10 = (bf16[64,1024]{1,0:T(8,128)(2,1)S(1)}, bf16[64,1024]{1,0:T(8,128)(2,1)S(1)}, u32[]{:S(2)}, u32[]{:S(2)}) collective-permute-start(bf16[64,1024]{1,0:T(8,128)(2,1)S(1)} %get-tuple-element.34), channel_id=1, source_target_pairs={{0,8},{4,12},{8,0},{12,4},{16,24},{20,28},{24,16},{28,20},{1,9},{5... | collective-permute-start | bytes 393224 | tf_op jit(solution)/shard_map/ppermute | solution.py:46
  83.2 8.1 %collective-permute-start.11 = (bf16[64,1024]{1,0:T(8,128)(2,1)S(1)}, bf16[64,1024]{1,0:T(8,128)(2,1)S(1)}, u32[]{:S(2)}, u32[]{:S(2)}) collective-permute-start(bf16[64,1024]{1,0:T(8,128)(2,1)S(1)} %get-tuple-element.35), channel_id=1, source_target_pairs={{0,16},{4,20},{8,24},{12,28},{16,0},{20,4},{24,8},{28,12},{1,17},{... | collective-permute-start | bytes 393224 | tf_op jit(solution)/shard_map/ppermute | solution.py:46
  84.8 6.6 %collective-permute-start.12 = (bf16[64,1024]{1,0:T(8,128)(2,1)S(1)}, bf16[64,1024]{1,0:T(8,128)(2,1)S(1)}, u32[]{:S(2)}, u32[]{:S(2)}) collective-permute-start(bf16[64,1024]{1,0:T(8,128)(2,1)S(1)} %get-tuple-element.36), channel_id=1, source_target_pairs={{0,24},{4,28},{8,16},{12,20},{16,8},{20,12},{24,0},{28,4},{1,25},{... | collective-permute-start | bytes 393224 | tf_op jit(solution)/shard_map/ppermute | solution.py:46
  91.4 6.0 %collective-permute-start.13 = (bf16[64,1024]{1,0:T(8,128)(2,1)S(1)}, bf16[64,1024]{1,0:T(8,128)(2,1)S(1)}, u32[]{:S(2)}, u32[]{:S(2)}) collective-permute-start(bf16[64,1024]{1,0:T(8,128)(2,1)S(1)} %get-tuple-element.38.own), channel_id=1, source_target_pairs={{0,8},{4,12},{8,0},{12,4},{16,24},{20,28},{24,16},{28,20},{1,9},{5... | collective-permute-start | bytes 393224 | tf_op jit(solution)/shard_map/ppermute | solution.py:46
  92.7 7.2 %collective-permute-start.14 = (bf16[64,1024]{1,0:T(8,128)(2,1)S(1)}, bf16[64,1024]{1,0:T(8,128)(2,1)S(1)}, u32[]{:S(2)}, u32[]{:S(2)}) collective-permute-start(bf16[64,1024]{1,0:T(8,128)(2,1)S(1)} %get-tuple-element.38.own), channel_id=1, source_target_pairs={{0,16},{4,20},{8,24},{12,28},{16,0},{20,4},{24,8},{28,12},{1,17},{... | collective-permute-start | bytes 393224 | tf_op jit(solution)/shard_map/ppermute | solution.py:46
  93.5 6.4 %collective-permute-start.15 = (bf16[64,1024]{1,0:T(8,128)(2,1)S(1)}, bf16[64,1024]{1,0:T(8,128)(2,1)S(1)}, u32[]{:S(2)}, u32[]{:S(2)}) collective-permute-start(bf16[64,1024]{1,0:T(8,128)(2,1)S(1)} %get-tuple-element.38.own), channel_id=1, source_target_pairs={{0,24},{4,28},{8,16},{12,20},{16,8},{20,12},{24,0},{28,4},{1,25},{... | collective-permute-start | bytes 393224 | tf_op jit(solution)/shard_map/ppermute | solution.py:46
  100.0 14.1 %collective-permute-start.16 = (bf16[256,1024]{1,0:T(8,128)(2,1)S(1)}, bf16[256,1024]{1,0:T(8,128)(2,1)S(1)}, u32[]{:S(2)}, u32[]{:S(2)}) collective-permute-start(bf16[256,1024]{1,0:T(8,128)(2,1)S(1)} %gather.1.refs_1_), channel_id=1, source_target_pairs={{0,4},{4,0},{8,12},{12,8},{16,20},{20,16},{24,28},{28,24},{1,5},{5... | collective-permute-start | bytes 1572872 | tf_op jit(solution)/shard_map/ppermute | solution.py:46
  100.0 5.5 %collective-permute-start.17 = (f32[16,128]{1,0:T(8,128)S(1)}, f32[16,128]{1,0:T(8,128)S(1)}, u32[]{:S(2)}, u32[]{:S(2)}) collective-permute-start(f32[16,128]{1,0:T(8,128)S(1)} %get-tuple-element.39), channel_id=1, source_target_pairs={{0,1},{1,2},{2,3},{3,0},{4,5},{5,6},{6,7},{7,4},{8,9},{9,10},{10,1... | collective-permute-start | bytes 24584 | tf_op jit(solution)/shard_map/ppermute | solution.py:41
  100.1 5.4 %collective-permute-start.18 = (f32[16,128]{1,0:T(8,128)S(1)}, f32[16,128]{1,0:T(8,128)S(1)}, u32[]{:S(2)}, u32[]{:S(2)}) collective-permute-start(f32[16,128]{1,0:T(8,128)S(1)} %get-tuple-element.39), channel_id=1, source_target_pairs={{0,2},{1,3},{2,0},{3,1},{4,6},{5,7},{6,4},{7,5},{8,10},{9,11},{10,... | collective-permute-start | bytes 24584 | tf_op jit(solution)/shard_map/ppermute | solution.py:41
  101.0 5.1 %collective-permute-start.19 = (f32[16,128]{1,0:T(8,128)S(1)}, f32[16,128]{1,0:T(8,128)S(1)}, u32[]{:S(2)}, u32[]{:S(2)}) collective-permute-start(f32[16,128]{1,0:T(8,128)S(1)} %get-tuple-element.39), channel_id=1, source_target_pairs={{0,3},{1,0},{2,1},{3,2},{4,7},{5,4},{6,5},{7,6},{8,11},{9,8},{10,9... | collective-permute-start | bytes 24584 | tf_op jit(solution)/shard_map/ppermute | solution.py:41
  106.1 3.7 %collective-permute-start.20 = (f32[16,128]{1,0:T(8,128)S(1)}, f32[16,128]{1,0:T(8,128)S(1)}, u32[]{:S(2)}, u32[]{:S(2)}) collective-permute-start(f32[16,128]{1,0:T(8,128)S(1)} %add_add_fusion.1), channel_id=1, source_target_pairs={{0,8},{4,12},{8,0},{12,4},{16,24},{20,28},{24,16},{28,20},{1,9},{5... | collective-permute-start | bytes 24584 | tf_op jit(solution)/shard_map/ppermute | solution.py:46
  107.4 3.7 %collective-permute-start.21 = (f32[16,128]{1,0:T(8,128)S(1)}, f32[16,128]{1,0:T(8,128)S(1)}, u32[]{:S(2)}, u32[]{:S(2)}) collective-permute-start(f32[16,128]{1,0:T(8,128)S(1)} %add_add_fusion.1), channel_id=1, source_target_pairs={{0,16},{4,20},{8,24},{12,28},{16,0},{20,4},{24,8},{28,12},{1,17},{... | collective-permute-start | bytes 24584 | tf_op jit(solution)/shard_map/ppermute | solution.py:46
  108.3 4.5 %collective-permute-start.22 = (f32[16,128]{1,0:T(8,128)S(1)}, f32[16,128]{1,0:T(8,128)S(1)}, u32[]{:S(2)}, u32[]{:S(2)}) collective-permute-start(f32[16,128]{1,0:T(8,128)S(1)} %add_add_fusion.1), channel_id=1, source_target_pairs={{0,24},{4,28},{8,16},{12,20},{16,8},{20,12},{24,0},{28,4},{1,25},{... | collective-permute-start | bytes 24584 | tf_op jit(solution)/shard_map/ppermute | solution.py:46
  112.8 1.2 %collective-permute-start.23 = (f32[16,128]{1,0:T(8,128)S(1)}, f32[16,128]{1,0:T(8,128)S(1)}, u32[]{:S(2)}, u32[]{:S(2)}) collective-permute-start(f32[16,128]{1,0:T(8,128)S(1)} %add_add_fusion.refs_3_), channel_id=1, source_target_pairs={{0,4},{4,0},{8,12},{12,8},{16,20},{20,16},{24,28},{28,24},{1,5},{5... | collective-permute-start | bytes 24584 | tf_op jit(solution)/shard_map/ppermute | solution.py:46
  (8 other events, 45.6 us)

commit v2 on v0

v2 whole, which is shorter than its diff:
```python
import functools
import math

import jax
import jax.numpy as jnp
from jax import lax
from jax.experimental import pallas as pl
from jax.experimental.pallas import tpu as pltpu
from jax.sharding import PartitionSpec as P

FIELD = 18
MAPS = 8
STRIDE = 2
TILE_PX = 16
INPUTS = 972
HALO = 16
POS = 64
SPAN = TILE_PX + HALO
SIDE_POS = TILE_PX // STRIDE
UNITS = POS * MAPS
HALF = UNITS // 2
PLANE = SPAN * SPAN
QUAD = TILE_PX * TILE_PX
PATCH = FIELD * FIELD
LANES = 128
PAD_IN = -(-INPUTS // LANES) * LANES
PAD_STRIP = -(-FIELD * SPAN // LANES) * LANES
GRAB = 512
STEP_IN = 256
LAST = INPUTS % LANES

sparsity_weight = 1.0
smooth_eps = 0.01
guard_eps = 1e-06

BF = jnp.bfloat16
F32 = jnp.float32
VMEM_CAP = 24 * 1024 * 1024
RELAY_TILES = 4


def send(value, axis, pairs):
    return lax.ppermute(value, axis, pairs)


def ring(count, steps):
    return [(s, (s + steps) % count) for s in range(count)]


def flips(count, flip):
    return [(s, s ^ flip) for s in range(count)]


def flip_all(pairs):
    return [(b, a) for a, b in pairs]


def routes(n_tile):
    side = math.isqrt(n_tile)
    if n_tile == RELAY_TILES:
        return (
            [(0, 2), (3, 1), (1, 0), (2, 3)],
            [(1, 3), (2, 0), (0, 1), (3, 2)],
            [(1, 2), (2, 1)],
            [(2, 3), (1, 0)],
        )
    return ring(n_tile, -1), ring(n_tile, -side), ring(n_tile, -side - 1), None


def quadrants():
    if lax.axis_size("tile") != RELAY_TILES:
        return 1, 2, 3
    t = lax.axis_index("tile")
    inner = (t == 1) | (t == 2)
    first = jnp.where(inner, 2, jnp.where(t == 0, 1, 3))
    second = jnp.where(t == 1, 3, jnp.where(t == 2, 1, 2))
    third = jnp.where(t % 2 == 0, 3, 1)
    return first, second, third


def kernel_call(body, outs, scratch=(), n_in=0, flops=0, name=None, scalar_out=False):
    places = [pltpu.VMEM] * (len(outs) - scalar_out) + [pltpu.SMEM] * scalar_out
    return pl.pallas_call(
        body,
        out_shape=outs,
        in_specs=[pl.BlockSpec(memory_space=pltpu.VMEM)] * n_in,
        out_specs=tuple(pl.BlockSpec(memory_space=place) for place in places),
        scratch_shapes=list(scratch),
        compiler_params=pltpu.CompilerParams(vmem_limit_bytes=VMEM_CAP),
        cost_estimate=pl.CostEstimate(flops=flops, transcendentals=0, bytes_accessed=flops // 256),
        name=name,
    )


def positions(rows):
    for i in range(rows):
        for j in range(0, SIDE_POS, 2):
            lead = i * STRIDE * SPAN // LANES * LANES
            rest = i * STRIDE * SPAN - lead
            yield (i * SIDE_POS + j) * MAPS, lead, (rest + STRIDE * j, rest + STRIDE * (j + 1))


def place(dst, own, slots):
    for q, load in zip((0,) + tuple(quadrants()), (own,) + tuple(slots)):
        top = pl.multiple_of(q // 2 * TILE_PX, TILE_PX)
        left = pl.multiple_of(q % 2 * TILE_PX, TILE_PX)
        for ch in range(3):
            dst[ch, pl.ds(top, TILE_PX), pl.ds(left, TILE_PX), :] = load(ch)


def loader(*refs):
    def load(ch):
        value = refs[0][ch]
        for ref in refs[1:]:
            value = value + ref[ch]
        return value

    return load


def expand_body(w_ref, con_ref, x_ref, wd_ref, wt_ref, st_ref, copy_ref, wp_ref, v_ref, s_ref):
    copy_ref[...] = x_ref[...]
    wp_ref[:, PAD_IN - LANES :] = jnp.zeros((UNITS, LANES), BF)
    wp_ref[:, :INPUTS] = w_ref[...]

    def wanted(shape, axis):
        n = lax.broadcasted_iota(jnp.int32, shape, axis)
        row, col = n // SPAN, n % SPAN
        return (col < FIELD) & (row < FIELD), row * FIELD + col

    inside, source = wanted((1, PAD_STRIP), 1)
    inside_t, source_t = wanted((PAD_STRIP, 1), 0)
    k = lax.broadcasted_iota(jnp.int32, (GRAB, PAD_STRIP), 0)
    k_t = lax.broadcasted_iota(jnp.int32, (PAD_STRIP, GRAB), 1)
    for ch in range(3):
        skip = ch * (PATCH - STEP_IN)
        want = jnp.where(inside, source + skip, -1)
        s_ref[...] = jnp.where(k == want, 1.0, 0.0).astype(BF)
        want = jnp.where(inside_t, source_t + skip, -1)
        st_ref[ch] = jnp.where(k_t == want, 1.0, 0.0).astype(BF)
        v = jnp.dot(
            wp_ref[:, ch * STEP_IN : ch * STEP_IN + GRAB], s_ref[...], preferred_element_type=F32
        )
        v_ref[...] = v * con_ref[:, ch : ch + 1]
        base = ch * PLANE
        for u, lead, shifts in positions(SIDE_POS):
            parts = []
            for h, s in enumerate(shifts):
                blk = v_ref[u + h * MAPS : u + (h + 1) * MAPS, :]
                parts.append(pltpu.roll(blk, s, 1) if s else blk)
            rows = slice(u, u + 2 * MAPS)
            if lead:
                wd_ref[rows, base : base + lead] = jnp.zeros((2 * MAPS, lead), BF)
            end = lead + PAD_STRIP
            wd_ref[rows, base + lead : base + end] = jnp.concatenate(parts, 0).astype(BF)
            if end < PLANE:
                wd_ref[rows, base + end : base + PLANE] = jnp.zeros((2 * MAPS, PLANE - end), BF)
        for at in range(0, PLANE, LANES):
            flipped = wd_ref[:, base + at : base + at + LANES].T
            for sub in range(0, LANES, TILE_PX):
                row, col = (at + sub) // SPAN, (at + sub) % SPAN
                q = row // TILE_PX * 2 + col // TILE_PX
                to = ch * QUAD + row % TILE_PX * TILE_PX
                wt_ref[q, to : to + TILE_PX, :] = flipped[sub : sub + TILE_PX]


def coded_body(relay, x_ref, *refs):
    slots, (wd_ref, wt_ref, coded_ref, out_ref, xe) = refs[: 4 if relay else 3], refs[-5:]
    third = slots[2:]
    place(xe, loader(x_ref), (loader(slots[0]), loader(slots[1]), loader(*third)))
    batch = x_ref.shape[-1]
    coded = jnp.dot(wd_ref[...], xe[...].reshape(3 * PLANE, batch), preferred_element_type=F32)
    coded_ref[...] = coded
    part = jnp.dot(wt_ref[quadrants()[2]], coded.astype(BF), preferred_element_type=F32)
    out_ref[...] = part.astype(BF).reshape(out_ref.shape)


def spill_body(wt_ref, coded_ref, a_ref, b_ref):
    rounded = coded_ref[...].astype(BF)
    first, second, _ = quadrants()
    for q, ref in ((second, b_ref), (first, a_ref)):
        part = jnp.dot(wt_ref[q], rounded, preferred_element_type=F32)
        ref[...] = part.astype(BF).reshape(ref.shape)


def own_body(wt_ref, coded_ref, x_ref, own_ref, loss_ref):
    coded = coded_ref[...]
    batch = coded.shape[-1]
    part = jnp.dot(wt_ref[0], coded.astype(BF), preferred_element_type=F32)
    own_ref[...] = part.reshape(own_ref.shape) - x_ref[...].astype(F32)
    root = jnp.sqrt(smooth_eps + coded * coded)
    loss_ref[...] = sparsity_weight * jnp.sum(root.reshape(UNITS // 8, 8, batch), 0)


def join_body(a_ref, d_ref, out_ref):
    out_ref[...] = (a_ref[...].astype(F32) + d_ref[...].astype(F32)).astype(BF)


def error_body(own, fa, fb, fc, sp, e_ref, loss_ref):
    batch = own.shape[-1]
    total = sp[...]
    for ch in range(3):
        err = own[ch] + fa[ch].astype(F32) + fb[ch].astype(F32) + fc[ch].astype(F32)
        e_ref[ch] = err.astype(BF)
        total = total + jnp.sum((err * err).reshape(QUAD // 8, 8, batch), 0)
    loss_ref[...] = total


def ready_body(relay, coded_ref, e_ref, x_ref, *refs):
    slots, (left_ref, pull_ref, xe, copy_ref) = refs[:-4], refs[-4:]
    copy_ref[...] = e_ref[...]
    coded = coded_ref[...]
    left_ref[...] = (2.0 * coded).astype(BF)
    pull_ref[...] = sparsity_weight * coded / jnp.sqrt(smooth_eps + coded * coded)
    place(xe, loader(x_ref), (loader(slots[0]), loader(slots[1]), loader(*slots[2:])))


def gradient_rows(half, wd_ref, left_ref, pull_ref, con_ref, st_ref, ex, gd, gs, out):
    at = pl.multiple_of(half * HALF, HALF)
    rows = pl.ds(at, HALF)
    batch = left_ref.shape[-1]
    e_all = ex[:, :, :batch].reshape(3 * PLANE, batch)
    enc = jnp.dot(wd_ref[rows, :], e_all, preferred_element_type=F32)
    left = left_ref[rows, :].astype(F32)
    right = 2.0 * enc + pull_ref[rows, :]
    con = con_ref[rows, :]
    shift = half * (SIDE_POS // 2 * STRIDE * SPAN)
    out[...] = jnp.zeros((HALF, PAD_IN), F32)
    for ch in range(3):
        opened = con[:, ch : ch + 1]
        both = jnp.concatenate([(left * opened).astype(BF), (right * opened).astype(BF)], 1)
        gd[...] = lax.dot_general(
            both, ex[ch], (((1,), (1,)), ((), ())), preferred_element_type=F32
        )
        for u, lead, shifts in positions(SIDE_POS // 2):
            parts = []
            lanes = pl.ds(pl.multiple_of(lead + shift, LANES), PAD_STRIP)
            for h, s in enumerate(shifts):
                blk = gd[u + h * MAPS : u + (h + 1) * MAPS, lanes]
                parts.append(pltpu.roll(blk, PAD_STRIP - s, 1) if s else blk)
            gs[u : u + 2 * MAPS, :] = jnp.concatenate(parts, 0).astype(BF)
        cols = slice(ch * STEP_IN, ch * STEP_IN + GRAB)
        out[:, cols] = out[:, cols] + jnp.dot(gs[...], st_ref[ch], preferred_element_type=F32)


def away_body(relay, wd_ref, left_ref, pull_ref, con_ref, st_ref, xe, e_ref, *refs):
    slots, (send_ref, ex, tmp, gd, gs, out) = refs[:-6], refs[-6:]
    batch = e_ref.shape[-1]
    place(tmp, loader(e_ref), (loader(slots[0]), loader(slots[1]), loader(*slots[2:])))
    for ch in range(3):
        ex[ch, :, :batch] = tmp[ch].reshape(PLANE, batch)
        ex[ch, :, batch:] = xe[ch].reshape(PLANE, batch)
    core = lax.axis_index("dp") % 2
    gradient_rows(1 - core, wd_ref, left_ref, pull_ref, con_ref, st_ref, ex, gd, gs, out)
    send_ref[...] = out[...].astype(BF)


def home_body(wd_ref, left_ref, pull_ref, con_ref, st_ref, ex, keep_ref, gd, gs):
    core = lax.axis_index("dp") % 2
    gradient_rows(core, wd_ref, left_ref, pull_ref, con_ref, st_ref, ex, gd, gs, keep_ref)


def pair_body(keep, got, *refs):
    own_ref, sends, scr = refs[0], refs[1:-1], refs[-1]
    rows = own_ref.shape[0]
    scr[...] = keep[...] + got[...].astype(F32)
    chip = lax.axis_index("dp") // 2
    own_ref[...] = scr[pl.ds(pl.multiple_of(chip * rows, rows), rows), :]
    for x, ref in enumerate(sends):
        at = pl.multiple_of((chip ^ (x + 1)) * rows, rows)
        ref[...] = scr[pl.ds(at, rows), :].astype(BF)


def pieces(value):
    high = value.astype(BF)
    rest = value - high.astype(F32)
    mid = rest.astype(BF)
    low = (rest - mid.astype(F32)).astype(BF)
    return high.astype(F32), mid.astype(F32), low.astype(F32)


def total_of(value):
    return jnp.sum(jnp.sum(value, 0, keepdims=True), 1, keepdims=True)


def shard_body(own, *refs):
    got, loss, shard_ref = refs[:-2], refs[-2], refs[-1]
    total = own[...]
    for ref in got:
        total = total + ref[...].astype(F32)
    lane = lax.broadcasted_iota(jnp.int32, (1, LANES), 1)
    tail = total[:, PAD_IN - LANES :]
    for at, value in enumerate(pieces(total_of(loss[...])) + pieces(total_of(total * total))):
        tail = jnp.where(lane == LAST + at, value, tail)
    shard_ref[:, : PAD_IN - LANES] = total[:, : PAD_IN - LANES].astype(BF)
    shard_ref[:, PAD_IN - LANES :] = tail.astype(BF)


def gather_body(own, *refs):
    got, half_ref = refs[:-1], refs[-1]
    rows = own.shape[0]
    chip = lax.axis_index("dp") // 2
    half_ref[pl.ds(pl.multiple_of(chip * rows, rows), rows), :] = own[...]
    for x, ref in enumerate(got):
        at = pl.multiple_of((chip ^ (x + 1)) * rows, rows)
        half_ref[pl.ds(at, rows), :] = ref[...]


def tally_body(rows, mine, other, tally_ref):
    total = jnp.zeros((8, LANES), F32)
    for ref in (mine, other):
        for at in range(0, HALF, rows):
            total = total + ref[at : at + TILE_PX, PAD_IN - LANES :].astype(F32)[:8]
    tally_ref[...] = total


def finish_body(entries, frames_total, mine, other, *refs):
    tallies, up_ref, loss_ref = refs[:-2], refs[-2], refs[-1]
    tally = tallies[0][...]
    for ref in tallies[1:]:
        tally = tally + ref[...]
    lane = lax.broadcasted_iota(jnp.int32, (1, LANES), 1)
    row = tally[:1]
    square = total_of(jnp.where((lane >= LAST + 3) & (lane < LAST + 6), row, 0.0))
    factor = -lax.rsqrt(square / entries + guard_eps)
    core = lax.axis_index("dp") % 2
    for half, ref in ((core, mine), (1 - core, other)):
        at = pl.multiple_of(half * HALF, HALF)
        up_ref[pl.ds(at, HALF), :] = (ref[:, :INPUTS].astype(F32) * factor).astype(BF)
    loss_ref[0, 0] = jnp.sum(jnp.where((lane >= LAST) & (lane < LAST + 3), row, 0.0)) / frames_total


def local(frames, weights, connect):
    batch = frames.shape[-1]
    n_tile = lax.axis_size("tile")
    n_dp = lax.axis_size("dp")
    chips = n_dp // 2
    sds = jax.ShapeDtypeStruct
    mac = 2 * UNITS * 3 * PLANE * batch
    quad = (3, TILE_PX, TILE_PX, batch)
    units = (UNITS, batch)
    plane = (3, SPAN, SPAN, batch)
    to_first, to_second, to_third, onward = routes(n_tile)
    relay = onward is not None

    def spread_out(now, later):
        first = send(now, "tile", to_first)
        second = send(later, "tile", to_second)
        third = send(later, "tile", to_third)
        return [first, second, third] + ([send(first, "tile", onward)] if relay else [])

    x0 = frames[0]
    con = connect.reshape(UNITS, 3).astype(F32)
    wd, wt, st, x_late = kernel_call(
        expand_body,
        (
            sds((UNITS, 3 * PLANE), BF),
            sds((4, 3 * QUAD, UNITS), BF),
            sds((3, PAD_STRIP, GRAB), BF),
            sds(quad, BF),
        ),
        [
            pltpu.VMEM((UNITS, PAD_IN), BF),
            pltpu.VMEM((UNITS, PAD_STRIP), F32),
            pltpu.VMEM((GRAB, PAD_STRIP), BF),
        ],
        n_in=3, flops=4 * mac, name="expand",
    )(weights.reshape(UNITS, INPUTS), con, x0)
    xs = spread_out(x0, x_late if relay else x0)

    coded, sc = kernel_call(
        functools.partial(coded_body, relay),
        (sds(units, F32), sds(quad, BF)),
        [pltpu.VMEM(plane, BF)],
        n_in=3 + len(xs), flops=mac, name="coded",
    )(x0, *xs, wd, wt)
    sa, sb = kernel_call(
        spill_body, (sds(quad, BF), sds(quad, BF)), n_in=2, flops=mac // 2, name="spill"
    )(wt, coded)
    if relay:
        passed = send(sc, "tile", flip_all(onward))
    fb = send(sb, "tile", flip_all(to_second))
    fc = send(sc, "tile", flip_all(to_third))
    own, sparse = kernel_call(
        own_body, (sds(quad, F32), sds((8, batch), F32)), n_in=3, flops=mac // 4, name="own"
    )(wt, coded, x0)
    if relay:
        (sa,) = kernel_call(join_body, (sds(quad, BF),), n_in=2, flops=mac // 64, name="join")(sa, passed)
    fa = send(sa, "tile", flip_all(to_first))
    e0, loss_part = kernel_call(
        error_body, (sds(quad, BF), sds((8, batch), F32)), n_in=5, flops=mac // 32, name="errors"
    )(own, fa, fb, fc, sparse)

    left, pull, xe, e_late = kernel_call(
        functools.partial(ready_body, relay),
        (sds(units, BF), sds(units, F32), sds(plane, BF), sds(quad, BF)),
        n_in=3 + len(xs), flops=mac // 16, name="ready",
    )(coded, e0, x0, *xs)
    es = spread_out(e0, e_late if relay else e0)

    half = (HALF, PAD_IN)
    work = [pltpu.VMEM((HALF, PLANE), F32), pltpu.VMEM((HALF, PAD_STRIP), BF)]
    away, ex = kernel_call(
        functools.partial(away_body, relay),
        (sds(half, BF), sds((3, PLANE, 2 * batch), BF)),
        [pltpu.VMEM(plane, BF)] + work + [pltpu.VMEM(half, F32)],
        n_in=7 + len(es), flops=2 * mac, name="away",
    )(wd, left, pull, con, st, xe, e0, *es)
    got = send(away, "dp", flips(n_dp, 1))
    (keep,) = kernel_call(
        home_body, (sds(half, F32),), work, n_in=6, flops=2 * mac, name="home"
    )(wd, left, pull, con, st, ex)

    rows = HALF // chips
    shard = sds((rows, PAD_IN), BF)
    split = kernel_call(
        pair_body,
        (sds((rows, PAD_IN), F32),) + (shard,) * (chips - 1),
        [pltpu.VMEM(half, F32)],
        n_in=2, flops=mac // 32, name="pair",
    )(keep, got)
    arrived = [send(v, "dp", flips(n_dp, 2 * (x + 1))) for x, v in enumerate(split[1:])]
    (mine,) = kernel_call(shard_body, (shard,), n_in=chips + 1, flops=mac // 64, name="shard")(
        split[0], *arrived, loss_part
    )
    others = [send(mine, "dp", flips(n_dp, 2 * x)) for x in range(1, chips)]
    (mine_half,) = kernel_call(gather_body, (sds(half, BF),), n_in=chips, flops=mac // 64, name="gather")(
        mine, *others
    )
    other_half = send(mine_half, "dp", flips(n_dp, 1))
    (tally,) = kernel_call(
        functools.partial(tally_body, rows), (sds((8, LANES), F32),), n_in=2, flops=mac // 64, name="tally"
    )(mine_half, other_half)
    tallies = [send(tally, "tile", ring(n_tile, s)) for s in range(1, n_tile)]

    entries = n_tile * POS * MAPS * INPUTS
    update, loss = kernel_call(
        functools.partial(finish_body, float(entries), float(batch * n_dp)),
        (sds((UNITS, INPUTS), BF), sds((1, 1), F32)),
        n_in=2 + n_tile, flops=mac // 32, name="finish", scalar_out=True,
    )(mine_half, other_half, tally, *tallies)
    return update.reshape(1, POS, MAPS, INPUTS), loss.reshape(())


def solution(mesh):
    placed = (
        P("tile", None, None, None, "dp"),
        P("tile", None, None, None),
        P("tile", None, None, None),
    )
    return jax.shard_map(
        local,
        mesh=mesh,
        in_specs=placed,
        out_specs=(P("tile", None, None, None), P()),
        check_vma=False,
    )
```

time: 984 us -> 91.7 us (0.09)
  local copies, waits for them, and re-layouts: 656 us -> 2.33 us
  matrix products: 73 us -> 0 us
  blocking collectives: 51.1 us -> 0 us
  loops' own time: 46.2 us -> 0 us
  other arithmetic: 40.9 us -> 0.71 us
  waiting for transfers between devices: 83.5 us -> 43.7 us
  starting transfers between devices: 7.3 us -> 30.8 us
  between operations: 17.9 us -> 0.85 us
  Pallas kernels: 0 us -> 13.1 us
    scatter-add x64 -> x0, local copies, waits for them, and re-layouts: 306 us -> none  [spread(): canvas_strip.at[:, :, column * STRIDE:column * STRIDE + FIELD]]
    another operation x272 -> x0, local copies, waits for them, and re-layouts: 241 us -> none  [the longest x216 197 us: patch_block(): blocks = jnp.stack(pieces, 0)]
    dot_general x32 -> x0, matrix products: 73 us -> none  [the longest x8 32 us: grad_row(): jnp.einsum('cmb,ckb->cmk', right_coef, frame_block, preferred_element_typ...]
    psum x2 -> x0, blocking collectives: 51.1 us -> none  [the longest x1 38.8 us: local(): error_tot, sparse_tot = lax.psum((error_sq, sparse), ('dp', 'tile'))]
    another operation x2 -> x0, loops' own time: 46.2 us -> none  [the longest x1 23.8 us: local(): lax.scan(grad_row, jnp.zeros((), jnp.float32), (jnp.arange(rows_out, dtyp...]
    slice x26 -> x0, local copies, waits for them, and re-layouts: 46 us -> none  [the longest x16 32.8 us: patch_block(): strip_rows[:, :, column * STRIDE:column * STRIDE + FIELD]]
    while x440 -> x0, local copies, waits for them, and re-layouts: 40.9 us -> none
    ppermute x6 -> x23, starting transfers between devices: 7.27 us -> 30.8 us  [send(): return lax.ppermute(value, axis, pairs)]
  transfers between devices with their start and end apart: 7 -> 23, of which waited for: 7 -> 15; matrix products, arithmetic and copies ran while one was open for 1% -> 1% of each run, Pallas kernels for 0% -> 8%
where the time goes in v2:
time: 91.7 us; the launch traced here: 91.4 us
  waiting for transfers between devices  43.7 us (48%)
  starting transfers between devices  30.8 us (34%)
  Pallas kernels  13.1 us (14%)
  local copies, waits for them, and re-layouts  2.33 us (3%)
    ppermute x23, waiting for transfers between devices, send(): return lax.ppermute(value, axis, pairs)  43.7 us
    ppermute x23, starting transfers between devices, send(): return lax.ppermute(value, axis, pairs)  30.8 us
    pallas_call x1, Pallas kernels, local(): kernel_call(expand_body, (sds((UNITS, 3 * PLANE), BF), sds((4, 3 * QUAD,...  3.56 us
    pallas_call x1, Pallas kernels, local(): kernel_call(functools.partial(away_body, relay), (sds(half, BF), sds((3,...  2.36 us
    pallas_call x1, Pallas kernels, local(): kernel_call(home_body, (sds(half, F32),), work, n_in=6, flops=2 * mac, na...  2.27 us
    unnamed x6, local copies, waits for them, and re-layouts  2.15 us
  transfers between devices with their start and end apart: 23, of which 15 were waited for; matrix products, arithmetic and copies ran while one was open for 1% of the time, Pallas kernels for 8%

profile of v2, /device:TPU:0, one launch (start us, length us, event | category | flops | bytes accessed | tf_op | source)
XLA Modules:
  0.0 91.4 jit_solution(16282199202144595071)
XLA Ops:
  0.6 4.1 %collective-permute-start = (bf16[3,16,16,128]{3,2,1,0:T(8,128)(2,1)}, bf16[3,16,16,128]{3,2,1,0:T(8,128)(2,1)S(1)}, u32[]{:S(2)}, u32[]{:S(2)}) collective-permute-start(bf16[3,16,16,128]{3,2,1,0:T(8,128)(2,1)} %bitcast.8), channel_id=1, source_target_pairs={{0,2},{3,1},{1,0},{2,3},{4,6},{7,5},{5,4},{6,7},{8,10},{11,9},{9,8... | collective-permute-start | bytes 589832 | tf_op jit(solution)/shard_map/ppermute | solution.py:43
  7.8 3.6 %expand.1 = (bf16[512,3072]{1,0:T(8,128)(2,1)S(1)}, bf16[4,768,512]{2,1,0:T(8,128)(2,1)S(1)}, bf16[3,640,512]{2,1,0:T(8,128)(2,1)S(1)}, bf16[3,16,16,128]{3,2,1,0:T(8,128)(2,1)S(1)}) custom-call(bf16[512,972]{1,0:T(8,128)(2,1)S(1)} %bitcast.13, f32[512,3]{1,0:T(8,128)S(1)} %bitcast.5, bf16[3,16,16,128]{3,2,1,0:T(8,128)(2,1)S(1)} %bitcast.9), custom_call_target="tpu_custom_call" | custom-call | flops 1610612736 | bytes 6291456 | tf_op jit(solution)/shard_map/expand/pallas_call | solution.py:354
  13.4 6.7 %collective-permute-done.1.refs_1_ = bf16[3,16,16,128]{3,2,1,0:T(8,128)(2,1)S(1)} collective-permute-done((bf16[3,16,16,128]{3,2,1,0:T(8,128)(2,1)S(1)}, bf16[3,16,16,128]{3,2,1,0:T(8,128)(2,1)S(1)}, u32[]{:S(2)}, u32[]{:S(2)}) %collective-permute-start.1) | collective-permute-done | bytes 196640 | tf_op jit(solution)/shard_map/ppermute | solution.py:43
  20.1 3.1 %collective-permute-done.3.refs_3_ = bf16[3,16,16,128]{3,2,1,0:T(8,128)(2,1)S(1)} collective-permute-done((bf16[3,16,16,128]{3,2,1,0:T(8,128)(2,1)S(1)}, bf16[3,16,16,128]{3,2,1,0:T(8,128)(2,1)S(1)}, u32[]{:S(2)}, u32[]{:S(2)}) %collective-permute-start.3) | collective-permute-done | bytes 196640 | tf_op jit(solution)/shard_map/ppermute | solution.py:43
  23.2 1.7 %coded.1 = (f32[512,128]{1,0:T(8,128)S(1)}, bf16[3,16,16,128]{3,2,1,0:T(8,128)(2,1)S(1)}) custom-call(bf16[3,16,16,128]{3,2,1,0:T(8,128)(2,1)S(1)} %bitcast.10, bf16[3,16,16,128]{3,2,1,0:T(8,128)(2,1)S(1)} %collective-permute-done.refs_0_, bf16[3,16,16,128]{3,2,1,0:T(8,128)(2,1)S(1)} %collective-permute-done.1.refs_1_, ...), custom_call_target="tpu_custom_call" | custom-call | flops 402653184 | bytes 1572864 | tf_op jit(solution)/shard_map/coded/pallas_call | solution.py:371
  24.9 2.1 %collective-permute-start.4 = (bf16[3,16,16,128]{3,2,1,0:T(8,128)(2,1)S(1)}, bf16[3,16,16,128]{3,2,1,0:T(8,128)(2,1)S(1)}, u32[]{:S(2)}, u32[]{:S(2)}) collective-permute-start(bf16[3,16,16,128]{3,2,1,0:T(8,128)(2,1)S(1)} %get-tuple-element.32), channel_id=1, source_target_pairs={{3,2},{0,1},{7,6},{4,5},{11,10},{8,9},{15,14},{12,13},{19,18},{16,... | collective-permute-start | bytes 589832 | tf_op jit(solution)/shard_map/ppermute | solution.py:43
  28.4 2.1 %collective-permute-start.6 = (bf16[3,16,16,128]{3,2,1,0:T(8,128)(2,1)S(1)}, bf16[3,16,16,128]{3,2,1,0:T(8,128)(2,1)S(1)}, u32[]{:S(2)}, u32[]{:S(2)}) collective-permute-start(bf16[3,16,16,128]{3,2,1,0:T(8,128)(2,1)S(1)} %get-tuple-element.33), channel_id=1, source_target_pairs={{3,1},{0,2},{1,0},{2,3},{7,5},{4,6},{5,4},{6,7},{11,9},{8,10},{9,8... | collective-permute-start | bytes 589832 | tf_op jit(solution)/shard_map/ppermute | solution.py:43
  31.6 2.5 %collective-permute-start.5 = (bf16[3,16,16,128]{3,2,1,0:T(8,128)(2,1)S(1)}, bf16[3,16,16,128]{3,2,1,0:T(8,128)(2,1)S(1)}, u32[]{:S(2)}, u32[]{:S(2)}) collective-permute-start(bf16[3,16,16,128]{3,2,1,0:T(8,128)(2,1)S(1)} %join.1), channel_id=1, source_target_pairs={{2,0},{1,3},{0,1},{3,2},{6,4},{5,7},{4,5},{7,6},{10,8},{9,11},{8,9... | collective-permute-start | bytes 589832 | tf_op jit(solution)/shard_map/ppermute | solution.py:43
  35.8 6.0 %collective-permute-done.5.fa = bf16[3,16,16,128]{3,2,1,0:T(8,128)(2,1)S(1)} collective-permute-done((bf16[3,16,16,128]{3,2,1,0:T(8,128)(2,1)S(1)}, bf16[3,16,16,128]{3,2,1,0:T(8,128)(2,1)S(1)}, u32[]{:S(2)}, u32[]{:S(2)}) %collective-permute-start.5) | collective-permute-done | bytes 196640 | tf_op jit(solution)/shard_map/ppermute | solution.py:43
  42.9 4.0 %collective-permute-start.9 = (bf16[3,16,16,128]{3,2,1,0:T(8,128)(2,1)S(1)}, bf16[3,16,16,128]{3,2,1,0:T(8,128)(2,1)S(1)}, u32[]{:S(2)}, u32[]{:S(2)}) collective-permute-start(bf16[3,16,16,128]{3,2,1,0:T(8,128)(2,1)S(1)} %get-tuple-element.40), channel_id=1, source_target_pairs={{1,3},{2,0},{0,1},{3,2},{5,7},{6,4},{4,5},{7,6},{9,11},{10,8},{8,9... | collective-permute-start | bytes 589832 | tf_op jit(solution)/shard_map/ppermute | solution.py:43
  49.0 7.0 %collective-permute-done.9.refs_1_ = bf16[3,16,16,128]{3,2,1,0:T(8,128)(2,1)S(1)} collective-permute-done((bf16[3,16,16,128]{3,2,1,0:T(8,128)(2,1)S(1)}, bf16[3,16,16,128]{3,2,1,0:T(8,128)(2,1)S(1)}, u32[]{:S(2)}, u32[]{:S(2)}) %collective-permute-start.9) | collective-permute-done | bytes 196640 | tf_op jit(solution)/shard_map/ppermute | solution.py:43
  55.9 1.9 %collective-permute-done.11.refs_3_ = bf16[3,16,16,128]{3,2,1,0:T(8,128)(2,1)S(1)} collective-permute-done((bf16[3,16,16,128]{3,2,1,0:T(8,128)(2,1)S(1)}, bf16[3,16,16,128]{3,2,1,0:T(8,128)(2,1)S(1)}, u32[]{:S(2)}, u32[]{:S(2)}) %collective-permute-start.11) | collective-permute-done | bytes 196640 | tf_op jit(solution)/shard_map/ppermute | solution.py:43
  57.8 2.4 %away.1 = (bf16[256,1024]{1,0:T(8,128)(2,1)S(1)}, bf16[3,1024,256]{2,1,0:T(8,128)(2,1)S(1)}) custom-call(bf16[512,3072]{1,0:T(8,128)(2,1)S(1)} %get-tuple-element.26.refs_4_.wd_ref, bf16[512,128]{1,0:T(8,128)(2,1)S(1)} %get-tuple-element.36.left_ref, f32[512,128]{1,0:T(8,128)S(1)} %get-tuple-element.37.pull_ref, f32[512,3]{1,0:T(8,128)S(1)} %bitcast.6, ...), custom_call_target="tpu_custom_call" | custom-call | flops 805306368 | bytes 3145728 | tf_op jit(solution)/shard_map/away/pallas_call | solution.py:403
  60.3 2.3 %home.1.keep = f32[256,1024]{1,0:T(8,128)S(1)} custom-call(bf16[512,3072]{1,0:T(8,128)(2,1)S(1)} %get-tuple-element.26.refs_4_.wd_ref, bf16[512,128]{1,0:T(8,128)(2,1)S(1)} %get-tuple-element.36.left_ref, f32[512,128]{1,0:T(8,128)S(1)} %get-tuple-element.37.pull_ref, f32[512,3]{1,0:T(8,128)S(1)} %bitcast.7, ...), custom_call_target="tpu_custom_call" | custom-call | flops 805306368 | bytes 3145728 | tf_op jit(solution)/shard_map/home/pallas_call | solution.py:410
  62.8 1.5 %collective-permute-start.13 = (bf16[64,1024]{1,0:T(8,128)(2,1)S(1)}, bf16[64,1024]{1,0:T(8,128)(2,1)S(1)}, u32[]{:S(2)}, u32[]{:S(2)}) collective-permute-start(bf16[64,1024]{1,0:T(8,128)(2,1)S(1)} %get-tuple-element.44), channel_id=1, source_target_pairs={{0,8},{4,12},{8,0},{12,4},{16,24},{20,28},{24,16},{28,20},{1,9},{5... | collective-permute-start | bytes 393224 | tf_op jit(solution)/shard_map/ppermute | solution.py:43
  64.3 1.5 %collective-permute-start.14 = (bf16[64,1024]{1,0:T(8,128)(2,1)S(1)}, bf16[64,1024]{1,0:T(8,128)(2,1)S(1)}, u32[]{:S(2)}, u32[]{:S(2)}) collective-permute-start(bf16[64,1024]{1,0:T(8,128)(2,1)S(1)} %get-tuple-element.45), channel_id=1, source_target_pairs={{0,16},{4,20},{8,24},{12,28},{16,0},{20,4},{24,8},{28,12},{1,17},{... | collective-permute-start | bytes 393224 | tf_op jit(solution)/shard_map/ppermute | solution.py:43
  66.3 2.8 %collective-permute-done.13.refs_0_ = bf16[64,1024]{1,0:T(8,128)(2,1)S(1)} collective-permute-done((bf16[64,1024]{1,0:T(8,128)(2,1)S(1)}, bf16[64,1024]{1,0:T(8,128)(2,1)S(1)}, u32[]{:S(2)}, u32[]{:S(2)}) %collective-permute-start.13) | collective-permute-done | bytes 131104 | tf_op jit(solution)/shard_map/ppermute | solution.py:43
  69.1 3.6 %collective-permute-done.14.refs_1_ = bf16[64,1024]{1,0:T(8,128)(2,1)S(1)} collective-permute-done((bf16[64,1024]{1,0:T(8,128)(2,1)S(1)}, bf16[64,1024]{1,0:T(8,128)(2,1)S(1)}, u32[]{:S(2)}, u32[]{:S(2)}) %collective-permute-start.14) | collective-permute-done | bytes 131104 | tf_op jit(solution)/shard_map/ppermute | solution.py:43
  75.0 1.4 %collective-permute-start.18 = (bf16[64,1024]{1,0:T(8,128)(2,1)S(1)}, bf16[64,1024]{1,0:T(8,128)(2,1)S(1)}, u32[]{:S(2)}, u32[]{:S(2)}) collective-permute-start(bf16[64,1024]{1,0:T(8,128)(2,1)S(1)} %shard.1.own), channel_id=1, source_target_pairs={{0,24},{4,28},{8,16},{12,20},{16,8},{20,12},{24,0},{28,4},{1,25},{... | collective-permute-start | bytes 393224 | tf_op jit(solution)/shard_map/ppermute | solution.py:43
  76.4 2.1 %collective-permute-done.16.refs_0_ = bf16[64,1024]{1,0:T(8,128)(2,1)S(1)} collective-permute-done((bf16[64,1024]{1,0:T(8,128)(2,1)S(1)}, bf16[64,1024]{1,0:T(8,128)(2,1)S(1)}, u32[]{:S(2)}, u32[]{:S(2)}) %collective-permute-start.16) | collective-permute-done | bytes 131104 | tf_op jit(solution)/shard_map/ppermute | solution.py:43
  78.5 3.2 %collective-permute-done.17.refs_1_ = bf16[64,1024]{1,0:T(8,128)(2,1)S(1)} collective-permute-done((bf16[64,1024]{1,0:T(8,128)(2,1)S(1)}, bf16[64,1024]{1,0:T(8,128)(2,1)S(1)}, u32[]{:S(2)}, u32[]{:S(2)}) %collective-permute-start.17) | collective-permute-done | bytes 131104 | tf_op jit(solution)/shard_map/ppermute | solution.py:43
  81.9 1.9 %collective-permute-done.19.other = bf16[256,1024]{1,0:T(8,128)(2,1)S(1)} collective-permute-done((bf16[256,1024]{1,0:T(8,128)(2,1)S(1)}, bf16[256,1024]{1,0:T(8,128)(2,1)S(1)}, u32[]{:S(2)}, u32[]{:S(2)}) %collective-permute-start.19) | collective-permute-done | bytes 524320 | tf_op jit(solution)/shard_map/ppermute | solution.py:43
  83.9 2.6 %collective-permute-start.21 = (f32[8,128]{1,0:T(8,128)S(1)}, f32[8,128]{1,0:T(8,128)S(1)}, u32[]{:S(2)}, u32[]{:S(2)}) collective-permute-start(f32[8,128]{1,0:T(8,128)S(1)} %tally.1.refs_0_), channel_id=1, source_target_pairs={{0,2},{1,3},{2,0},{3,1},{4,6},{5,7},{6,4},{7,5},{8,10},{9,11},{10,... | collective-permute-start | bytes 12296 | tf_op jit(solution)/shard_map/ppermute | solution.py:43
  87.7 1.6 %collective-permute-done.20.refs_1_ = f32[8,128]{1,0:T(8,128)S(1)} collective-permute-done((f32[8,128]{1,0:T(8,128)S(1)}, f32[8,128]{1,0:T(8,128)S(1)}, u32[]{:S(2)}, u32[]{:S(2)}) %collective-permute-start.20) | collective-permute-done | bytes 4128 | tf_op jit(solution)/shard_map/ppermute | solution.py:43
  (44 shorter events, 18.8 us)
Async XLA Ops:
  0.6 11.5 %collective-permute-start = (bf16[3,16,16,128]{3,2,1,0:T(8,128)(2,1)}, bf16[3,16,16,128]{3,2,1,0:T(8,128)(2,1)S(1)}, u32[]{:S(2)}, u32[]{:S(2)}) collective-permute-start(bf16[3,16,16,128]{3,2,1,0:T(8,128)(2,1)} %bitcast.8), channel_id=1, source_target_pairs={{0,2},{3,1},{1,0},{2,3},{4,6},{7,5},{5,4},{6,7},{8,10},{11,9},{9,8... | collective-permute-start | bytes 589832 | tf_op jit(solution)/shard_map/ppermute | solution.py:43
  11.4 8.7 %collective-permute-start.1 = (bf16[3,16,16,128]{3,2,1,0:T(8,128)(2,1)S(1)}, bf16[3,16,16,128]{3,2,1,0:T(8,128)(2,1)S(1)}, u32[]{:S(2)}, u32[]{:S(2)}) collective-permute-start(bf16[3,16,16,128]{3,2,1,0:T(8,128)(2,1)S(1)} %get-tuple-element.27), channel_id=1, source_target_pairs={{1,3},{2,0},{0,1},{3,2},{5,7},{6,4},{4,5},{7,6},{9,11},{10,8},{8,9... | collective-permute-start | bytes 589832 | tf_op jit(solution)/shard_map/ppermute | solution.py:43
  11.4 8.7 %collective-permute-start.2 = (bf16[3,16,16,128]{3,2,1,0:T(8,128)(2,1)S(1)}, bf16[3,16,16,128]{3,2,1,0:T(8,128)(2,1)S(1)}, u32[]{:S(2)}, u32[]{:S(2)}) collective-permute-start(bf16[3,16,16,128]{3,2,1,0:T(8,128)(2,1)S(1)} %get-tuple-element.27), channel_id=1, source_target_pairs={{1,2},{2,1},{5,6},{6,5},{9,10},{10,9},{13,14},{14,13},{17,18},{18,... | collective-permute-start | bytes 589832 | tf_op jit(solution)/shard_map/ppermute | solution.py:43
  12.1 11.1 %collective-permute-start.3 = (bf16[3,16,16,128]{3,2,1,0:T(8,128)(2,1)S(1)}, bf16[3,16,16,128]{3,2,1,0:T(8,128)(2,1)S(1)}, u32[]{:S(2)}, u32[]{:S(2)}) collective-permute-start(bf16[3,16,16,128]{3,2,1,0:T(8,128)(2,1)S(1)} %collective-permute-done.refs_0_), channel_id=1, source_target_pairs={{2,3},{1,0},{6,7},{5,4},{10,11},{9,8},{14,15},{13,12},{18,19},{17,... | collective-permute-start | bytes 589832 | tf_op jit(solution)/shard_map/ppermute | solution.py:43
  24.9 6.6 %collective-permute-start.4 = (bf16[3,16,16,128]{3,2,1,0:T(8,128)(2,1)S(1)}, bf16[3,16,16,128]{3,2,1,0:T(8,128)(2,1)S(1)}, u32[]{:S(2)}, u32[]{:S(2)}) collective-permute-start(bf16[3,16,16,128]{3,2,1,0:T(8,128)(2,1)S(1)} %get-tuple-element.32), channel_id=1, source_target_pairs={{3,2},{0,1},{7,6},{4,5},{11,10},{8,9},{15,14},{12,13},{19,18},{16,... | collective-permute-start | bytes 589832 | tf_op jit(solution)/shard_map/ppermute | solution.py:43
  27.1 8.7 %collective-permute-start.7 = (bf16[3,16,16,128]{3,2,1,0:T(8,128)(2,1)S(1)}, bf16[3,16,16,128]{3,2,1,0:T(8,128)(2,1)S(1)}, u32[]{:S(2)}, u32[]{:S(2)}) collective-permute-start(bf16[3,16,16,128]{3,2,1,0:T(8,128)(2,1)S(1)} %get-tuple-element.32), channel_id=1, source_target_pairs={{2,1},{1,2},{6,5},{5,6},{10,9},{9,10},{14,13},{13,14},{18,17},{17,... | collective-permute-start | bytes 589832 | tf_op jit(solution)/shard_map/ppermute | solution.py:43
  28.4 13.6 %copy-start.1 = (bf16[1,3,16,16,128]{4,3,2,1,0:T(8,128)(2,1)S(1)}, bf16[1,3,16,16,128]{4,3,2,1,0:T(8,128)(2,1)}, u32[]{:S(2)}) copy-start(bf16[1,3,16,16,128]{4,3,2,1,0:T(8,128)(2,1)} %param.3) | copy-start | bytes 589828
  28.4 7.5 %collective-permute-start.6 = (bf16[3,16,16,128]{3,2,1,0:T(8,128)(2,1)S(1)}, bf16[3,16,16,128]{3,2,1,0:T(8,128)(2,1)S(1)}, u32[]{:S(2)}, u32[]{:S(2)}) collective-permute-start(bf16[3,16,16,128]{3,2,1,0:T(8,128)(2,1)S(1)} %get-tuple-element.33), channel_id=1, source_target_pairs={{3,1},{0,2},{1,0},{2,3},{7,5},{4,6},{5,4},{6,7},{11,9},{8,10},{9,8... | collective-permute-start | bytes 589832 | tf_op jit(solution)/shard_map/ppermute | solution.py:43
  31.6 10.3 %collective-permute-start.5 = (bf16[3,16,16,128]{3,2,1,0:T(8,128)(2,1)S(1)}, bf16[3,16,16,128]{3,2,1,0:T(8,128)(2,1)S(1)}, u32[]{:S(2)}, u32[]{:S(2)}) collective-permute-start(bf16[3,16,16,128]{3,2,1,0:T(8,128)(2,1)S(1)} %join.1), channel_id=1, source_target_pairs={{2,0},{1,3},{0,1},{3,2},{6,4},{5,7},{4,5},{7,6},{10,8},{9,11},{8,9... | collective-permute-start | bytes 589832 | tf_op jit(solution)/shard_map/ppermute | solution.py:43
  41.9 5.7 %collective-permute-start.8 = (bf16[3,16,16,128]{3,2,1,0:T(8,128)(2,1)S(1)}, bf16[3,16,16,128]{3,2,1,0:T(8,128)(2,1)S(1)}, u32[]{:S(2)}, u32[]{:S(2)}) collective-permute-start(bf16[3,16,16,128]{3,2,1,0:T(8,128)(2,1)S(1)} %get-tuple-element.35.e_ref), channel_id=1, source_target_pairs={{0,2},{3,1},{1,0},{2,3},{4,6},{7,5},{5,4},{6,7},{8,10},{11,9},{9,8... | collective-permute-start | bytes 589832 | tf_op jit(solution)/shard_map/ppermute | solution.py:43
  42.3 6.7 %collective-permute-start.10 = (bf16[3,16,16,128]{3,2,1,0:T(8,128)(2,1)S(1)}, bf16[3,16,16,128]{3,2,1,0:T(8,128)(2,1)S(1)}, u32[]{:S(2)}, u32[]{:S(2)}) collective-permute-start(bf16[3,16,16,128]{3,2,1,0:T(8,128)(2,1)S(1)} %get-tuple-element.40), channel_id=1, source_target_pairs={{1,2},{2,1},{5,6},{6,5},{9,10},{10,9},{13,14},{14,13},{17,18},{18,... | collective-permute-start | bytes 589832 | tf_op jit(solution)/shard_map/ppermute | solution.py:43
  42.9 13.0 %collective-permute-start.9 = (bf16[3,16,16,128]{3,2,1,0:T(8,128)(2,1)S(1)}, bf16[3,16,16,128]{3,2,1,0:T(8,128)(2,1)S(1)}, u32[]{:S(2)}, u32[]{:S(2)}) collective-permute-start(bf16[3,16,16,128]{3,2,1,0:T(8,128)(2,1)S(1)} %get-tuple-element.40), channel_id=1, source_target_pairs={{1,3},{2,0},{0,1},{3,2},{5,7},{6,4},{4,5},{7,6},{9,11},{10,8},{8,9... | collective-permute-start | bytes 589832 | tf_op jit(solution)/shard_map/ppermute | solution.py:43
  47.7 10.2 %collective-permute-start.11 = (bf16[3,16,16,128]{3,2,1,0:T(8,128)(2,1)S(1)}, bf16[3,16,16,128]{3,2,1,0:T(8,128)(2,1)S(1)}, u32[]{:S(2)}, u32[]{:S(2)}) collective-permute-start(bf16[3,16,16,128]{3,2,1,0:T(8,128)(2,1)S(1)} %collective-permute-done.8.refs_0_), channel_id=1, source_target_pairs={{2,3},{1,0},{6,7},{5,4},{10,11},{9,8},{14,15},{13,12},{18,19},{17,... | collective-permute-start | bytes 589832 | tf_op jit(solution)/shard_map/ppermute | solution.py:43
  60.2 2.4 %collective-permute-start.12 = (bf16[256,1024]{1,0:T(8,128)(2,1)S(1)}, bf16[256,1024]{1,0:T(8,128)(2,1)S(1)}, u32[]{:S(2)}, u32[]{:S(2)}) collective-permute-start(bf16[256,1024]{1,0:T(8,128)(2,1)S(1)} %get-tuple-element.42), channel_id=1, source_target_pairs={{0,4},{4,0},{8,12},{12,8},{16,20},{20,16},{24,28},{28,24},{1,5},{5... | collective-permute-start | bytes 1572872 | tf_op jit(solution)/shard_map/ppermute | solution.py:43
  62.8 6.4 %collective-permute-start.13 = (bf16[64,1024]{1,0:T(8,128)(2,1)S(1)}, bf16[64,1024]{1,0:T(8,128)(2,1)S(1)}, u32[]{:S(2)}, u32[]{:S(2)}) collective-permute-start(bf16[64,1024]{1,0:T(8,128)(2,1)S(1)} %get-tuple-element.44), channel_id=1, source_target_pairs={{0,8},{4,12},{8,0},{12,4},{16,24},{20,28},{24,16},{28,20},{1,9},{5... | collective-permute-start | bytes 393224 | tf_op jit(solution)/shard_map/ppermute | solution.py:43
  64.3 8.4 %collective-permute-start.14 = (bf16[64,1024]{1,0:T(8,128)(2,1)S(1)}, bf16[64,1024]{1,0:T(8,128)(2,1)S(1)}, u32[]{:S(2)}, u32[]{:S(2)}) collective-permute-start(bf16[64,1024]{1,0:T(8,128)(2,1)S(1)} %get-tuple-element.45), channel_id=1, source_target_pairs={{0,16},{4,20},{8,24},{12,28},{16,0},{20,4},{24,8},{28,12},{1,17},{... | collective-permute-start | bytes 393224 | tf_op jit(solution)/shard_map/ppermute | solution.py:43
  65.8 6.9 %collective-permute-start.15 = (bf16[64,1024]{1,0:T(8,128)(2,1)S(1)}, bf16[64,1024]{1,0:T(8,128)(2,1)S(1)}, u32[]{:S(2)}, u32[]{:S(2)}) collective-permute-start(bf16[64,1024]{1,0:T(8,128)(2,1)S(1)} %get-tuple-element.46), channel_id=1, source_target_pairs={{0,24},{4,28},{8,16},{12,20},{16,8},{20,12},{24,0},{28,4},{1,25},{... | collective-permute-start | bytes 393224 | tf_op jit(solution)/shard_map/ppermute | solution.py:43
  72.9 5.6 %collective-permute-start.16 = (bf16[64,1024]{1,0:T(8,128)(2,1)S(1)}, bf16[64,1024]{1,0:T(8,128)(2,1)S(1)}, u32[]{:S(2)}, u32[]{:S(2)}) collective-permute-start(bf16[64,1024]{1,0:T(8,128)(2,1)S(1)} %shard.1.own), channel_id=1, source_target_pairs={{0,8},{4,12},{8,0},{12,4},{16,24},{20,28},{24,16},{28,20},{1,9},{5... | collective-permute-start | bytes 393224 | tf_op jit(solution)/shard_map/ppermute | solution.py:43
  74.2 7.5 %collective-permute-start.17 = (bf16[64,1024]{1,0:T(8,128)(2,1)S(1)}, bf16[64,1024]{1,0:T(8,128)(2,1)S(1)}, u32[]{:S(2)}, u32[]{:S(2)}) collective-permute-start(bf16[64,1024]{1,0:T(8,128)(2,1)S(1)} %shard.1.own), channel_id=1, source_target_pairs={{0,16},{4,20},{8,24},{12,28},{16,0},{20,4},{24,8},{28,12},{1,17},{... | collective-permute-start | bytes 393224 | tf_op jit(solution)/shard_map/ppermute | solution.py:43
  75.0 6.7 %collective-permute-start.18 = (bf16[64,1024]{1,0:T(8,128)(2,1)S(1)}, bf16[64,1024]{1,0:T(8,128)(2,1)S(1)}, u32[]{:S(2)}, u32[]{:S(2)}) collective-permute-start(bf16[64,1024]{1,0:T(8,128)(2,1)S(1)} %shard.1.own), channel_id=1, source_target_pairs={{0,24},{4,28},{8,16},{12,20},{16,8},{20,12},{24,0},{28,4},{1,25},{... | collective-permute-start | bytes 393224 | tf_op jit(solution)/shard_map/ppermute | solution.py:43
  81.8 2.0 %collective-permute-start.19 = (bf16[256,1024]{1,0:T(8,128)(2,1)S(1)}, bf16[256,1024]{1,0:T(8,128)(2,1)S(1)}, u32[]{:S(2)}, u32[]{:S(2)}) collective-permute-start(bf16[256,1024]{1,0:T(8,128)(2,1)S(1)} %gather.1.mine), channel_id=1, source_target_pairs={{0,4},{4,0},{8,12},{12,8},{16,20},{20,16},{24,28},{28,24},{1,5},{5... | collective-permute-start | bytes 1572872 | tf_op jit(solution)/shard_map/ppermute | solution.py:43
  83.8 5.5 %collective-permute-start.20 = (f32[8,128]{1,0:T(8,128)S(1)}, f32[8,128]{1,0:T(8,128)S(1)}, u32[]{:S(2)}, u32[]{:S(2)}) collective-permute-start(f32[8,128]{1,0:T(8,128)S(1)} %tally.1.refs_0_), channel_id=1, source_target_pairs={{0,1},{1,2},{2,3},{3,0},{4,5},{5,6},{6,7},{7,4},{8,9},{9,10},{10,1... | collective-permute-start | bytes 12296 | tf_op jit(solution)/shard_map/ppermute | solution.py:43
  83.9 5.4 %collective-permute-start.21 = (f32[8,128]{1,0:T(8,128)S(1)}, f32[8,128]{1,0:T(8,128)S(1)}, u32[]{:S(2)}, u32[]{:S(2)}) collective-permute-start(f32[8,128]{1,0:T(8,128)S(1)} %tally.1.refs_0_), channel_id=1, source_target_pairs={{0,2},{1,3},{2,0},{3,1},{4,6},{5,7},{6,4},{7,5},{8,10},{9,11},{10,... | collective-permute-start | bytes 12296 | tf_op jit(solution)/shard_map/ppermute | solution.py:43
  86.4 3.6 %collective-permute-start.22 = (f32[8,128]{1,0:T(8,128)S(1)}, f32[8,128]{1,0:T(8,128)S(1)}, u32[]{:S(2)}, u32[]{:S(2)}) collective-permute-start(f32[8,128]{1,0:T(8,128)S(1)} %tally.1.refs_0_), channel_id=1, source_target_pairs={{0,3},{1,0},{2,1},{3,2},{4,7},{5,4},{6,5},{7,6},{8,11},{9,8},{10,9... | collective-permute-start | bytes 12296 | tf_op jit(solution)/shard_map/ppermute | solution.py:43
  (2 other events, 2.2 us)

commit v3 on v2

--- a/solution.py
+++ b/solution.py
@@ -7,6 +7,7 @@
 from jax.experimental import pallas as pl
 from jax.experimental.pallas import tpu as pltpu
 from jax.sharding import PartitionSpec as P
+
 
 FIELD = 18
 MAPS = 8
@@ -61,24 +62,32 @@
         return (
             [(0, 2), (3, 1), (1, 0), (2, 3)],
             [(1, 3), (2, 0), (0, 1), (3, 2)],
-            [(1, 2), (2, 1)],
-            [(2, 3), (1, 0)],
+            [(1, 2), (2, 1), (0, 0), (3, 3)],
+            [(2, 3), (1, 0), (0, 1), (3, 2)],
         )
     return ring(n_tile, -1), ring(n_tile, -side), ring(n_tile, -side - 1), None
+
+
+def inner_tile():
+    t = lax.axis_index("tile")
+    return (t == 1) | (t == 2)
 
 
 def quadrants():
     if lax.axis_size("tile") != RELAY_TILES:
         return 1, 2, 3
     t = lax.axis_index("tile")
-    inner = (t == 1) | (t == 2)
-    first = jnp.where(inner, 2, jnp.where(t == 0, 1, 3))
+    first = jnp.where(inner_tile(), 2, jnp.where(t == 0, 1, 3))
     second = jnp.where(t == 1, 3, jnp.where(t == 2, 1, 2))
     third = jnp.where(t % 2 == 0, 3, 1)
     return first, second, third
 
 
-def kernel_call(body, outs, scratch=(), n_in=0, flops=0, name=None, scalar_out=False):
+def spilled():
+    return quadrants()[::-1]
+
+
+def kernel_call(body, outs, scratch=(), n_in=0, flops=0, scalar_out=False):
     places = [pltpu.VMEM] * (len(outs) - scalar_out) + [pltpu.SMEM] * scalar_out
     return pl.pallas_call(
         body,
@@ -88,7 +97,6 @@
         scratch_shapes=list(scratch),
         compiler_params=pltpu.CompilerParams(vmem_limit_bytes=VMEM_CAP),
         cost_estimate=pl.CostEstimate(flops=flops, transcendentals=0, bytes_accessed=flops // 256),
-        name=name,
     )
 
 
@@ -101,28 +109,31 @@
 
 
 def place(dst, own, slots):
-    for q, load in zip((0,) + tuple(quadrants()), (own,) + tuple(slots)):
+    def put(q, ref):
         top = pl.multiple_of(q // 2 * TILE_PX, TILE_PX)
         left = pl.multiple_of(q % 2 * TILE_PX, TILE_PX)
         for ch in range(3):
-            dst[ch, pl.ds(top, TILE_PX), pl.ds(left, TILE_PX), :] = load(ch)
-
-
-def loader(*refs):
-    def load(ch):
-        value = refs[0][ch]
-        for ref in refs[1:]:
-            value = value + ref[ch]
-        return value
-
-    return load
-
-
-def expand_body(w_ref, con_ref, x_ref, wd_ref, wt_ref, st_ref, copy_ref, wp_ref, v_ref, s_ref):
+            dst[ch, pl.ds(top, TILE_PX), pl.ds(left, TILE_PX), :] = ref[ch]
+
+    first, second, third = quadrants()
+    put(0, own)
+    put(first, slots[0])
+    put(second, slots[1])
+    if len(slots) == 3:
+        put(third, slots[2])
+    else:
+        inner = inner_tile()
+        pl.when(inner)(lambda: put(third, slots[2]))
+        pl.when(jnp.logical_not(inner))(lambda: put(third, slots[3]))
+
+
+def stage_body(w_ref, x_ref, wp_ref, copy_ref):
     copy_ref[...] = x_ref[...]
     wp_ref[:, PAD_IN - LANES :] = jnp.zeros((UNITS, LANES), BF)
     wp_ref[:, :INPUTS] = w_ref[...]
 
+
+def expand_body(wp_ref, con_ref, wd_ref, wt_ref, st_ref, v_ref, s_ref):
     def wanted(shape, axis):
         n = lax.broadcasted_iota(jnp.int32, shape, axis)
         row, col = n // SPAN, n % SPAN
@@ -164,55 +175,60 @@
                 wt_ref[q, to : to + TILE_PX, :] = flipped[sub : sub + TILE_PX]
 
 
-def coded_body(relay, x_ref, *refs):
-    slots, (wd_ref, wt_ref, coded_ref, out_ref, xe) = refs[: 4 if relay else 3], refs[-5:]
-    third = slots[2:]
-    place(xe, loader(x_ref), (loader(slots[0]), loader(slots[1]), loader(*third)))
+def decoded(wt_ref, q, rounded, shape):
+    return jnp.dot(wt_ref[q], rounded, preferred_element_type=F32).reshape(shape)
+
+
+def coded_body(x_ref, *refs):
+    slots, (wd_ref, wt_ref, coded_ref, out_ref, xe) = refs[:-5], refs[-5:]
+    place(xe, x_ref, slots)
     batch = x_ref.shape[-1]
     coded = jnp.dot(wd_ref[...], xe[...].reshape(3 * PLANE, batch), preferred_element_type=F32)
     coded_ref[...] = coded
-    part = jnp.dot(wt_ref[quadrants()[2]], coded.astype(BF), preferred_element_type=F32)
-    out_ref[...] = part.astype(BF).reshape(out_ref.shape)
-
-
-def spill_body(wt_ref, coded_ref, a_ref, b_ref):
+    out_ref[...] = decoded(wt_ref, spilled()[0], coded.astype(BF), out_ref.shape).astype(BF)
+
+
+def spill_body(wt_ref, coded_ref, *outs):
     rounded = coded_ref[...].astype(BF)
-    first, second, _ = quadrants()
-    for q, ref in ((second, b_ref), (first, a_ref)):
-        part = jnp.dot(wt_ref[q], rounded, preferred_element_type=F32)
-        ref[...] = part.astype(BF).reshape(ref.shape)
-
-
-def own_body(wt_ref, coded_ref, x_ref, own_ref, loss_ref):
+    for q, ref in zip(spilled()[1:], outs):
+        ref[...] = decoded(wt_ref, q, rounded, ref.shape).astype(BF)
+
+
+def own_body(wt_ref, coded_ref, x_ref, own_ref, loss_ref, *last):
     coded = coded_ref[...]
+    rounded = coded.astype(BF)
     batch = coded.shape[-1]
-    part = jnp.dot(wt_ref[0], coded.astype(BF), preferred_element_type=F32)
-    own_ref[...] = part.reshape(own_ref.shape) - x_ref[...].astype(F32)
+    for ref in last:
+        ref[...] = decoded(wt_ref, spilled()[2], rounded, ref.shape)
+    own_ref[...] = decoded(wt_ref, 0, rounded, own_ref.shape) - x_ref[...].astype(F32)
     root = jnp.sqrt(smooth_eps + coded * coded)
     loss_ref[...] = sparsity_weight * jnp.sum(root.reshape(UNITS // 8, 8, batch), 0)
 
 
-def join_body(a_ref, d_ref, out_ref):
-    out_ref[...] = (a_ref[...].astype(F32) + d_ref[...].astype(F32)).astype(BF)
-
-
-def error_body(own, fa, fb, fc, sp, e_ref, loss_ref):
+def join_body(last, passed, out_ref):
+    out_ref[...] = (last[...] + passed[...].astype(F32)).astype(BF)
+
+
+def error_body(own, sp, *refs):
+    parts, (e_ref, loss_ref) = refs[:-2], refs[-2:]
     batch = own.shape[-1]
     total = sp[...]
     for ch in range(3):
-        err = own[ch] + fa[ch].astype(F32) + fb[ch].astype(F32) + fc[ch].astype(F32)
+        err = own[ch]
+        for ref in parts:
+            err = err + ref[ch].astype(F32)
         e_ref[ch] = err.astype(BF)
         total = total + jnp.sum((err * err).reshape(QUAD // 8, 8, batch), 0)
     loss_ref[...] = total
 
 
-def ready_body(relay, coded_ref, e_ref, x_ref, *refs):
+def ready_body(coded_ref, e_ref, x_ref, *refs):
     slots, (left_ref, pull_ref, xe, copy_ref) = refs[:-4], refs[-4:]
     copy_ref[...] = e_ref[...]
     coded = coded_ref[...]
     left_ref[...] = (2.0 * coded).astype(BF)
     pull_ref[...] = sparsity_weight * coded / jnp.sqrt(smooth_eps + coded * coded)
-    place(xe, loader(x_ref), (loader(slots[0]), loader(slots[1]), loader(*slots[2:])))
+    place(xe, x_ref, slots)
 
 
 def gradient_rows(half, wd_ref, left_ref, pull_ref, con_ref, st_ref, ex, gd, gs, out):
@@ -243,10 +259,10 @@
         out[:, cols] = out[:, cols] + jnp.dot(gs[...], st_ref[ch], preferred_element_type=F32)
 
 
-def away_body(relay, wd_ref, left_ref, pull_ref, con_ref, st_ref, xe, e_ref, *refs):
+def away_body(wd_ref, left_ref, pull_ref, con_ref, st_ref, xe, e_ref, *refs):
     slots, (send_ref, ex, tmp, gd, gs, out) = refs[:-6], refs[-6:]
     batch = e_ref.shape[-1]
-    place(tmp, loader(e_ref), (loader(slots[0]), loader(slots[1]), loader(*slots[2:])))
+    place(tmp, e_ref, slots)
     for ch in range(3):
         ex[ch, :, :batch] = tmp[ch].reshape(PLANE, batch)
         ex[ch, :, batch:] = xe[ch].reshape(PLANE, batch)
@@ -347,68 +363,69 @@
         first = send(now, "tile", to_first)
         second = send(later, "tile", to_second)
         third = send(later, "tile", to_third)
-        return [first, second, third] + ([send(first, "tile", onward)] if relay else [])
+        if not relay:
+            return [first, second, third]
+        return [first, second, third, send(first, "tile", onward)]
 
     x0 = frames[0]
     con = connect.reshape(UNITS, 3).astype(F32)
-    wd, wt, st, x_late = kernel_call(
+    wp, x_late = kernel_call(
+        stage_body, (sds((UNITS, PAD_IN), BF), sds(quad, BF)), n_in=2, flops=mac // 64
+    )(weights.reshape(UNITS, INPUTS), x0)
+    xs = spread_out(x0, x_late if relay else x0)
+    wd, wt, st = kernel_call(
         expand_body,
-        (
-            sds((UNITS, 3 * PLANE), BF),
-            sds((4, 3 * QUAD, UNITS), BF),
-            sds((3, PAD_STRIP, GRAB), BF),
-            sds(quad, BF),
-        ),
-        [
-            pltpu.VMEM((UNITS, PAD_IN), BF),
-            pltpu.VMEM((UNITS, PAD_STRIP), F32),
-            pltpu.VMEM((GRAB, PAD_STRIP), BF),
-        ],
-        n_in=3, flops=4 * mac, name="expand",
-    )(weights.reshape(UNITS, INPUTS), con, x0)
-    xs = spread_out(x0, x_late if relay else x0)
-
-    coded, sc = kernel_call(
-        functools.partial(coded_body, relay),
+        (sds((UNITS, 3 * PLANE), BF), sds((4, 3 * QUAD, UNITS), BF), sds((3, PAD_STRIP, GRAB), BF)),
+        [pltpu.VMEM((UNITS, PAD_STRIP), F32), pltpu.VMEM((GRAB, PAD_STRIP), BF)],
+        n_in=2, flops=4 * mac,
+    )(wp, con)
+
+    coded, s1 = kernel_call(
+        coded_body,
         (sds(units, F32), sds(quad, BF)),
         [pltpu.VMEM(plane, BF)],
-        n_in=3 + len(xs), flops=mac, name="coded",
+        n_in=3 + len(xs), flops=mac,
     )(x0, *xs, wd, wt)
-    sa, sb = kernel_call(
-        spill_body, (sds(quad, BF), sds(quad, BF)), n_in=2, flops=mac // 2, name="spill"
+    parts = []
+    if relay:
+        passed = send(s1, "tile", [(0, 1), (3, 2)])
+    parts.append(send(s1, "tile", [(1, 2), (2, 1)] if relay else flip_all(to_third)))
+    s2, *s3 = kernel_call(
+        spill_body,
+        (sds(quad, BF),) * (1 if relay else 2),
+        n_in=2, flops=mac // 4,
     )(wt, coded)
-    if relay:
-        passed = send(sc, "tile", flip_all(onward))
-    fb = send(sb, "tile", flip_all(to_second))
-    fc = send(sc, "tile", flip_all(to_third))
-    own, sparse = kernel_call(
-        own_body, (sds(quad, F32), sds((8, batch), F32)), n_in=3, flops=mac // 4, name="own"
+    parts.append(send(s2, "tile", flip_all(to_second)))
+    own, sparse, *last = kernel_call(
+        own_body,
+        (sds(quad, F32), sds((8, batch), F32)) + (sds(quad, F32),) * relay,
+        n_in=3, flops=mac // 2,
     )(wt, coded, x0)
     if relay:
-        (sa,) = kernel_call(join_body, (sds(quad, BF),), n_in=2, flops=mac // 64, name="join")(sa, passed)
-    fa = send(sa, "tile", flip_all(to_first))
+        s3 = kernel_call(join_body, (sds(quad, BF),), n_in=2, flops=mac // 64)(last[0], passed)
+    parts.append(send(s3[0], "tile", flip_all(to_first)))
     e0, loss_part = kernel_call(
-        error_body, (sds(quad, BF), sds((8, batch), F32)), n_in=5, flops=mac // 32, name="errors"
-    )(own, fa, fb, fc, sparse)
+        error_body, (sds(quad, BF), sds((8, batch), F32)), n_in=2 + len(parts), flops=mac // 32
+    )(own, sparse, *parts)
 
     left, pull, xe, e_late = kernel_call(
-        functools.partial(ready_body, relay),
+        ready_body,
         (sds(units, BF), sds(units, F32), sds(plane, BF), sds(quad, BF)),
-        n_in=3 + len(xs), flops=mac // 16, name="ready",
+        n_in=3 + len(xs), flops=mac // 16,
     )(coded, e0, x0, *xs)
     es = spread_out(e0, e_late if relay else e0)
 
     half = (HALF, PAD_IN)
     work = [pltpu.VMEM((HALF, PLANE), F32), pltpu.VMEM((HALF, PAD_STRIP), BF)]
     away, ex = kernel_call(
-        functools.partial(away_body, relay),
+        away_body,
         (sds(half, BF), sds((3, PLANE, 2 * batch), BF)),
         [pltpu.VMEM(plane, BF)] + work + [pltpu.VMEM(half, F32)],
-        n_in=7 + len(es), flops=2 * mac, name="away",
+        n_in=7 + len(es), flops=2 * mac,
     )(wd, left, pull, con, st, xe, e0, *es)
     got = send(away, "dp", flips(n_dp, 1))
     (keep,) = kernel_call(
-        home_body, (sds(half, F32),), work, n_in=6, flops=2 * mac, name="home"
+        home_body, (sds(half, F32),), work, n_in=6, flops=2 * mac
     )(wd, left, pull, con, st, ex)
 
     rows = HALF // chips
@@ -417,19 +434,19 @@
         pair_body,
         (sds((rows, PAD_IN), F32),) + (shard,) * (chips - 1),
         [pltpu.VMEM(half, F32)],
-        n_in=2, flops=mac // 32, name="pair",
+        n_in=2, flops=mac // 32,
     )(keep, got)
     arrived = [send(v, "dp", flips(n_dp, 2 * (x + 1))) for x, v in enumerate(split[1:])]
-    (mine,) = kernel_call(shard_body, (shard,), n_in=chips + 1, flops=mac // 64, name="shard")(
+    (mine,) = kernel_call(shard_body, (shard,), n_in=chips + 1, flops=mac // 64)(
         split[0], *arrived, loss_part
     )
     others = [send(mine, "dp", flips(n_dp, 2 * x)) for x in range(1, chips)]
-    (mine_half,) = kernel_call(gather_body, (sds(half, BF),), n_in=chips, flops=mac // 64, name="gather")(
+    (mine_half,) = kernel_call(gather_body, (sds(half, BF),), n_in=chips, flops=mac // 64)(
         mine, *others
     )
     other_half = send(mine_half, "dp", flips(n_dp, 1))
     (tally,) = kernel_call(
-        functools.partial(tally_body, rows), (sds((8, LANES), F32),), n_in=2, flops=mac // 64, name="tally"
+        functools.partial(tally_body, rows), (sds((8, LANES), F32),), n_in=2, flops=mac // 64
     )(mine_half, other_half)
     tallies = [send(tally, "tile", ring(n_tile, s)) for s in range(1, n_tile)]
 
@@ -437,7 +454,7 @@
     update, loss = kernel_call(
         functools.partial(finish_body, float(entries), float(batch * n_dp)),
         (sds((UNITS, INPUTS), BF), sds((1, 1), F32)),
-        n_in=2 + n_tile, flops=mac // 32, name="finish", scalar_out=True,
+        n_in=2 + n_tile, flops=mac // 32, scalar_out=True,
     )(mine_half, other_half, tally, *tallies)
     return update.reshape(1, POS, MAPS, INPUTS), loss.reshape(())
 

time: 91.7 us -> 89.6 us (0.977)
  waiting for transfers between devices: 43.7 us -> 41.2 us
    ppermute x23, waiting for transfers between devices: 43.7 us -> 41.2 us  [send(): return lax.ppermute(value, axis, pairs)]
    pallas_call x10 -> x11, Pallas kernels: 7.95 us -> 8.02 us  [the longest x1 2.38 us: local(): kernel_call(away_body, (sds(half, BF), sds((3, PLANE, 2 * batch), BF)), [...]
  transfers between devices with their start and end apart: 23 -> 23, of which waited for: 15 -> 17; matrix products, arithmetic and copies ran while one was open for 1% -> 1% of each run, Pallas kernels for 8% -> 8%
where the time goes in v3:
time: 89.6 us; the launch traced here: 89.3 us
  waiting for transfers between devices  41.2 us (46%)
  starting transfers between devices  31.1 us (35%)
  Pallas kernels  13 us (15%)
  local copies, waits for them, and re-layouts  2.37 us (3%)
    ppermute x23, waiting for transfers between devices, send(): return lax.ppermute(value, axis, pairs)  41.2 us
    ppermute x23, starting transfers between devices, send(): return lax.ppermute(value, axis, pairs)  31.1 us
    pallas_call x1, Pallas kernels, local(): kernel_call(expand_body, (sds((UNITS, 3 * PLANE), BF), sds((4, 3 * QUAD,...  3.48 us
    pallas_call x1, Pallas kernels, local(): kernel_call(away_body, (sds(half, BF), sds((3, PLANE, 2 * batch), BF)), [...  2.38 us
    pallas_call x1, Pallas kernels, local(): kernel_call(home_body, (sds(half, F32),), work, n_in=6, flops=2 * mac)  2.28 us
    unnamed x6, local copies, waits for them, and re-layouts  2.19 us
  transfers between devices with their start and end apart: 23, of which 17 were waited for; matrix products, arithmetic and copies ran while one was open for 1% of the time, Pallas kernels for 8%

profile of v3, /device:TPU:0, one launch (start us, length us, event | category | flops | bytes accessed | tf_op | source)
XLA Modules:
  0.0 89.3 jit_solution(12719462720023305264)
XLA Ops:
  0.6 4.1 %collective-permute-start = (bf16[3,16,16,128]{3,2,1,0:T(8,128)(2,1)}, bf16[3,16,16,128]{3,2,1,0:T(8,128)(2,1)S(1)}, u32[]{:S(2)}, u32[]{:S(2)}) collective-permute-start(bf16[3,16,16,128]{3,2,1,0:T(8,128)(2,1)} %bitcast.5), channel_id=1, source_target_pairs={{0,2},{3,1},{1,0},{2,3},{4,6},{7,5},{5,4},{6,7},{8,10},{11,9},{9,8... | collective-permute-start | bytes 589832 | tf_op jit(solution)/shard_map/ppermute | solution.py:44
  7.9 3.4 %collective-permute-start.1 = (bf16[3,16,16,128]{3,2,1,0:T(8,128)(2,1)S(1)}, bf16[3,16,16,128]{3,2,1,0:T(8,128)(2,1)S(1)}, u32[]{:S(2)}, u32[]{:S(2)}) collective-permute-start(bf16[3,16,16,128]{3,2,1,0:T(8,128)(2,1)S(1)} %get-tuple-element.28), channel_id=1, source_target_pairs={{1,3},{2,0},{0,1},{3,2},{5,7},{6,4},{4,5},{7,6},{9,11},{10,8},{8,9... | collective-permute-start | bytes 589832 | tf_op jit(solution)/shard_map/ppermute | solution.py:44
  12.4 3.5 %shard_map.51 = (bf16[512,3072]{1,0:T(8,128)(2,1)S(1)}, bf16[4,768,512]{2,1,0:T(8,128)(2,1)S(1)}, bf16[3,640,512]{2,1,0:T(8,128)(2,1)S(1)}) custom-call(bf16[512,1024]{1,0:T(8,128)(2,1)S(1)} %get-tuple-element.26.wp_ref, f32[512,3]{1,0:T(8,128)S(1)} %bitcast.10), custom_call_target="tpu_custom_call" | custom-call | flops 1610612736 | bytes 6291456 | tf_op jit(solution)/shard_map/pallas_call | solution.py:376
  15.9 3.7 %collective-permute-done.1.refs_1_ = bf16[3,16,16,128]{3,2,1,0:T(8,128)(2,1)S(1)} collective-permute-done((bf16[3,16,16,128]{3,2,1,0:T(8,128)(2,1)S(1)}, bf16[3,16,16,128]{3,2,1,0:T(8,128)(2,1)S(1)}, u32[]{:S(2)}, u32[]{:S(2)}) %collective-permute-start.1) | collective-permute-done | bytes 196640 | tf_op jit(solution)/shard_map/ppermute | solution.py:44
  19.6 1.7 %collective-permute-done.3.refs_3_ = bf16[3,16,16,128]{3,2,1,0:T(8,128)(2,1)S(1)} collective-permute-done((bf16[3,16,16,128]{3,2,1,0:T(8,128)(2,1)S(1)}, bf16[3,16,16,128]{3,2,1,0:T(8,128)(2,1)S(1)}, u32[]{:S(2)}, u32[]{:S(2)}) %collective-permute-start.3) | collective-permute-done | bytes 196640 | tf_op jit(solution)/shard_map/ppermute | solution.py:44
  21.3 1.7 %shard_map.52 = (f32[512,128]{1,0:T(8,128)S(1)}, bf16[3,16,16,128]{3,2,1,0:T(8,128)(2,1)S(1)}) custom-call(bf16[3,16,16,128]{3,2,1,0:T(8,128)(2,1)S(1)} %bitcast.7, bf16[3,16,16,128]{3,2,1,0:T(8,128)(2,1)S(1)} %collective-permute-done.refs_0_, bf16[3,16,16,128]{3,2,1,0:T(8,128)(2,1)S(1)} %collective-permute-done.1.refs_1_, ...), custom_call_target="tpu_custom_call" | custom-call | flops 402653184 | bytes 1572864 | tf_op jit(solution)/shard_map/pallas_call | solution.py:383
  23.0 2.2 %collective-permute-start.6 = (bf16[3,16,16,128]{3,2,1,0:T(8,128)(2,1)S(1)}, bf16[3,16,16,128]{3,2,1,0:T(8,128)(2,1)S(1)}, u32[]{:S(2)}, u32[]{:S(2)}) collective-permute-start(bf16[3,16,16,128]{3,2,1,0:T(8,128)(2,1)S(1)} %get-tuple-element.33), channel_id=1, source_target_pairs={{0,1},{3,2},{4,5},{7,6},{8,9},{11,10},{12,13},{15,14},{16,17},{19,... | collective-permute-start | bytes 589832 | tf_op jit(solution)/shard_map/ppermute | solution.py:44
  26.3 2.1 %collective-permute-start.5 = (bf16[3,16,16,128]{3,2,1,0:T(8,128)(2,1)S(1)}, bf16[3,16,16,128]{3,2,1,0:T(8,128)(2,1)S(1)}, u32[]{:S(2)}, u32[]{:S(2)}) collective-permute-start(bf16[3,16,16,128]{3,2,1,0:T(8,128)(2,1)S(1)} %shard_map.54), channel_id=1, source_target_pairs={{3,1},{0,2},{1,0},{2,3},{7,5},{4,6},{5,4},{6,7},{11,9},{8,10},{9,8... | collective-permute-start | bytes 589832 | tf_op jit(solution)/shard_map/ppermute | solution.py:44
  30.2 2.5 %collective-permute-start.7 = (bf16[3,16,16,128]{3,2,1,0:T(8,128)(2,1)S(1)}, bf16[3,16,16,128]{3,2,1,0:T(8,128)(2,1)S(1)}, u32[]{:S(2)}, u32[]{:S(2)}) collective-permute-start(bf16[3,16,16,128]{3,2,1,0:T(8,128)(2,1)S(1)} %shard_map.55), channel_id=1, source_target_pairs={{2,0},{1,3},{0,1},{3,2},{6,4},{5,7},{4,5},{7,6},{10,8},{9,11},{8,9... | collective-permute-start | bytes 589832 | tf_op jit(solution)/shard_map/ppermute | solution.py:44
  32.7 1.6 %collective-permute-done.5.refs_1_ = bf16[3,16,16,128]{3,2,1,0:T(8,128)(2,1)S(1)} collective-permute-done((bf16[3,16,16,128]{3,2,1,0:T(8,128)(2,1)S(1)}, bf16[3,16,16,128]{3,2,1,0:T(8,128)(2,1)S(1)}, u32[]{:S(2)}, u32[]{:S(2)}) %collective-permute-start.5) | collective-permute-done | bytes 196640 | tf_op jit(solution)/shard_map/ppermute | solution.py:44
  34.3 5.2 %collective-permute-done.7.refs_2_ = bf16[3,16,16,128]{3,2,1,0:T(8,128)(2,1)S(1)} collective-permute-done((bf16[3,16,16,128]{3,2,1,0:T(8,128)(2,1)S(1)}, bf16[3,16,16,128]{3,2,1,0:T(8,128)(2,1)S(1)}, u32[]{:S(2)}, u32[]{:S(2)}) %collective-permute-start.7) | collective-permute-done | bytes 196640 | tf_op jit(solution)/shard_map/ppermute | solution.py:44
  40.7 4.0 %collective-permute-start.9 = (bf16[3,16,16,128]{3,2,1,0:T(8,128)(2,1)S(1)}, bf16[3,16,16,128]{3,2,1,0:T(8,128)(2,1)S(1)}, u32[]{:S(2)}, u32[]{:S(2)}) collective-permute-start(bf16[3,16,16,128]{3,2,1,0:T(8,128)(2,1)S(1)} %get-tuple-element.40), channel_id=1, source_target_pairs={{1,3},{2,0},{0,1},{3,2},{5,7},{6,4},{4,5},{7,6},{9,11},{10,8},{8,9... | collective-permute-start | bytes 589832 | tf_op jit(solution)/shard_map/ppermute | solution.py:44
  46.1 7.9 %collective-permute-done.9.refs_1_ = bf16[3,16,16,128]{3,2,1,0:T(8,128)(2,1)S(1)} collective-permute-done((bf16[3,16,16,128]{3,2,1,0:T(8,128)(2,1)S(1)}, bf16[3,16,16,128]{3,2,1,0:T(8,128)(2,1)S(1)}, u32[]{:S(2)}, u32[]{:S(2)}) %collective-permute-start.9) | collective-permute-done | bytes 196640 | tf_op jit(solution)/shard_map/ppermute | solution.py:44
  55.0 2.4 %shard_map.58 = (bf16[256,1024]{1,0:T(8,128)(2,1)S(1)}, bf16[3,1024,256]{2,1,0:T(8,128)(2,1)S(1)}) custom-call(bf16[512,3072]{1,0:T(8,128)(2,1)S(1)} %get-tuple-element.27.refs_4_.wd_ref, bf16[512,128]{1,0:T(8,128)(2,1)S(1)} %get-tuple-element.36.left_ref, f32[512,128]{1,0:T(8,128)S(1)} %get-tuple-element.37.pull_ref, f32[512,3]{1,0:T(8,128)S(1)} %bitcast.11, ...), custom_call_target="tpu_custom_call" | custom-call | flops 805306368 | bytes 3145728 | tf_op jit(solution)/shard_map/pallas_call | solution.py:420
  57.5 2.3 %shard_map.59.keep = f32[256,1024]{1,0:T(8,128)S(1)} custom-call(bf16[512,3072]{1,0:T(8,128)(2,1)S(1)} %get-tuple-element.27.refs_4_.wd_ref, bf16[512,128]{1,0:T(8,128)(2,1)S(1)} %get-tuple-element.36.left_ref, f32[512,128]{1,0:T(8,128)S(1)} %get-tuple-element.37.pull_ref, f32[512,3]{1,0:T(8,128)S(1)} %bitcast.12, ...), custom_call_target="tpu_custom_call" | custom-call | flops 805306368 | bytes 3145728 | tf_op jit(solution)/shard_map/pallas_call | solution.py:427
  59.9 1.6 %collective-permute-start.13 = (bf16[64,1024]{1,0:T(8,128)(2,1)S(1)}, bf16[64,1024]{1,0:T(8,128)(2,1)S(1)}, u32[]{:S(2)}, u32[]{:S(2)}) collective-permute-start(bf16[64,1024]{1,0:T(8,128)(2,1)S(1)} %get-tuple-element.44), channel_id=1, source_target_pairs={{0,8},{4,12},{8,0},{12,4},{16,24},{20,28},{24,16},{28,20},{1,9},{5... | collective-permute-start | bytes 393224 | tf_op jit(solution)/shard_map/ppermute | solution.py:44
  61.5 1.5 %collective-permute-start.14 = (bf16[64,1024]{1,0:T(8,128)(2,1)S(1)}, bf16[64,1024]{1,0:T(8,128)(2,1)S(1)}, u32[]{:S(2)}, u32[]{:S(2)}) collective-permute-start(bf16[64,1024]{1,0:T(8,128)(2,1)S(1)} %get-tuple-element.45), channel_id=1, source_target_pairs={{0,16},{4,20},{8,24},{12,28},{16,0},{20,4},{24,8},{28,12},{1,17},{... | collective-permute-start | bytes 393224 | tf_op jit(solution)/shard_map/ppermute | solution.py:44
  63.5 2.8 %collective-permute-done.13.refs_0_ = bf16[64,1024]{1,0:T(8,128)(2,1)S(1)} collective-permute-done((bf16[64,1024]{1,0:T(8,128)(2,1)S(1)}, bf16[64,1024]{1,0:T(8,128)(2,1)S(1)}, u32[]{:S(2)}, u32[]{:S(2)}) %collective-permute-start.13) | collective-permute-done | bytes 131104 | tf_op jit(solution)/shard_map/ppermute | solution.py:44
  66.3 3.6 %collective-permute-done.14.refs_1_ = bf16[64,1024]{1,0:T(8,128)(2,1)S(1)} collective-permute-done((bf16[64,1024]{1,0:T(8,128)(2,1)S(1)}, bf16[64,1024]{1,0:T(8,128)(2,1)S(1)}, u32[]{:S(2)}, u32[]{:S(2)}) %collective-permute-start.14) | collective-permute-done | bytes 131104 | tf_op jit(solution)/shard_map/ppermute | solution.py:44
  70.1 1.5 %collective-permute-start.18 = (bf16[64,1024]{1,0:T(8,128)(2,1)S(1)}, bf16[64,1024]{1,0:T(8,128)(2,1)S(1)}, u32[]{:S(2)}, u32[]{:S(2)}) collective-permute-start(bf16[64,1024]{1,0:T(8,128)(2,1)S(1)} %shard_map.61.own), channel_id=1, source_target_pairs={{0,24},{4,28},{8,16},{12,20},{16,8},{20,12},{24,0},{28,4},{1,25},{... | collective-permute-start | bytes 393224 | tf_op jit(solution)/shard_map/ppermute | solution.py:44
  73.6 3.7 %collective-permute-done.18.refs_2_ = bf16[64,1024]{1,0:T(8,128)(2,1)S(1)} collective-permute-done((bf16[64,1024]{1,0:T(8,128)(2,1)S(1)}, bf16[64,1024]{1,0:T(8,128)(2,1)S(1)}, u32[]{:S(2)}, u32[]{:S(2)}) %collective-permute-start.18) | collective-permute-done | bytes 131104 | tf_op jit(solution)/shard_map/ppermute | solution.py:44
  78.8 1.9 %collective-permute-done.19.other = bf16[256,1024]{1,0:T(8,128)(2,1)S(1)} collective-permute-done((bf16[256,1024]{1,0:T(8,128)(2,1)S(1)}, bf16[256,1024]{1,0:T(8,128)(2,1)S(1)}, u32[]{:S(2)}, u32[]{:S(2)}) %collective-permute-start.19) | collective-permute-done | bytes 524320 | tf_op jit(solution)/shard_map/ppermute | solution.py:44
  80.7 1.8 %collective-permute-start.22 = (f32[8,128]{1,0:T(8,128)S(1)}, f32[8,128]{1,0:T(8,128)S(1)}, u32[]{:S(2)}, u32[]{:S(2)}) collective-permute-start(f32[8,128]{1,0:T(8,128)S(1)} %shard_map.63.refs_0_), channel_id=1, source_target_pairs={{0,3},{1,0},{2,1},{3,2},{4,7},{5,4},{6,5},{7,6},{8,11},{9,8},{10,9... | collective-permute-start | bytes 12296 | tf_op jit(solution)/shard_map/ppermute | solution.py:44
  84.4 2.6 %collective-permute-done.21.refs_2_ = f32[8,128]{1,0:T(8,128)S(1)} collective-permute-done((f32[8,128]{1,0:T(8,128)S(1)}, f32[8,128]{1,0:T(8,128)S(1)}, u32[]{:S(2)}, u32[]{:S(2)}) %collective-permute-start.21) | collective-permute-done | bytes 4128 | tf_op jit(solution)/shard_map/ppermute | solution.py:44
  (45 shorter events, 19.0 us)
Async XLA Ops:
  0.6 10.7 %collective-permute-start = (bf16[3,16,16,128]{3,2,1,0:T(8,128)(2,1)}, bf16[3,16,16,128]{3,2,1,0:T(8,128)(2,1)S(1)}, u32[]{:S(2)}, u32[]{:S(2)}) collective-permute-start(bf16[3,16,16,128]{3,2,1,0:T(8,128)(2,1)} %bitcast.5), channel_id=1, source_target_pairs={{0,2},{3,1},{1,0},{2,3},{4,6},{7,5},{5,4},{6,7},{8,10},{11,9},{9,8... | collective-permute-start | bytes 589832 | tf_op jit(solution)/shard_map/ppermute | solution.py:44
  7.1 14.3 %copy-start.1 = (bf16[1,3,16,16,128]{4,3,2,1,0:T(8,128)(2,1)S(1)}, bf16[1,3,16,16,128]{4,3,2,1,0:T(8,128)(2,1)}, u32[]{:S(2)}) copy-start(bf16[1,3,16,16,128]{4,3,2,1,0:T(8,128)(2,1)} %param.3) | copy-start | bytes 589828
  7.1 8.8 %collective-permute-start.2 = (bf16[3,16,16,128]{3,2,1,0:T(8,128)(2,1)S(1)}, bf16[3,16,16,128]{3,2,1,0:T(8,128)(2,1)S(1)}, u32[]{:S(2)}, u32[]{:S(2)}) collective-permute-start(bf16[3,16,16,128]{3,2,1,0:T(8,128)(2,1)S(1)} %get-tuple-element.28), channel_id=1, source_target_pairs={{1,2},{2,1},{0,0},{3,3},{5,6},{6,5},{4,4},{7,7},{9,10},{10,9},{8,8... | collective-permute-start | bytes 589832 | tf_op jit(solution)/shard_map/ppermute | solution.py:44
  7.9 11.7 %collective-permute-start.1 = (bf16[3,16,16,128]{3,2,1,0:T(8,128)(2,1)S(1)}, bf16[3,16,16,128]{3,2,1,0:T(8,128)(2,1)S(1)}, u32[]{:S(2)}, u32[]{:S(2)}) collective-permute-start(bf16[3,16,16,128]{3,2,1,0:T(8,128)(2,1)S(1)} %get-tuple-element.28), channel_id=1, source_target_pairs={{1,3},{2,0},{0,1},{3,2},{5,7},{6,4},{4,5},{7,6},{9,11},{10,8},{8,9... | collective-permute-start | bytes 589832 | tf_op jit(solution)/shard_map/ppermute | solution.py:44
  11.3 10.0 %collective-permute-start.3 = (bf16[3,16,16,128]{3,2,1,0:T(8,128)(2,1)S(1)}, bf16[3,16,16,128]{3,2,1,0:T(8,128)(2,1)S(1)}, u32[]{:S(2)}, u32[]{:S(2)}) collective-permute-start(bf16[3,16,16,128]{3,2,1,0:T(8,128)(2,1)S(1)} %collective-permute-done.refs_0_), channel_id=1, source_target_pairs={{2,3},{1,0},{0,1},{3,2},{6,7},{5,4},{4,5},{7,6},{10,11},{9,8},{8,9... | collective-permute-start | bytes 589832 | tf_op jit(solution)/shard_map/ppermute | solution.py:44
  23.0 7.1 %collective-permute-start.6 = (bf16[3,16,16,128]{3,2,1,0:T(8,128)(2,1)S(1)}, bf16[3,16,16,128]{3,2,1,0:T(8,128)(2,1)S(1)}, u32[]{:S(2)}, u32[]{:S(2)}) collective-permute-start(bf16[3,16,16,128]{3,2,1,0:T(8,128)(2,1)S(1)} %get-tuple-element.33), channel_id=1, source_target_pairs={{0,1},{3,2},{4,5},{7,6},{8,9},{11,10},{12,13},{15,14},{16,17},{19,... | collective-permute-start | bytes 589832 | tf_op jit(solution)/shard_map/ppermute | solution.py:44
  25.2 9.1 %collective-permute-start.4 = (bf16[3,16,16,128]{3,2,1,0:T(8,128)(2,1)S(1)}, bf16[3,16,16,128]{3,2,1,0:T(8,128)(2,1)S(1)}, u32[]{:S(2)}, u32[]{:S(2)}) collective-permute-start(bf16[3,16,16,128]{3,2,1,0:T(8,128)(2,1)S(1)} %get-tuple-element.33), channel_id=1, source_target_pairs={{1,2},{2,1},{5,6},{6,5},{9,10},{10,9},{13,14},{14,13},{17,18},{18,... | collective-permute-start | bytes 589832 | tf_op jit(solution)/shard_map/ppermute | solution.py:44
  26.3 8.1 %collective-permute-start.5 = (bf16[3,16,16,128]{3,2,1,0:T(8,128)(2,1)S(1)}, bf16[3,16,16,128]{3,2,1,0:T(8,128)(2,1)S(1)}, u32[]{:S(2)}, u32[]{:S(2)}) collective-permute-start(bf16[3,16,16,128]{3,2,1,0:T(8,128)(2,1)S(1)} %shard_map.54), channel_id=1, source_target_pairs={{3,1},{0,2},{1,0},{2,3},{7,5},{4,6},{5,4},{6,7},{11,9},{8,10},{9,8... | collective-permute-start | bytes 589832 | tf_op jit(solution)/shard_map/ppermute | solution.py:44
  30.2 9.4 %collective-permute-start.7 = (bf16[3,16,16,128]{3,2,1,0:T(8,128)(2,1)S(1)}, bf16[3,16,16,128]{3,2,1,0:T(8,128)(2,1)S(1)}, u32[]{:S(2)}, u32[]{:S(2)}) collective-permute-start(bf16[3,16,16,128]{3,2,1,0:T(8,128)(2,1)S(1)} %shard_map.55), channel_id=1, source_target_pairs={{2,0},{1,3},{0,1},{3,2},{6,4},{5,7},{4,5},{7,6},{10,8},{9,11},{8,9... | collective-permute-start | bytes 589832 | tf_op jit(solution)/shard_map/ppermute | solution.py:44
  39.7 5.8 %collective-permute-start.8 = (bf16[3,16,16,128]{3,2,1,0:T(8,128)(2,1)S(1)}, bf16[3,16,16,128]{3,2,1,0:T(8,128)(2,1)S(1)}, u32[]{:S(2)}, u32[]{:S(2)}) collective-permute-start(bf16[3,16,16,128]{3,2,1,0:T(8,128)(2,1)S(1)} %get-tuple-element.35.e_ref), channel_id=1, source_target_pairs={{0,2},{3,1},{1,0},{2,3},{4,6},{7,5},{5,4},{6,7},{8,10},{11,9},{9,8... | collective-permute-start | bytes 589832 | tf_op jit(solution)/shard_map/ppermute | solution.py:44
  40.0 6.1 %collective-permute-start.10 = (bf16[3,16,16,128]{3,2,1,0:T(8,128)(2,1)S(1)}, bf16[3,16,16,128]{3,2,1,0:T(8,128)(2,1)S(1)}, u32[]{:S(2)}, u32[]{:S(2)}) collective-permute-start(bf16[3,16,16,128]{3,2,1,0:T(8,128)(2,1)S(1)} %get-tuple-element.40), channel_id=1, source_target_pairs={{1,2},{2,1},{0,0},{3,3},{5,6},{6,5},{4,4},{7,7},{9,10},{10,9},{8,8... | collective-permute-start | bytes 589832 | tf_op jit(solution)/shard_map/ppermute | solution.py:44
  40.7 13.3 %collective-permute-start.9 = (bf16[3,16,16,128]{3,2,1,0:T(8,128)(2,1)S(1)}, bf16[3,16,16,128]{3,2,1,0:T(8,128)(2,1)S(1)}, u32[]{:S(2)}, u32[]{:S(2)}) collective-permute-start(bf16[3,16,16,128]{3,2,1,0:T(8,128)(2,1)S(1)} %get-tuple-element.40), channel_id=1, source_target_pairs={{1,3},{2,0},{0,1},{3,2},{5,7},{6,4},{4,5},{7,6},{9,11},{10,8},{8,9... | collective-permute-start | bytes 589832 | tf_op jit(solution)/shard_map/ppermute | solution.py:44
  45.5 9.5 %collective-permute-start.11 = (bf16[3,16,16,128]{3,2,1,0:T(8,128)(2,1)S(1)}, bf16[3,16,16,128]{3,2,1,0:T(8,128)(2,1)S(1)}, u32[]{:S(2)}, u32[]{:S(2)}) collective-permute-start(bf16[3,16,16,128]{3,2,1,0:T(8,128)(2,1)S(1)} %collective-permute-done.8.refs_0_), channel_id=1, source_target_pairs={{2,3},{1,0},{0,1},{3,2},{6,7},{5,4},{4,5},{7,6},{10,11},{9,8},{8,9... | collective-permute-start | bytes 589832 | tf_op jit(solution)/shard_map/ppermute | solution.py:44
  57.4 2.4 %collective-permute-start.12 = (bf16[256,1024]{1,0:T(8,128)(2,1)S(1)}, bf16[256,1024]{1,0:T(8,128)(2,1)S(1)}, u32[]{:S(2)}, u32[]{:S(2)}) collective-permute-start(bf16[256,1024]{1,0:T(8,128)(2,1)S(1)} %get-tuple-element.42), channel_id=1, source_target_pairs={{0,4},{4,0},{8,12},{12,8},{16,20},{20,16},{24,28},{28,24},{1,5},{5... | collective-permute-start | bytes 1572872 | tf_op jit(solution)/shard_map/ppermute | solution.py:44
  59.9 6.4 %collective-permute-start.13 = (bf16[64,1024]{1,0:T(8,128)(2,1)S(1)}, bf16[64,1024]{1,0:T(8,128)(2,1)S(1)}, u32[]{:S(2)}, u32[]{:S(2)}) collective-permute-start(bf16[64,1024]{1,0:T(8,128)(2,1)S(1)} %get-tuple-element.44), channel_id=1, source_target_pairs={{0,8},{4,12},{8,0},{12,4},{16,24},{20,28},{24,16},{28,20},{1,9},{5... | collective-permute-start | bytes 393224 | tf_op jit(solution)/shard_map/ppermute | solution.py:44
  61.5 8.4 %collective-permute-start.14 = (bf16[64,1024]{1,0:T(8,128)(2,1)S(1)}, bf16[64,1024]{1,0:T(8,128)(2,1)S(1)}, u32[]{:S(2)}, u32[]{:S(2)}) collective-permute-start(bf16[64,1024]{1,0:T(8,128)(2,1)S(1)} %get-tuple-element.45), channel_id=1, source_target_pairs={{0,16},{4,20},{8,24},{12,28},{16,0},{20,4},{24,8},{28,12},{1,17},{... | collective-permute-start | bytes 393224 | tf_op jit(solution)/shard_map/ppermute | solution.py:44
  63.0 6.9 %collective-permute-start.15 = (bf16[64,1024]{1,0:T(8,128)(2,1)S(1)}, bf16[64,1024]{1,0:T(8,128)(2,1)S(1)}, u32[]{:S(2)}, u32[]{:S(2)}) collective-permute-start(bf16[64,1024]{1,0:T(8,128)(2,1)S(1)} %get-tuple-element.46), channel_id=1, source_target_pairs={{0,24},{4,28},{8,16},{12,20},{16,8},{20,12},{24,0},{28,4},{1,25},{... | collective-permute-start | bytes 393224 | tf_op jit(solution)/shard_map/ppermute | solution.py:44
  70.1 7.2 %collective-permute-start.18 = (bf16[64,1024]{1,0:T(8,128)(2,1)S(1)}, bf16[64,1024]{1,0:T(8,128)(2,1)S(1)}, u32[]{:S(2)}, u32[]{:S(2)}) collective-permute-start(bf16[64,1024]{1,0:T(8,128)(2,1)S(1)} %shard_map.61.own), channel_id=1, source_target_pairs={{0,24},{4,28},{8,16},{12,20},{16,8},{20,12},{24,0},{28,4},{1,25},{... | collective-permute-start | bytes 393224 | tf_op jit(solution)/shard_map/ppermute | solution.py:44
  71.6 6.9 %collective-permute-start.17 = (bf16[64,1024]{1,0:T(8,128)(2,1)S(1)}, bf16[64,1024]{1,0:T(8,128)(2,1)S(1)}, u32[]{:S(2)}, u32[]{:S(2)}) collective-permute-start(bf16[64,1024]{1,0:T(8,128)(2,1)S(1)} %shard_map.61.own), channel_id=1, source_target_pairs={{0,16},{4,20},{8,24},{12,28},{16,0},{20,4},{24,8},{28,12},{1,17},{... | collective-permute-start | bytes 393224 | tf_op jit(solution)/shard_map/ppermute | solution.py:44
  72.8 5.9 %collective-permute-start.16 = (bf16[64,1024]{1,0:T(8,128)(2,1)S(1)}, bf16[64,1024]{1,0:T(8,128)(2,1)S(1)}, u32[]{:S(2)}, u32[]{:S(2)}) collective-permute-start(bf16[64,1024]{1,0:T(8,128)(2,1)S(1)} %shard_map.61.own), channel_id=1, source_target_pairs={{0,8},{4,12},{8,0},{12,4},{16,24},{20,28},{24,16},{28,20},{1,9},{5... | collective-permute-start | bytes 393224 | tf_op jit(solution)/shard_map/ppermute | solution.py:44
  78.7 2.0 %collective-permute-start.19 = (bf16[256,1024]{1,0:T(8,128)(2,1)S(1)}, bf16[256,1024]{1,0:T(8,128)(2,1)S(1)}, u32[]{:S(2)}, u32[]{:S(2)}) collective-permute-start(bf16[256,1024]{1,0:T(8,128)(2,1)S(1)} %shard_map.62.mine), channel_id=1, source_target_pairs={{0,4},{4,0},{8,12},{12,8},{16,20},{20,16},{24,28},{28,24},{1,5},{5... | collective-permute-start | bytes 1572872 | tf_op jit(solution)/shard_map/ppermute | solution.py:44
  80.7 3.7 %collective-permute-start.22 = (f32[8,128]{1,0:T(8,128)S(1)}, f32[8,128]{1,0:T(8,128)S(1)}, u32[]{:S(2)}, u32[]{:S(2)}) collective-permute-start(f32[8,128]{1,0:T(8,128)S(1)} %shard_map.63.refs_0_), channel_id=1, source_target_pairs={{0,3},{1,0},{2,1},{3,2},{4,7},{5,4},{6,5},{7,6},{8,11},{9,8},{10,9... | collective-permute-start | bytes 12296 | tf_op jit(solution)/shard_map/ppermute | solution.py:44
  82.5 4.5 %collective-permute-start.21 = (f32[8,128]{1,0:T(8,128)S(1)}, f32[8,128]{1,0:T(8,128)S(1)}, u32[]{:S(2)}, u32[]{:S(2)}) collective-permute-start(f32[8,128]{1,0:T(8,128)S(1)} %shard_map.63.refs_0_), channel_id=1, source_target_pairs={{0,2},{1,3},{2,0},{3,1},{4,6},{5,7},{6,4},{7,5},{8,10},{9,11},{10,... | collective-permute-start | bytes 12296 | tf_op jit(solution)/shard_map/ppermute | solution.py:44
  82.5 5.4 %collective-permute-start.20 = (f32[8,128]{1,0:T(8,128)S(1)}, f32[8,128]{1,0:T(8,128)S(1)}, u32[]{:S(2)}, u32[]{:S(2)}) collective-permute-start(f32[8,128]{1,0:T(8,128)S(1)} %shard_map.63.refs_0_), channel_id=1, source_target_pairs={{0,1},{1,2},{2,3},{3,0},{4,5},{5,6},{6,7},{7,4},{8,9},{9,10},{10,1... | collective-permute-start | bytes 12296 | tf_op jit(solution)/shard_map/ppermute | solution.py:44
  (2 other events, 2.2 us)

commit v4 on v3

--- a/solution.py
+++ b/solution.py
@@ -28,11 +28,11 @@
 PAD_STRIP = -(-FIELD * SPAN // LANES) * LANES
 GRAB = 512
 STEP_IN = 256
-LAST = INPUTS % LANES
 
 sparsity_weight = 1.0
 smooth_eps = 0.01
 guard_eps = 1e-06
+
 
 BF = jnp.bfloat16
 F32 = jnp.float32
@@ -50,6 +50,13 @@
 
 def flips(count, flip):
     return [(s, s ^ flip) for s in range(count)]
+
+
+def in_turn(values, axis, routes):
+    out = []
+    for value, pairs in zip(values, routes):
+        out.append(send(value, axis, pairs))
+    return out
 
 
 def flip_all(pairs):
@@ -287,29 +294,26 @@
         ref[...] = scr[pl.ds(at, rows), :].astype(BF)
 
 
-def pieces(value):
-    high = value.astype(BF)
-    rest = value - high.astype(F32)
-    mid = rest.astype(BF)
-    low = (rest - mid.astype(F32)).astype(BF)
-    return high.astype(F32), mid.astype(F32), low.astype(F32)
-
-
 def total_of(value):
     return jnp.sum(jnp.sum(value, 0, keepdims=True), 1, keepdims=True)
 
 
 def shard_body(own, *refs):
-    got, loss, shard_ref = refs[:-2], refs[-2], refs[-1]
+    got, loss, shard_ref, tally_ref = refs[:-3], refs[-3], refs[-2], refs[-1]
     total = own[...]
     for ref in got:
         total = total + ref[...].astype(F32)
-    lane = lax.broadcasted_iota(jnp.int32, (1, LANES), 1)
-    tail = total[:, PAD_IN - LANES :]
-    for at, value in enumerate(pieces(total_of(loss[...])) + pieces(total_of(total * total))):
-        tail = jnp.where(lane == LAST + at, value, tail)
-    shard_ref[:, : PAD_IN - LANES] = total[:, : PAD_IN - LANES].astype(BF)
-    shard_ref[:, PAD_IN - LANES :] = tail.astype(BF)
+    shard_ref[...] = total.astype(BF)
+    lane = lax.broadcasted_iota(jnp.int32, (8, LANES), 1)
+    squares = total_of(total * total)
+    tally_ref[...] = jnp.where(lane == 0, total_of(loss[...]), jnp.where(lane == 1, squares, 0.0))
+
+
+def sum_body(*refs):
+    total = refs[0][...]
+    for ref in refs[1:-1]:
+        total = total + ref[...]
+    refs[-1][...] = total
 
 
 def gather_body(own, *refs):
@@ -322,14 +326,6 @@
         half_ref[pl.ds(at, rows), :] = ref[...]
 
 
-def tally_body(rows, mine, other, tally_ref):
-    total = jnp.zeros((8, LANES), F32)
-    for ref in (mine, other):
-        for at in range(0, HALF, rows):
-            total = total + ref[at : at + TILE_PX, PAD_IN - LANES :].astype(F32)[:8]
-    tally_ref[...] = total
-
-
 def finish_body(entries, frames_total, mine, other, *refs):
     tallies, up_ref, loss_ref = refs[:-2], refs[-2], refs[-1]
     tally = tallies[0][...]
@@ -337,13 +333,13 @@
         tally = tally + ref[...]
     lane = lax.broadcasted_iota(jnp.int32, (1, LANES), 1)
     row = tally[:1]
-    square = total_of(jnp.where((lane >= LAST + 3) & (lane < LAST + 6), row, 0.0))
+    square = total_of(jnp.where(lane == 1, row, 0.0))
     factor = -lax.rsqrt(square / entries + guard_eps)
     core = lax.axis_index("dp") % 2
     for half, ref in ((core, mine), (1 - core, other)):
         at = pl.multiple_of(half * HALF, HALF)
         up_ref[pl.ds(at, HALF), :] = (ref[:, :INPUTS].astype(F32) * factor).astype(BF)
-    loss_ref[0, 0] = jnp.sum(jnp.where((lane >= LAST) & (lane < LAST + 3), row, 0.0)) / frames_total
+    loss_ref[0, 0] = jnp.sum(jnp.where(lane == 0, row, 0.0)) / frames_total
 
 
 def local(frames, weights, connect):
@@ -437,18 +433,25 @@
         n_in=2, flops=mac // 32,
     )(keep, got)
     arrived = [send(v, "dp", flips(n_dp, 2 * (x + 1))) for x, v in enumerate(split[1:])]
-    (mine,) = kernel_call(shard_body, (shard,), n_in=chips + 1, flops=mac // 64)(
+    line = sds((8, LANES), F32)
+    mine, tally = kernel_call(shard_body, (shard, line), n_in=chips + 1, flops=mac // 64)(
         split[0], *arrived, loss_part
     )
-    others = [send(mine, "dp", flips(n_dp, 2 * x)) for x in range(1, chips)]
-    (mine_half,) = kernel_call(gather_body, (sds(half, BF),), n_in=chips, flops=mac // 64)(
-        mine, *others
-    )
+
+    def add_up(*values):
+        return kernel_call(sum_body, (line,), n_in=len(values), flops=mac // 64)(*values)[0]
+
+    across = [flips(n_dp, 2 * x) for x in range(1, chips)]
+    told = in_turn([tally] * (chips - 1), "dp", across)
+    others = in_turn([mine] * (chips - 1), "dp", across)
+    tally = add_up(tally, *told)
+    tally = add_up(tally, send(tally, "dp", flips(n_dp, 1)))
+    tallies = in_turn([tally] * (n_tile - 1), "tile", [ring(n_tile, s) for s in range(1, n_tile)])
+    tally = add_up(tally)
+    (mine_half,) = kernel_call(
+        gather_body, (sds(half, BF),), n_in=chips, flops=mac // 64
+    )(mine, *others)
     other_half = send(mine_half, "dp", flips(n_dp, 1))
-    (tally,) = kernel_call(
-        functools.partial(tally_body, rows), (sds((8, LANES), F32),), n_in=2, flops=mac // 64
-    )(mine_half, other_half)
-    tallies = [send(tally, "tile", ring(n_tile, s)) for s in range(1, n_tile)]
 
     entries = n_tile * POS * MAPS * INPUTS
     update, loss = kernel_call(

time: 89.6 us -> 95.6 us (1.067)
  starting transfers between devices: 31.1 us -> 34.5 us
  waiting for transfers between devices: 41.2 us -> 43.6 us
    ppermute x23 -> x27, starting transfers between devices: 31.1 us -> 34.5 us  [send(): return lax.ppermute(value, axis, pairs)]
    ppermute x23 -> x27, waiting for transfers between devices: 41.2 us -> 43.6 us  [send(): return lax.ppermute(value, axis, pairs)]
  transfers between devices with their start and end apart: 23 -> 27, of which waited for: 17 -> 20; matrix products, arithmetic and copies ran while one was open for 1% -> 1% of each run, Pallas kernels for 8% -> 7%
where the time goes in v4:
time: 95.6 us; the launch traced here: 95.3 us
  waiting for transfers between devices  43.6 us (46%)
  starting transfers between devices  34.5 us (36%)
  Pallas kernels  13.2 us (14%)
  local copies, waits for them, and re-layouts  2.37 us (2%)
  between operations  0.98 us (1%)
    ppermute x27, waiting for transfers between devices, send(): return lax.ppermute(value, axis, pairs)  43.6 us
    ppermute x27, starting transfers between devices, send(): return lax.ppermute(value, axis, pairs)  34.5 us
    pallas_call x1, Pallas kernels, local(): kernel_call(expand_body, (sds((UNITS, 3 * PLANE), BF), sds((4, 3 * QUAD,...  3.48 us
    pallas_call x1, Pallas kernels, local(): kernel_call(away_body, (sds(half, BF), sds((3, PLANE, 2 * batch), BF)), [...  2.55 us
    pallas_call x1, Pallas kernels, local(): kernel_call(home_body, (sds(half, F32),), work, n_in=6, flops=2 * mac)  2.27 us
    unnamed x6, local copies, waits for them, and re-layouts  2.19 us
  transfers between devices with their start and end apart: 27, of which 20 were waited for; matrix products, arithmetic and copies ran while one was open for 1% of the time, Pallas kernels for 7%

profile of v4, /device:TPU:0, one launch (start us, length us, event | category | flops | bytes accessed | tf_op | source)
XLA Modules:
  0.0 95.3 jit_solution(2162332067297499572)
XLA Ops:
  0.6 4.1 %collective-permute-start = (bf16[3,16,16,128]{3,2,1,0:T(8,128)(2,1)}, bf16[3,16,16,128]{3,2,1,0:T(8,128)(2,1)S(1)}, u32[]{:S(2)}, u32[]{:S(2)}) collective-permute-start(bf16[3,16,16,128]{3,2,1,0:T(8,128)(2,1)} %bitcast.5), channel_id=1, source_target_pairs={{0,2},{3,1},{1,0},{2,3},{4,6},{7,5},{5,4},{6,7},{8,10},{11,9},{9,8... | collective-permute-start | bytes 589832 | tf_op jit(solution)/shard_map/ppermute | solution.py:44
  7.9 3.4 %collective-permute-start.1 = (bf16[3,16,16,128]{3,2,1,0:T(8,128)(2,1)S(1)}, bf16[3,16,16,128]{3,2,1,0:T(8,128)(2,1)S(1)}, u32[]{:S(2)}, u32[]{:S(2)}) collective-permute-start(bf16[3,16,16,128]{3,2,1,0:T(8,128)(2,1)S(1)} %get-tuple-element.30), channel_id=1, source_target_pairs={{1,3},{2,0},{0,1},{3,2},{5,7},{6,4},{4,5},{7,6},{9,11},{10,8},{8,9... | collective-permute-start | bytes 589832 | tf_op jit(solution)/shard_map/ppermute | solution.py:44
  12.4 3.5 %shard_map.51 = (bf16[512,3072]{1,0:T(8,128)(2,1)S(1)}, bf16[4,768,512]{2,1,0:T(8,128)(2,1)S(1)}, bf16[3,640,512]{2,1,0:T(8,128)(2,1)S(1)}) custom-call(bf16[512,1024]{1,0:T(8,128)(2,1)S(1)} %get-tuple-element.28.wp_ref, f32[512,3]{1,0:T(8,128)S(1)} %bitcast.10), custom_call_target="tpu_custom_call" | custom-call | flops 1610612736 | bytes 6291456 | tf_op jit(solution)/shard_map/pallas_call | solution.py:372
  15.9 3.7 %collective-permute-done.1.refs_1_ = bf16[3,16,16,128]{3,2,1,0:T(8,128)(2,1)S(1)} collective-permute-done((bf16[3,16,16,128]{3,2,1,0:T(8,128)(2,1)S(1)}, bf16[3,16,16,128]{3,2,1,0:T(8,128)(2,1)S(1)}, u32[]{:S(2)}, u32[]{:S(2)}) %collective-permute-start.1) | collective-permute-done | bytes 196640 | tf_op jit(solution)/shard_map/ppermute | solution.py:44
  19.6 1.7 %collective-permute-done.3.refs_3_ = bf16[3,16,16,128]{3,2,1,0:T(8,128)(2,1)S(1)} collective-permute-done((bf16[3,16,16,128]{3,2,1,0:T(8,128)(2,1)S(1)}, bf16[3,16,16,128]{3,2,1,0:T(8,128)(2,1)S(1)}, u32[]{:S(2)}, u32[]{:S(2)}) %collective-permute-start.3) | collective-permute-done | bytes 196640 | tf_op jit(solution)/shard_map/ppermute | solution.py:44
  21.3 1.7 %shard_map.52 = (f32[512,128]{1,0:T(8,128)S(1)}, bf16[3,16,16,128]{3,2,1,0:T(8,128)(2,1)S(1)}) custom-call(bf16[3,16,16,128]{3,2,1,0:T(8,128)(2,1)S(1)} %bitcast.7, bf16[3,16,16,128]{3,2,1,0:T(8,128)(2,1)S(1)} %collective-permute-done.refs_0_, bf16[3,16,16,128]{3,2,1,0:T(8,128)(2,1)S(1)} %collective-permute-done.1.refs_1_, ...), custom_call_target="tpu_custom_call" | custom-call | flops 402653184 | bytes 1572864 | tf_op jit(solution)/shard_map/pallas_call | solution.py:379
  23.0 2.2 %collective-permute-start.6 = (bf16[3,16,16,128]{3,2,1,0:T(8,128)(2,1)S(1)}, bf16[3,16,16,128]{3,2,1,0:T(8,128)(2,1)S(1)}, u32[]{:S(2)}, u32[]{:S(2)}) collective-permute-start(bf16[3,16,16,128]{3,2,1,0:T(8,128)(2,1)S(1)} %get-tuple-element.35), channel_id=1, source_target_pairs={{0,1},{3,2},{4,5},{7,6},{8,9},{11,10},{12,13},{15,14},{16,17},{19,... | collective-permute-start | bytes 589832 | tf_op jit(solution)/shard_map/ppermute | solution.py:44
  26.3 2.1 %collective-permute-start.5 = (bf16[3,16,16,128]{3,2,1,0:T(8,128)(2,1)S(1)}, bf16[3,16,16,128]{3,2,1,0:T(8,128)(2,1)S(1)}, u32[]{:S(2)}, u32[]{:S(2)}) collective-permute-start(bf16[3,16,16,128]{3,2,1,0:T(8,128)(2,1)S(1)} %shard_map.54), channel_id=1, source_target_pairs={{3,1},{0,2},{1,0},{2,3},{7,5},{4,6},{5,4},{6,7},{11,9},{8,10},{9,8... | collective-permute-start | bytes 589832 | tf_op jit(solution)/shard_map/ppermute | solution.py:44
  30.2 2.5 %collective-permute-start.7 = (bf16[3,16,16,128]{3,2,1,0:T(8,128)(2,1)S(1)}, bf16[3,16,16,128]{3,2,1,0:T(8,128)(2,1)S(1)}, u32[]{:S(2)}, u32[]{:S(2)}) collective-permute-start(bf16[3,16,16,128]{3,2,1,0:T(8,128)(2,1)S(1)} %shard_map.55), channel_id=1, source_target_pairs={{2,0},{1,3},{0,1},{3,2},{6,4},{5,7},{4,5},{7,6},{10,8},{9,11},{8,9... | collective-permute-start | bytes 589832 | tf_op jit(solution)/shard_map/ppermute | solution.py:44
  32.7 1.6 %collective-permute-done.5.refs_1_ = bf16[3,16,16,128]{3,2,1,0:T(8,128)(2,1)S(1)} collective-permute-done((bf16[3,16,16,128]{3,2,1,0:T(8,128)(2,1)S(1)}, bf16[3,16,16,128]{3,2,1,0:T(8,128)(2,1)S(1)}, u32[]{:S(2)}, u32[]{:S(2)}) %collective-permute-start.5) | collective-permute-done | bytes 196640 | tf_op jit(solution)/shard_map/ppermute | solution.py:44
  34.3 5.2 %collective-permute-done.7.refs_2_ = bf16[3,16,16,128]{3,2,1,0:T(8,128)(2,1)S(1)} collective-permute-done((bf16[3,16,16,128]{3,2,1,0:T(8,128)(2,1)S(1)}, bf16[3,16,16,128]{3,2,1,0:T(8,128)(2,1)S(1)}, u32[]{:S(2)}, u32[]{:S(2)}) %collective-permute-start.7) | collective-permute-done | bytes 196640 | tf_op jit(solution)/shard_map/ppermute | solution.py:44
  40.7 4.0 %collective-permute-start.9 = (bf16[3,16,16,128]{3,2,1,0:T(8,128)(2,1)S(1)}, bf16[3,16,16,128]{3,2,1,0:T(8,128)(2,1)S(1)}, u32[]{:S(2)}, u32[]{:S(2)}) collective-permute-start(bf16[3,16,16,128]{3,2,1,0:T(8,128)(2,1)S(1)} %get-tuple-element.42), channel_id=1, source_target_pairs={{1,3},{2,0},{0,1},{3,2},{5,7},{6,4},{4,5},{7,6},{9,11},{10,8},{8,9... | collective-permute-start | bytes 589832 | tf_op jit(solution)/shard_map/ppermute | solution.py:44
  46.1 7.9 %collective-permute-done.9.refs_1_ = bf16[3,16,16,128]{3,2,1,0:T(8,128)(2,1)S(1)} collective-permute-done((bf16[3,16,16,128]{3,2,1,0:T(8,128)(2,1)S(1)}, bf16[3,16,16,128]{3,2,1,0:T(8,128)(2,1)S(1)}, u32[]{:S(2)}, u32[]{:S(2)}) %collective-permute-start.9) | collective-permute-done | bytes 196640 | tf_op jit(solution)/shard_map/ppermute | solution.py:44
  55.0 2.6 %shard_map.58 = (bf16[256,1024]{1,0:T(8,128)(2,1)S(1)}, bf16[3,1024,256]{2,1,0:T(8,128)(2,1)S(1)}) custom-call(bf16[512,3072]{1,0:T(8,128)(2,1)S(1)} %get-tuple-element.29.refs_4_.wd_ref, bf16[512,128]{1,0:T(8,128)(2,1)S(1)} %get-tuple-element.38.left_ref, f32[512,128]{1,0:T(8,128)S(1)} %get-tuple-element.39.pull_ref, f32[512,3]{1,0:T(8,128)S(1)} %bitcast.11, ...), custom_call_target="tpu_custom_call" | custom-call | flops 805306368 | bytes 3145728 | tf_op jit(solution)/shard_map/pallas_call | solution.py:416
  57.6 2.3 %shard_map.59.keep = f32[256,1024]{1,0:T(8,128)S(1)} custom-call(bf16[512,3072]{1,0:T(8,128)(2,1)S(1)} %get-tuple-element.29.refs_4_.wd_ref, bf16[512,128]{1,0:T(8,128)(2,1)S(1)} %get-tuple-element.38.left_ref, f32[512,128]{1,0:T(8,128)S(1)} %get-tuple-element.39.pull_ref, f32[512,3]{1,0:T(8,128)S(1)} %bitcast.12, ...), custom_call_target="tpu_custom_call" | custom-call | flops 805306368 | bytes 3145728 | tf_op jit(solution)/shard_map/pallas_call | solution.py:423
  60.1 1.5 %collective-permute-start.13 = (bf16[64,1024]{1,0:T(8,128)(2,1)S(1)}, bf16[64,1024]{1,0:T(8,128)(2,1)S(1)}, u32[]{:S(2)}, u32[]{:S(2)}) collective-permute-start(bf16[64,1024]{1,0:T(8,128)(2,1)S(1)} %get-tuple-element.46), channel_id=1, source_target_pairs={{0,8},{4,12},{8,0},{12,4},{16,24},{20,28},{24,16},{28,20},{1,9},{5... | collective-permute-start | bytes 393224 | tf_op jit(solution)/shard_map/ppermute | solution.py:44
  61.6 1.5 %collective-permute-start.14 = (bf16[64,1024]{1,0:T(8,128)(2,1)S(1)}, bf16[64,1024]{1,0:T(8,128)(2,1)S(1)}, u32[]{:S(2)}, u32[]{:S(2)}) collective-permute-start(bf16[64,1024]{1,0:T(8,128)(2,1)S(1)} %get-tuple-element.47), channel_id=1, source_target_pairs={{0,16},{4,20},{8,24},{12,28},{16,0},{20,4},{24,8},{28,12},{1,17},{... | collective-permute-start | bytes 393224 | tf_op jit(solution)/shard_map/ppermute | solution.py:44
  63.7 2.8 %collective-permute-done.13.refs_0_ = bf16[64,1024]{1,0:T(8,128)(2,1)S(1)} collective-permute-done((bf16[64,1024]{1,0:T(8,128)(2,1)S(1)}, bf16[64,1024]{1,0:T(8,128)(2,1)S(1)}, u32[]{:S(2)}, u32[]{:S(2)}) %collective-permute-start.13) | collective-permute-done | bytes 131104 | tf_op jit(solution)/shard_map/ppermute | solution.py:44
  66.5 3.6 %collective-permute-done.14.refs_1_ = bf16[64,1024]{1,0:T(8,128)(2,1)S(1)} collective-permute-done((bf16[64,1024]{1,0:T(8,128)(2,1)S(1)}, bf16[64,1024]{1,0:T(8,128)(2,1)S(1)}, u32[]{:S(2)}, u32[]{:S(2)}) %collective-permute-start.14) | collective-permute-done | bytes 131104 | tf_op jit(solution)/shard_map/ppermute | solution.py:44
  70.2 1.5 %collective-permute-start.18 = (bf16[64,1024]{1,0:T(8,128)(2,1)S(1)}, bf16[64,1024]{1,0:T(8,128)(2,1)S(1)}, u32[]{:S(2)}, u32[]{:S(2)}) collective-permute-start(bf16[64,1024]{1,0:T(8,128)(2,1)S(1)} %get-tuple-element.50.own), channel_id=1, source_target_pairs={{0,24},{4,28},{8,16},{12,20},{16,8},{20,12},{24,0},{28,4},{1,25},{... | collective-permute-start | bytes 393224 | tf_op jit(solution)/shard_map/ppermute | solution.py:44
  73.7 3.7 %collective-permute-done.18.refs_2_ = bf16[64,1024]{1,0:T(8,128)(2,1)S(1)} collective-permute-done((bf16[64,1024]{1,0:T(8,128)(2,1)S(1)}, bf16[64,1024]{1,0:T(8,128)(2,1)S(1)}, u32[]{:S(2)}, u32[]{:S(2)}) %collective-permute-start.18) | collective-permute-done | bytes 131104 | tf_op jit(solution)/shard_map/ppermute | solution.py:44
  84.0 1.5 %collective-permute-done.20.refs_1_ = f32[8,128]{1,0:T(8,128)S(1)} collective-permute-done((f32[8,128]{1,0:T(8,128)S(1)}, f32[8,128]{1,0:T(8,128)S(1)}, u32[]{:S(2)}, u32[]{:S(2)}) %collective-permute-start.20) | collective-permute-done | bytes 4128 | tf_op jit(solution)/shard_map/ppermute | solution.py:44
  86.7 1.7 %collective-permute-start.26 = (f32[8,128]{1,0:T(8,128)S(1)}, f32[8,128]{1,0:T(8,128)S(1)}, u32[]{:S(2)}, u32[]{:S(2)}) collective-permute-start(f32[8,128]{1,0:T(8,128)S(1)} %shard_map.64.refs_0_), channel_id=1, source_target_pairs={{0,3},{1,0},{2,1},{3,2},{4,7},{5,4},{6,5},{7,6},{8,11},{9,8},{10,9... | collective-permute-start | bytes 12296 | tf_op jit(solution)/shard_map/ppermute | solution.py:44
  90.3 2.6 %collective-permute-done.25.refs_2_ = f32[8,128]{1,0:T(8,128)S(1)} collective-permute-done((f32[8,128]{1,0:T(8,128)S(1)}, f32[8,128]{1,0:T(8,128)S(1)}, u32[]{:S(2)}, u32[]{:S(2)}) %collective-permute-start.25) | collective-permute-done | bytes 4128 | tf_op jit(solution)/shard_map/ppermute | solution.py:44
  (55 shorter events, 25.3 us)
Async XLA Ops:
  0.6 10.7 %collective-permute-start = (bf16[3,16,16,128]{3,2,1,0:T(8,128)(2,1)}, bf16[3,16,16,128]{3,2,1,0:T(8,128)(2,1)S(1)}, u32[]{:S(2)}, u32[]{:S(2)}) collective-permute-start(bf16[3,16,16,128]{3,2,1,0:T(8,128)(2,1)} %bitcast.5), channel_id=1, source_target_pairs={{0,2},{3,1},{1,0},{2,3},{4,6},{7,5},{5,4},{6,7},{8,10},{11,9},{9,8... | collective-permute-start | bytes 589832 | tf_op jit(solution)/shard_map/ppermute | solution.py:44
  7.1 8.8 %collective-permute-start.2 = (bf16[3,16,16,128]{3,2,1,0:T(8,128)(2,1)S(1)}, bf16[3,16,16,128]{3,2,1,0:T(8,128)(2,1)S(1)}, u32[]{:S(2)}, u32[]{:S(2)}) collective-permute-start(bf16[3,16,16,128]{3,2,1,0:T(8,128)(2,1)S(1)} %get-tuple-element.30), channel_id=1, source_target_pairs={{1,2},{2,1},{0,0},{3,3},{5,6},{6,5},{4,4},{7,7},{9,10},{10,9},{8,8... | collective-permute-start | bytes 589832 | tf_op jit(solution)/shard_map/ppermute | solution.py:44
  7.9 11.7 %collective-permute-start.1 = (bf16[3,16,16,128]{3,2,1,0:T(8,128)(2,1)S(1)}, bf16[3,16,16,128]{3,2,1,0:T(8,128)(2,1)S(1)}, u32[]{:S(2)}, u32[]{:S(2)}) collective-permute-start(bf16[3,16,16,128]{3,2,1,0:T(8,128)(2,1)S(1)} %get-tuple-element.30), channel_id=1, source_target_pairs={{1,3},{2,0},{0,1},{3,2},{5,7},{6,4},{4,5},{7,6},{9,11},{10,8},{8,9... | collective-permute-start | bytes 589832 | tf_op jit(solution)/shard_map/ppermute | solution.py:44
  11.3 10.0 %collective-permute-start.3 = (bf16[3,16,16,128]{3,2,1,0:T(8,128)(2,1)S(1)}, bf16[3,16,16,128]{3,2,1,0:T(8,128)(2,1)S(1)}, u32[]{:S(2)}, u32[]{:S(2)}) collective-permute-start(bf16[3,16,16,128]{3,2,1,0:T(8,128)(2,1)S(1)} %collective-permute-done.refs_0_), channel_id=1, source_target_pairs={{2,3},{1,0},{0,1},{3,2},{6,7},{5,4},{4,5},{7,6},{10,11},{9,8},{8,9... | collective-permute-start | bytes 589832 | tf_op jit(solution)/shard_map/ppermute | solution.py:44
  23.0 7.1 %collective-permute-start.6 = (bf16[3,16,16,128]{3,2,1,0:T(8,128)(2,1)S(1)}, bf16[3,16,16,128]{3,2,1,0:T(8,128)(2,1)S(1)}, u32[]{:S(2)}, u32[]{:S(2)}) collective-permute-start(bf16[3,16,16,128]{3,2,1,0:T(8,128)(2,1)S(1)} %get-tuple-element.35), channel_id=1, source_target_pairs={{0,1},{3,2},{4,5},{7,6},{8,9},{11,10},{12,13},{15,14},{16,17},{19,... | collective-permute-start | bytes 589832 | tf_op jit(solution)/shard_map/ppermute | solution.py:44
  25.2 9.1 %collective-permute-start.4 = (bf16[3,16,16,128]{3,2,1,0:T(8,128)(2,1)S(1)}, bf16[3,16,16,128]{3,2,1,0:T(8,128)(2,1)S(1)}, u32[]{:S(2)}, u32[]{:S(2)}) collective-permute-start(bf16[3,16,16,128]{3,2,1,0:T(8,128)(2,1)S(1)} %get-tuple-element.35), channel_id=1, source_target_pairs={{1,2},{2,1},{5,6},{6,5},{9,10},{10,9},{13,14},{14,13},{17,18},{18,... | collective-permute-start | bytes 589832 | tf_op jit(solution)/shard_map/ppermute | solution.py:44
  26.3 8.1 %collective-permute-start.5 = (bf16[3,16,16,128]{3,2,1,0:T(8,128)(2,1)S(1)}, bf16[3,16,16,128]{3,2,1,0:T(8,128)(2,1)S(1)}, u32[]{:S(2)}, u32[]{:S(2)}) collective-permute-start(bf16[3,16,16,128]{3,2,1,0:T(8,128)(2,1)S(1)} %shard_map.54), channel_id=1, source_target_pairs={{3,1},{0,2},{1,0},{2,3},{7,5},{4,6},{5,4},{6,7},{11,9},{8,10},{9,8... | collective-permute-start | bytes 589832 | tf_op jit(solution)/shard_map/ppermute | solution.py:44
  30.2 9.4 %collective-permute-start.7 = (bf16[3,16,16,128]{3,2,1,0:T(8,128)(2,1)S(1)}, bf16[3,16,16,128]{3,2,1,0:T(8,128)(2,1)S(1)}, u32[]{:S(2)}, u32[]{:S(2)}) collective-permute-start(bf16[3,16,16,128]{3,2,1,0:T(8,128)(2,1)S(1)} %shard_map.55), channel_id=1, source_target_pairs={{2,0},{1,3},{0,1},{3,2},{6,4},{5,7},{4,5},{7,6},{10,8},{9,11},{8,9... | collective-permute-start | bytes 589832 | tf_op jit(solution)/shard_map/ppermute | solution.py:44
  39.7 5.8 %collective-permute-start.8 = (bf16[3,16,16,128]{3,2,1,0:T(8,128)(2,1)S(1)}, bf16[3,16,16,128]{3,2,1,0:T(8,128)(2,1)S(1)}, u32[]{:S(2)}, u32[]{:S(2)}) collective-permute-start(bf16[3,16,16,128]{3,2,1,0:T(8,128)(2,1)S(1)} %get-tuple-element.37.e_ref), channel_id=1, source_target_pairs={{0,2},{3,1},{1,0},{2,3},{4,6},{7,5},{5,4},{6,7},{8,10},{11,9},{9,8... | collective-permute-start | bytes 589832 | tf_op jit(solution)/shard_map/ppermute | solution.py:44
  40.0 6.1 %collective-permute-start.10 = (bf16[3,16,16,128]{3,2,1,0:T(8,128)(2,1)S(1)}, bf16[3,16,16,128]{3,2,1,0:T(8,128)(2,1)S(1)}, u32[]{:S(2)}, u32[]{:S(2)}) collective-permute-start(bf16[3,16,16,128]{3,2,1,0:T(8,128)(2,1)S(1)} %get-tuple-element.42), channel_id=1, source_target_pairs={{1,2},{2,1},{0,0},{3,3},{5,6},{6,5},{4,4},{7,7},{9,10},{10,9},{8,8... | collective-permute-start | bytes 589832 | tf_op jit(solution)/shard_map/ppermute | solution.py:44
  40.7 13.3 %collective-permute-start.9 = (bf16[3,16,16,128]{3,2,1,0:T(8,128)(2,1)S(1)}, bf16[3,16,16,128]{3,2,1,0:T(8,128)(2,1)S(1)}, u32[]{:S(2)}, u32[]{:S(2)}) collective-permute-start(bf16[3,16,16,128]{3,2,1,0:T(8,128)(2,1)S(1)} %get-tuple-element.42), channel_id=1, source_target_pairs={{1,3},{2,0},{0,1},{3,2},{5,7},{6,4},{4,5},{7,6},{9,11},{10,8},{8,9... | collective-permute-start | bytes 589832 | tf_op jit(solution)/shard_map/ppermute | solution.py:44
  45.5 9.5 %collective-permute-start.11 = (bf16[3,16,16,128]{3,2,1,0:T(8,128)(2,1)S(1)}, bf16[3,16,16,128]{3,2,1,0:T(8,128)(2,1)S(1)}, u32[]{:S(2)}, u32[]{:S(2)}) collective-permute-start(bf16[3,16,16,128]{3,2,1,0:T(8,128)(2,1)S(1)} %collective-permute-done.8.refs_0_), channel_id=1, source_target_pairs={{2,3},{1,0},{0,1},{3,2},{6,7},{5,4},{4,5},{7,6},{10,11},{9,8},{8,9... | collective-permute-start | bytes 589832 | tf_op jit(solution)/shard_map/ppermute | solution.py:44
  60.1 6.4 %collective-permute-start.13 = (bf16[64,1024]{1,0:T(8,128)(2,1)S(1)}, bf16[64,1024]{1,0:T(8,128)(2,1)S(1)}, u32[]{:S(2)}, u32[]{:S(2)}) collective-permute-start(bf16[64,1024]{1,0:T(8,128)(2,1)S(1)} %get-tuple-element.46), channel_id=1, source_target_pairs={{0,8},{4,12},{8,0},{12,4},{16,24},{20,28},{24,16},{28,20},{1,9},{5... | collective-permute-start | bytes 393224 | tf_op jit(solution)/shard_map/ppermute | solution.py:44
  61.6 8.4 %collective-permute-start.14 = (bf16[64,1024]{1,0:T(8,128)(2,1)S(1)}, bf16[64,1024]{1,0:T(8,128)(2,1)S(1)}, u32[]{:S(2)}, u32[]{:S(2)}) collective-permute-start(bf16[64,1024]{1,0:T(8,128)(2,1)S(1)} %get-tuple-element.47), channel_id=1, source_target_pairs={{0,16},{4,20},{8,24},{12,28},{16,0},{20,4},{24,8},{28,12},{1,17},{... | collective-permute-start | bytes 393224 | tf_op jit(solution)/shard_map/ppermute | solution.py:44
  63.2 6.9 %collective-permute-start.15 = (bf16[64,1024]{1,0:T(8,128)(2,1)S(1)}, bf16[64,1024]{1,0:T(8,128)(2,1)S(1)}, u32[]{:S(2)}, u32[]{:S(2)}) collective-permute-start(bf16[64,1024]{1,0:T(8,128)(2,1)S(1)} %get-tuple-element.48), channel_id=1, source_target_pairs={{0,24},{4,28},{8,16},{12,20},{16,8},{20,12},{24,0},{28,4},{1,25},{... | collective-permute-start | bytes 393224 | tf_op jit(solution)/shard_map/ppermute | solution.py:44
  70.2 7.2 %collective-permute-start.18 = (bf16[64,1024]{1,0:T(8,128)(2,1)S(1)}, bf16[64,1024]{1,0:T(8,128)(2,1)S(1)}, u32[]{:S(2)}, u32[]{:S(2)}) collective-permute-start(bf16[64,1024]{1,0:T(8,128)(2,1)S(1)} %get-tuple-element.50.own), channel_id=1, source_target_pairs={{0,24},{4,28},{8,16},{12,20},{16,8},{20,12},{24,0},{28,4},{1,25},{... | collective-permute-start | bytes 393224 | tf_op jit(solution)/shard_map/ppermute | solution.py:44
  71.7 6.9 %collective-permute-start.17 = (bf16[64,1024]{1,0:T(8,128)(2,1)S(1)}, bf16[64,1024]{1,0:T(8,128)(2,1)S(1)}, u32[]{:S(2)}, u32[]{:S(2)}) collective-permute-start(bf16[64,1024]{1,0:T(8,128)(2,1)S(1)} %get-tuple-element.50.own), channel_id=1, source_target_pairs={{0,16},{4,20},{8,24},{12,28},{16,0},{20,4},{24,8},{28,12},{1,17},{... | collective-permute-start | bytes 393224 | tf_op jit(solution)/shard_map/ppermute | solution.py:44
  73.0 5.9 %collective-permute-start.16 = (bf16[64,1024]{1,0:T(8,128)(2,1)S(1)}, bf16[64,1024]{1,0:T(8,128)(2,1)S(1)}, u32[]{:S(2)}, u32[]{:S(2)}) collective-permute-start(bf16[64,1024]{1,0:T(8,128)(2,1)S(1)} %get-tuple-element.50.own), channel_id=1, source_target_pairs={{0,8},{4,12},{8,0},{12,4},{16,24},{20,28},{24,16},{28,20},{1,9},{5... | collective-permute-start | bytes 393224 | tf_op jit(solution)/shard_map/ppermute | solution.py:44
  78.9 14.9 %collective-permute-start.19 = (bf16[256,1024]{1,0:T(8,128)(2,1)S(1)}, bf16[256,1024]{1,0:T(8,128)(2,1)S(1)}, u32[]{:S(2)}, u32[]{:S(2)}) collective-permute-start(bf16[256,1024]{1,0:T(8,128)(2,1)S(1)} %shard_map.62.mine), channel_id=1, source_target_pairs={{0,4},{4,0},{8,12},{12,8},{16,20},{20,16},{24,28},{28,24},{1,5},{5... | collective-permute-start | bytes 1572872 | tf_op jit(solution)/shard_map/ppermute | solution.py:44
  79.0 4.6 %collective-permute-start.22 = (f32[8,128]{1,0:T(8,128)S(1)}, f32[8,128]{1,0:T(8,128)S(1)}, u32[]{:S(2)}, u32[]{:S(2)}) collective-permute-start(f32[8,128]{1,0:T(8,128)S(1)} %get-tuple-element.51.refs_0_), channel_id=1, source_target_pairs={{0,24},{4,28},{8,16},{12,20},{16,8},{20,12},{24,0},{28,4},{1,25},{... | collective-permute-start | bytes 12296 | tf_op jit(solution)/shard_map/ppermute | solution.py:44
  80.4 3.6 %collective-permute-start.21 = (f32[8,128]{1,0:T(8,128)S(1)}, f32[8,128]{1,0:T(8,128)S(1)}, u32[]{:S(2)}, u32[]{:S(2)}) collective-permute-start(f32[8,128]{1,0:T(8,128)S(1)} %get-tuple-element.51.refs_0_), channel_id=1, source_target_pairs={{0,16},{4,20},{8,24},{12,28},{16,0},{20,4},{24,8},{28,12},{1,17},{... | collective-permute-start | bytes 12296 | tf_op jit(solution)/shard_map/ppermute | solution.py:44
  81.9 3.6 %collective-permute-start.20 = (f32[8,128]{1,0:T(8,128)S(1)}, f32[8,128]{1,0:T(8,128)S(1)}, u32[]{:S(2)}, u32[]{:S(2)}) collective-permute-start(f32[8,128]{1,0:T(8,128)S(1)} %get-tuple-element.51.refs_0_), channel_id=1, source_target_pairs={{0,8},{4,12},{8,0},{12,4},{16,24},{20,28},{24,16},{28,20},{1,9},{5... | collective-permute-start | bytes 12296 | tf_op jit(solution)/shard_map/ppermute | solution.py:44
  88.4 4.5 %collective-permute-start.25 = (f32[8,128]{1,0:T(8,128)S(1)}, f32[8,128]{1,0:T(8,128)S(1)}, u32[]{:S(2)}, u32[]{:S(2)}) collective-permute-start(f32[8,128]{1,0:T(8,128)S(1)} %shard_map.64.refs_0_), channel_id=1, source_target_pairs={{0,2},{1,3},{2,0},{3,1},{4,6},{5,7},{6,4},{7,5},{8,10},{9,11},{10,... | collective-permute-start | bytes 12296 | tf_op jit(solution)/shard_map/ppermute | solution.py:44
  88.4 5.4 %collective-permute-start.24 = (f32[8,128]{1,0:T(8,128)S(1)}, f32[8,128]{1,0:T(8,128)S(1)}, u32[]{:S(2)}, u32[]{:S(2)}) collective-permute-start(f32[8,128]{1,0:T(8,128)S(1)} %shard_map.64.refs_0_), channel_id=1, source_target_pairs={{0,1},{1,2},{2,3},{3,0},{4,5},{5,6},{6,7},{7,4},{8,9},{9,10},{10,1... | collective-permute-start | bytes 12296 | tf_op jit(solution)/shard_map/ppermute | solution.py:44
  (6 other events, 23.6 us)

commit v5 on v4

--- a/solution.py
+++ b/solution.py
@@ -238,49 +238,57 @@
     place(xe, x_ref, slots)
 
 
-def gradient_rows(half, wd_ref, left_ref, pull_ref, con_ref, st_ref, ex, gd, gs, out):
+def gradient_rows(half, wd_ref, left_ref, pull_ref, con_ref, st_ref, ex, gd, gs, acc, out):
     at = pl.multiple_of(half * HALF, HALF)
     rows = pl.ds(at, HALF)
     batch = left_ref.shape[-1]
-    e_all = ex[:, :, :batch].reshape(3 * PLANE, batch)
+    e_all = ex[:, :, :, :batch].reshape(3 * PLANE, batch)
     enc = jnp.dot(wd_ref[rows, :], e_all, preferred_element_type=F32)
     left = left_ref[rows, :].astype(F32)
     right = 2.0 * enc + pull_ref[rows, :]
     con = con_ref[rows, :]
     shift = half * (SIDE_POS // 2 * STRIDE * SPAN)
-    out[...] = jnp.zeros((HALF, PAD_IN), F32)
     for ch in range(3):
         opened = con[:, ch : ch + 1]
         both = jnp.concatenate([(left * opened).astype(BF), (right * opened).astype(BF)], 1)
-        gd[...] = lax.dot_general(
-            both, ex[ch], (((1,), (1,)), ((), ())), preferred_element_type=F32
+        gd[ch][...] = lax.dot_general(
+            both,
+            ex[ch].reshape(PLANE, 2 * batch),
+            (((1,), (1,)), ((), ())),
+            preferred_element_type=F32,
         )
+    for ch in range(3):
         for u, lead, shifts in positions(SIDE_POS // 2):
             parts = []
             lanes = pl.ds(pl.multiple_of(lead + shift, LANES), PAD_STRIP)
             for h, s in enumerate(shifts):
-                blk = gd[u + h * MAPS : u + (h + 1) * MAPS, lanes]
+                blk = gd[ch][u + h * MAPS : u + (h + 1) * MAPS, lanes]
                 parts.append(pltpu.roll(blk, PAD_STRIP - s, 1) if s else blk)
-            gs[u : u + 2 * MAPS, :] = jnp.concatenate(parts, 0).astype(BF)
-        cols = slice(ch * STEP_IN, ch * STEP_IN + GRAB)
-        out[:, cols] = out[:, cols] + jnp.dot(gs[...], st_ref[ch], preferred_element_type=F32)
+            gs[ch][u : u + 2 * MAPS, :] = jnp.concatenate(parts, 0).astype(BF)
+        acc[ch][...] = jnp.dot(gs[ch][...], st_ref[ch], preferred_element_type=F32)
+    for at in range(0, PAD_IN, STEP_IN):
+        first = at // STEP_IN
+        parts = [acc[ch][:, at - ch * STEP_IN : at - ch * STEP_IN + STEP_IN] for ch in (first, first - 1) if 0 <= ch < 3]
+        out[:, at : at + STEP_IN] = sum(parts[1:], parts[0]).astype(out.dtype)
 
 
 def away_body(wd_ref, left_ref, pull_ref, con_ref, st_ref, xe, e_ref, *refs):
-    slots, (send_ref, ex, tmp, gd, gs, out) = refs[:-6], refs[-6:]
+    slots, (send_ref, ex), work = refs[:-11], refs[-11:-9], refs[-9:]
     batch = e_ref.shape[-1]
-    place(tmp, e_ref, slots)
+    place(ex.at[:, :, :, :batch], e_ref, slots)
     for ch in range(3):
-        ex[ch, :, :batch] = tmp[ch].reshape(PLANE, batch)
-        ex[ch, :, batch:] = xe[ch].reshape(PLANE, batch)
+        ex[ch, :, :, batch:] = xe[ch]
     core = lax.axis_index("dp") % 2
-    gradient_rows(1 - core, wd_ref, left_ref, pull_ref, con_ref, st_ref, ex, gd, gs, out)
-    send_ref[...] = out[...].astype(BF)
-
-
-def home_body(wd_ref, left_ref, pull_ref, con_ref, st_ref, ex, keep_ref, gd, gs):
+    gradient_rows(
+        1 - core, wd_ref, left_ref, pull_ref, con_ref, st_ref, ex, work[:3], work[3:6], work[6:], send_ref
+    )
+
+
+def home_body(wd_ref, left_ref, pull_ref, con_ref, st_ref, ex, keep_ref, *work):
     core = lax.axis_index("dp") % 2
-    gradient_rows(core, wd_ref, left_ref, pull_ref, con_ref, st_ref, ex, gd, gs, keep_ref)
+    gradient_rows(
+        core, wd_ref, left_ref, pull_ref, con_ref, st_ref, ex, work[:3], work[3:6], work[6:], keep_ref
+    )
 
 
 def pair_body(keep, got, *refs):
@@ -365,10 +373,10 @@
 
     x0 = frames[0]
     con = connect.reshape(UNITS, 3).astype(F32)
-    wp, x_late = kernel_call(
+    wp, _ = kernel_call(
         stage_body, (sds((UNITS, PAD_IN), BF), sds(quad, BF)), n_in=2, flops=mac // 64
     )(weights.reshape(UNITS, INPUTS), x0)
-    xs = spread_out(x0, x_late if relay else x0)
+    xs = spread_out(x0, x0)
     wd, wt, st = kernel_call(
         expand_body,
         (sds((UNITS, 3 * PLANE), BF), sds((4, 3 * QUAD, UNITS), BF), sds((3, PAD_STRIP, GRAB), BF)),
@@ -412,11 +420,12 @@
     es = spread_out(e0, e_late if relay else e0)
 
     half = (HALF, PAD_IN)
-    work = [pltpu.VMEM((HALF, PLANE), F32), pltpu.VMEM((HALF, PAD_STRIP), BF)]
+    work = [pltpu.VMEM((HALF, PLANE), F32)] * 3
+    work += [pltpu.VMEM((HALF, PAD_STRIP), BF)] * 3 + [pltpu.VMEM((HALF, GRAB), F32)] * 3
     away, ex = kernel_call(
         away_body,
-        (sds(half, BF), sds((3, PLANE, 2 * batch), BF)),
-        [pltpu.VMEM(plane, BF)] + work + [pltpu.VMEM(half, F32)],
+        (sds(half, BF), sds((3, SPAN, SPAN, 2 * batch), BF)),
+        work,
         n_in=7 + len(es), flops=2 * mac,
     )(wd, left, pull, con, st, xe, e0, *es)
     got = send(away, "dp", flips(n_dp, 1))

time: 95.6 us -> 94.5 us (0.988)
  waiting for transfers between devices: 43.6 us -> 40.3 us
  starting transfers between devices: 34.5 us -> 36.7 us
    ppermute x27, waiting for transfers between devices: 43.6 us -> 40.3 us  [send(): return lax.ppermute(value, axis, pairs)]
    ppermute x27, starting transfers between devices: 34.5 us -> 36.7 us  [send(): return lax.ppermute(value, axis, pairs)]
  transfers between devices with their start and end apart: 27 -> 27, of which waited for: 20 -> 20; matrix products, arithmetic and copies ran while one was open for 1% -> 1% of each run, Pallas kernels for 7% -> 8%
where the time goes in v5:
time: 94.5 us; the launch traced here: 94.2 us
  waiting for transfers between devices  40.3 us (43%)
  starting transfers between devices  36.7 us (39%)
  Pallas kernels  13.4 us (14%)
  local copies, waits for them, and re-layouts  2.33 us (2%)
    ppermute x27, waiting for transfers between devices, send(): return lax.ppermute(value, axis, pairs)  40.3 us
    ppermute x27, starting transfers between devices, send(): return lax.ppermute(value, axis, pairs)  36.7 us
    pallas_call x1, Pallas kernels, local(): kernel_call(expand_body, (sds((UNITS, 3 * PLANE), BF), sds((4, 3 * QUAD,...  3.48 us
    pallas_call x1, Pallas kernels, local(): kernel_call(away_body, (sds(half, BF), sds((3, SPAN, SPAN, 2 * batch), BF...  2.27 us
    unnamed x6, local copies, waits for them, and re-layouts  2.15 us
    pallas_call x1, Pallas kernels, local(): kernel_call(home_body, (sds(half, F32),), work, n_in=6, flops=2 * mac)  2.02 us
  transfers between devices with their start and end apart: 27, of which 20 were waited for; matrix products, arithmetic and copies ran while one was open for 1% of the time, Pallas kernels for 8%

profile of v5, /device:TPU:0, one launch (start us, length us, event | category | flops | bytes accessed | tf_op | source)
XLA Modules:
  0.0 94.2 jit_solution(5489593269288892981)
XLA Ops:
  0.6 4.1 %collective-permute-start = (bf16[3,16,16,128]{3,2,1,0:T(8,128)(2,1)}, bf16[3,16,16,128]{3,2,1,0:T(8,128)(2,1)S(1)}, u32[]{:S(2)}, u32[]{:S(2)}) collective-permute-start(bf16[3,16,16,128]{3,2,1,0:T(8,128)(2,1)} %bitcast.5), channel_id=1, source_target_pairs={{0,2},{3,1},{1,0},{2,3},{4,6},{7,5},{5,4},{6,7},{8,10},{11,9},{9,8... | collective-permute-start | bytes 589832 | tf_op jit(solution)/shard_map/ppermute | solution.py:44
  4.7 1.6 %collective-permute-start.2 = (bf16[3,16,16,128]{3,2,1,0:T(8,128)(2,1)}, bf16[3,16,16,128]{3,2,1,0:T(8,128)(2,1)S(1)}, u32[]{:S(2)}, u32[]{:S(2)}) collective-permute-start(bf16[3,16,16,128]{3,2,1,0:T(8,128)(2,1)} %bitcast.6), channel_id=1, source_target_pairs={{1,2},{2,1},{0,0},{3,3},{5,6},{6,5},{4,4},{7,7},{9,10},{10,9},{8,8... | collective-permute-start | bytes 589832 | tf_op jit(solution)/shard_map/ppermute | solution.py:44
  6.3 2.5 %collective-permute-start.1 = (bf16[3,16,16,128]{3,2,1,0:T(8,128)(2,1)}, bf16[3,16,16,128]{3,2,1,0:T(8,128)(2,1)S(1)}, u32[]{:S(2)}, u32[]{:S(2)}) collective-permute-start(bf16[3,16,16,128]{3,2,1,0:T(8,128)(2,1)} %bitcast.7), channel_id=1, source_target_pairs={{1,3},{2,0},{0,1},{3,2},{5,7},{6,4},{4,5},{7,6},{9,11},{10,8},{8,9... | collective-permute-start | bytes 589832 | tf_op jit(solution)/shard_map/ppermute | solution.py:44
  9.9 2.4 %collective-permute-start.3 = (bf16[3,16,16,128]{3,2,1,0:T(8,128)(2,1)S(1)}, bf16[3,16,16,128]{3,2,1,0:T(8,128)(2,1)S(1)}, u32[]{:S(2)}, u32[]{:S(2)}) collective-permute-start(bf16[3,16,16,128]{3,2,1,0:T(8,128)(2,1)S(1)} %collective-permute-done.refs_0_), channel_id=1, source_target_pairs={{2,3},{1,0},{0,1},{3,2},{6,7},{5,4},{4,5},{7,6},{10,11},{9,8},{8,9... | collective-permute-start | bytes 589832 | tf_op jit(solution)/shard_map/ppermute | solution.py:44
  16.2 3.5 %shard_map.51 = (bf16[512,3072]{1,0:T(8,128)(2,1)S(1)}, bf16[4,768,512]{2,1,0:T(8,128)(2,1)S(1)}, bf16[3,640,512]{2,1,0:T(8,128)(2,1)S(1)}) custom-call(bf16[512,1024]{1,0:T(8,128)(2,1)S(1)} %get-tuple-element.27.wp_ref, f32[512,3]{1,0:T(8,128)S(1)} %bitcast.12), custom_call_target="tpu_custom_call" | custom-call | flops 1610612736 | bytes 6291456 | tf_op jit(solution)/shard_map/pallas_call | solution.py:380
  20.2 1.7 %shard_map.52 = (f32[512,128]{1,0:T(8,128)S(1)}, bf16[3,16,16,128]{3,2,1,0:T(8,128)(2,1)S(1)}) custom-call(bf16[3,16,16,128]{3,2,1,0:T(8,128)(2,1)S(1)} %bitcast.9, bf16[3,16,16,128]{3,2,1,0:T(8,128)(2,1)S(1)} %collective-permute-done.refs_0_, bf16[3,16,16,128]{3,2,1,0:T(8,128)(2,1)S(1)} %collective-permute-done.1.refs_1_, ...), custom_call_target="tpu_custom_call" | custom-call | flops 402653184 | bytes 1572864 | tf_op jit(solution)/shard_map/pallas_call | solution.py:387
  21.9 1.8 %collective-permute-start.6 = (bf16[3,16,16,128]{3,2,1,0:T(8,128)(2,1)S(1)}, bf16[3,16,16,128]{3,2,1,0:T(8,128)(2,1)S(1)}, u32[]{:S(2)}, u32[]{:S(2)}) collective-permute-start(bf16[3,16,16,128]{3,2,1,0:T(8,128)(2,1)S(1)} %get-tuple-element.33), channel_id=1, source_target_pairs={{0,1},{3,2},{4,5},{7,6},{8,9},{11,10},{12,13},{15,14},{16,17},{19,... | collective-permute-start | bytes 589832 | tf_op jit(solution)/shard_map/ppermute | solution.py:44
  24.7 2.1 %collective-permute-start.5 = (bf16[3,16,16,128]{3,2,1,0:T(8,128)(2,1)S(1)}, bf16[3,16,16,128]{3,2,1,0:T(8,128)(2,1)S(1)}, u32[]{:S(2)}, u32[]{:S(2)}) collective-permute-start(bf16[3,16,16,128]{3,2,1,0:T(8,128)(2,1)S(1)} %shard_map.54), channel_id=1, source_target_pairs={{3,1},{0,2},{1,0},{2,3},{7,5},{4,6},{5,4},{6,7},{11,9},{8,10},{9,8... | collective-permute-start | bytes 589832 | tf_op jit(solution)/shard_map/ppermute | solution.py:44
  28.4 2.5 %collective-permute-start.7 = (bf16[3,16,16,128]{3,2,1,0:T(8,128)(2,1)S(1)}, bf16[3,16,16,128]{3,2,1,0:T(8,128)(2,1)S(1)}, u32[]{:S(2)}, u32[]{:S(2)}) collective-permute-start(bf16[3,16,16,128]{3,2,1,0:T(8,128)(2,1)S(1)} %shard_map.55), channel_id=1, source_target_pairs={{2,0},{1,3},{0,1},{3,2},{6,4},{5,7},{4,5},{7,6},{10,8},{9,11},{8,9... | collective-permute-start | bytes 589832 | tf_op jit(solution)/shard_map/ppermute | solution.py:44
  31.0 1.7 %collective-permute-done.5.refs_1_ = bf16[3,16,16,128]{3,2,1,0:T(8,128)(2,1)S(1)} collective-permute-done((bf16[3,16,16,128]{3,2,1,0:T(8,128)(2,1)S(1)}, bf16[3,16,16,128]{3,2,1,0:T(8,128)(2,1)S(1)}, u32[]{:S(2)}, u32[]{:S(2)}) %collective-permute-start.5) | collective-permute-done | bytes 196640 | tf_op jit(solution)/shard_map/ppermute | solution.py:44
  32.7 6.1 %collective-permute-done.7.refs_2_ = bf16[3,16,16,128]{3,2,1,0:T(8,128)(2,1)S(1)} collective-permute-done((bf16[3,16,16,128]{3,2,1,0:T(8,128)(2,1)S(1)}, bf16[3,16,16,128]{3,2,1,0:T(8,128)(2,1)S(1)}, u32[]{:S(2)}, u32[]{:S(2)}) %collective-permute-start.7) | collective-permute-done | bytes 196640 | tf_op jit(solution)/shard_map/ppermute | solution.py:44
  40.1 4.0 %collective-permute-start.9 = (bf16[3,16,16,128]{3,2,1,0:T(8,128)(2,1)S(1)}, bf16[3,16,16,128]{3,2,1,0:T(8,128)(2,1)S(1)}, u32[]{:S(2)}, u32[]{:S(2)}) collective-permute-start(bf16[3,16,16,128]{3,2,1,0:T(8,128)(2,1)S(1)} %get-tuple-element.40), channel_id=1, source_target_pairs={{1,3},{2,0},{0,1},{3,2},{5,7},{6,4},{4,5},{7,6},{9,11},{10,8},{8,9... | collective-permute-start | bytes 589832 | tf_op jit(solution)/shard_map/ppermute | solution.py:44
  45.3 7.9 %collective-permute-done.9.refs_1_ = bf16[3,16,16,128]{3,2,1,0:T(8,128)(2,1)S(1)} collective-permute-done((bf16[3,16,16,128]{3,2,1,0:T(8,128)(2,1)S(1)}, bf16[3,16,16,128]{3,2,1,0:T(8,128)(2,1)S(1)}, u32[]{:S(2)}, u32[]{:S(2)}) %collective-permute-start.9) | collective-permute-done | bytes 196640 | tf_op jit(solution)/shard_map/ppermute | solution.py:44
  54.2 2.3 %shard_map.58 = (bf16[256,1024]{1,0:T(8,128)(2,1)S(1)}, bf16[3,32,32,256]{3,2,1,0:T(8,128)(2,1)S(1)}) custom-call(bf16[512,3072]{1,0:T(8,128)(2,1)S(1)} %get-tuple-element.28.refs_4_.wd_ref, bf16[512,128]{1,0:T(8,128)(2,1)S(1)} %get-tuple-element.36.left_ref, f32[512,128]{1,0:T(8,128)S(1)} %get-tuple-element.37.pull_ref, f32[512,3]{1,0:T(8,128)S(1)} %bitcast.13, ...), custom_call_target="tpu_custom_call" | custom-call | flops 805306368 | bytes 3145728 | tf_op jit(solution)/shard_map/pallas_call | solution.py:425
  56.5 2.0 %shard_map.59.keep = f32[256,1024]{1,0:T(8,128)S(1)} custom-call(bf16[512,3072]{1,0:T(8,128)(2,1)S(1)} %get-tuple-element.28.refs_4_.wd_ref, bf16[512,128]{1,0:T(8,128)(2,1)S(1)} %get-tuple-element.36.left_ref, f32[512,128]{1,0:T(8,128)S(1)} %get-tuple-element.37.pull_ref, f32[512,3]{1,0:T(8,128)S(1)} %bitcast.14, ...), custom_call_target="tpu_custom_call" | custom-call | flops 805306368 | bytes 3145728 | tf_op jit(solution)/shard_map/pallas_call | solution.py:432
  58.7 1.6 %collective-permute-start.13 = (bf16[64,1024]{1,0:T(8,128)(2,1)S(1)}, bf16[64,1024]{1,0:T(8,128)(2,1)S(1)}, u32[]{:S(2)}, u32[]{:S(2)}) collective-permute-start(bf16[64,1024]{1,0:T(8,128)(2,1)S(1)} %get-tuple-element.44), channel_id=1, source_target_pairs={{0,8},{4,12},{8,0},{12,4},{16,24},{20,28},{24,16},{28,20},{1,9},{5... | collective-permute-start | bytes 393224 | tf_op jit(solution)/shard_map/ppermute | solution.py:44
  60.3 1.5 %collective-permute-start.14 = (bf16[64,1024]{1,0:T(8,128)(2,1)S(1)}, bf16[64,1024]{1,0:T(8,128)(2,1)S(1)}, u32[]{:S(2)}, u32[]{:S(2)}) collective-permute-start(bf16[64,1024]{1,0:T(8,128)(2,1)S(1)} %get-tuple-element.45), channel_id=1, source_target_pairs={{0,16},{4,20},{8,24},{12,28},{16,0},{20,4},{24,8},{28,12},{1,17},{... | collective-permute-start | bytes 393224 | tf_op jit(solution)/shard_map/ppermute | solution.py:44
  62.3 2.8 %collective-permute-done.13.refs_0_ = bf16[64,1024]{1,0:T(8,128)(2,1)S(1)} collective-permute-done((bf16[64,1024]{1,0:T(8,128)(2,1)S(1)}, bf16[64,1024]{1,0:T(8,128)(2,1)S(1)}, u32[]{:S(2)}, u32[]{:S(2)}) %collective-permute-start.13) | collective-permute-done | bytes 131104 | tf_op jit(solution)/shard_map/ppermute | solution.py:44
  65.1 3.6 %collective-permute-done.14.refs_1_ = bf16[64,1024]{1,0:T(8,128)(2,1)S(1)} collective-permute-done((bf16[64,1024]{1,0:T(8,128)(2,1)S(1)}, bf16[64,1024]{1,0:T(8,128)(2,1)S(1)}, u32[]{:S(2)}, u32[]{:S(2)}) %collective-permute-start.14) | collective-permute-done | bytes 131104 | tf_op jit(solution)/shard_map/ppermute | solution.py:44
  68.9 1.5 %collective-permute-start.18 = (bf16[64,1024]{1,0:T(8,128)(2,1)S(1)}, bf16[64,1024]{1,0:T(8,128)(2,1)S(1)}, u32[]{:S(2)}, u32[]{:S(2)}) collective-permute-start(bf16[64,1024]{1,0:T(8,128)(2,1)S(1)} %get-tuple-element.48.own), channel_id=1, source_target_pairs={{0,24},{4,28},{8,16},{12,20},{16,8},{20,12},{24,0},{28,4},{1,25},{... | collective-permute-start | bytes 393224 | tf_op jit(solution)/shard_map/ppermute | solution.py:44
  72.4 3.7 %collective-permute-done.18.refs_2_ = bf16[64,1024]{1,0:T(8,128)(2,1)S(1)} collective-permute-done((bf16[64,1024]{1,0:T(8,128)(2,1)S(1)}, bf16[64,1024]{1,0:T(8,128)(2,1)S(1)}, u32[]{:S(2)}, u32[]{:S(2)}) %collective-permute-start.18) | collective-permute-done | bytes 131104 | tf_op jit(solution)/shard_map/ppermute | solution.py:44
  77.6 1.5 %collective-permute-start.22 = (f32[8,128]{1,0:T(8,128)S(1)}, f32[8,128]{1,0:T(8,128)S(1)}, u32[]{:S(2)}, u32[]{:S(2)}) collective-permute-start(f32[8,128]{1,0:T(8,128)S(1)} %get-tuple-element.49.refs_0_), channel_id=1, source_target_pairs={{0,24},{4,28},{8,16},{12,20},{16,8},{20,12},{24,0},{28,4},{1,25},{... | collective-permute-start | bytes 12296 | tf_op jit(solution)/shard_map/ppermute | solution.py:44
  85.3 2.1 %collective-permute-start.26 = (f32[8,128]{1,0:T(8,128)S(1)}, f32[8,128]{1,0:T(8,128)S(1)}, u32[]{:S(2)}, u32[]{:S(2)}) collective-permute-start(f32[8,128]{1,0:T(8,128)S(1)} %shard_map.64.refs_0_), channel_id=1, source_target_pairs={{0,3},{1,0},{2,1},{3,2},{4,7},{5,4},{6,5},{7,6},{8,11},{9,8},{10,9... | collective-permute-start | bytes 12296 | tf_op jit(solution)/shard_map/ppermute | solution.py:44
  89.0 3.0 %collective-permute-done.25.refs_2_ = f32[8,128]{1,0:T(8,128)S(1)} collective-permute-done((f32[8,128]{1,0:T(8,128)S(1)}, f32[8,128]{1,0:T(8,128)S(1)}, u32[]{:S(2)}, u32[]{:S(2)}) %collective-permute-start.25) | collective-permute-done | bytes 4128 | tf_op jit(solution)/shard_map/ppermute | solution.py:44
  (55 shorter events, 25.9 us)
Async XLA Ops:
  0.6 9.3 %collective-permute-start = (bf16[3,16,16,128]{3,2,1,0:T(8,128)(2,1)}, bf16[3,16,16,128]{3,2,1,0:T(8,128)(2,1)S(1)}, u32[]{:S(2)}, u32[]{:S(2)}) collective-permute-start(bf16[3,16,16,128]{3,2,1,0:T(8,128)(2,1)} %bitcast.5), channel_id=1, source_target_pairs={{0,2},{3,1},{1,0},{2,3},{4,6},{7,5},{5,4},{6,7},{8,10},{11,9},{9,8... | collective-permute-start | bytes 589832 | tf_op jit(solution)/shard_map/ppermute | solution.py:44
  4.7 14.9 %collective-permute-start.2 = (bf16[3,16,16,128]{3,2,1,0:T(8,128)(2,1)}, bf16[3,16,16,128]{3,2,1,0:T(8,128)(2,1)S(1)}, u32[]{:S(2)}, u32[]{:S(2)}) collective-permute-start(bf16[3,16,16,128]{3,2,1,0:T(8,128)(2,1)} %bitcast.6), channel_id=1, source_target_pairs={{1,2},{2,1},{0,0},{3,3},{5,6},{6,5},{4,4},{7,7},{9,10},{10,9},{8,8... | collective-permute-start | bytes 589832 | tf_op jit(solution)/shard_map/ppermute | solution.py:44
  6.3 13.3 %collective-permute-start.1 = (bf16[3,16,16,128]{3,2,1,0:T(8,128)(2,1)}, bf16[3,16,16,128]{3,2,1,0:T(8,128)(2,1)S(1)}, u32[]{:S(2)}, u32[]{:S(2)}) collective-permute-start(bf16[3,16,16,128]{3,2,1,0:T(8,128)(2,1)} %bitcast.7), channel_id=1, source_target_pairs={{1,3},{2,0},{0,1},{3,2},{5,7},{6,4},{4,5},{7,6},{9,11},{10,8},{8,9... | collective-permute-start | bytes 589832 | tf_op jit(solution)/shard_map/ppermute | solution.py:44
  9.9 10.3 %collective-permute-start.3 = (bf16[3,16,16,128]{3,2,1,0:T(8,128)(2,1)S(1)}, bf16[3,16,16,128]{3,2,1,0:T(8,128)(2,1)S(1)}, u32[]{:S(2)}, u32[]{:S(2)}) collective-permute-start(bf16[3,16,16,128]{3,2,1,0:T(8,128)(2,1)S(1)} %collective-permute-done.refs_0_), channel_id=1, source_target_pairs={{2,3},{1,0},{0,1},{3,2},{6,7},{5,4},{4,5},{7,6},{10,11},{9,8},{8,9... | collective-permute-start | bytes 589832 | tf_op jit(solution)/shard_map/ppermute | solution.py:44
  21.9 6.5 %collective-permute-start.6 = (bf16[3,16,16,128]{3,2,1,0:T(8,128)(2,1)S(1)}, bf16[3,16,16,128]{3,2,1,0:T(8,128)(2,1)S(1)}, u32[]{:S(2)}, u32[]{:S(2)}) collective-permute-start(bf16[3,16,16,128]{3,2,1,0:T(8,128)(2,1)S(1)} %get-tuple-element.33), channel_id=1, source_target_pairs={{0,1},{3,2},{4,5},{7,6},{8,9},{11,10},{12,13},{15,14},{16,17},{19,... | collective-permute-start | bytes 589832 | tf_op jit(solution)/shard_map/ppermute | solution.py:44
  23.7 9.0 %collective-permute-start.4 = (bf16[3,16,16,128]{3,2,1,0:T(8,128)(2,1)S(1)}, bf16[3,16,16,128]{3,2,1,0:T(8,128)(2,1)S(1)}, u32[]{:S(2)}, u32[]{:S(2)}) collective-permute-start(bf16[3,16,16,128]{3,2,1,0:T(8,128)(2,1)S(1)} %get-tuple-element.33), channel_id=1, source_target_pairs={{1,2},{2,1},{5,6},{6,5},{9,10},{10,9},{13,14},{14,13},{17,18},{18,... | collective-permute-start | bytes 589832 | tf_op jit(solution)/shard_map/ppermute | solution.py:44
  24.7 7.9 %collective-permute-start.5 = (bf16[3,16,16,128]{3,2,1,0:T(8,128)(2,1)S(1)}, bf16[3,16,16,128]{3,2,1,0:T(8,128)(2,1)S(1)}, u32[]{:S(2)}, u32[]{:S(2)}) collective-permute-start(bf16[3,16,16,128]{3,2,1,0:T(8,128)(2,1)S(1)} %shard_map.54), channel_id=1, source_target_pairs={{3,1},{0,2},{1,0},{2,3},{7,5},{4,6},{5,4},{6,7},{11,9},{8,10},{9,8... | collective-permute-start | bytes 589832 | tf_op jit(solution)/shard_map/ppermute | solution.py:44
  28.4 10.3 %collective-permute-start.7 = (bf16[3,16,16,128]{3,2,1,0:T(8,128)(2,1)S(1)}, bf16[3,16,16,128]{3,2,1,0:T(8,128)(2,1)S(1)}, u32[]{:S(2)}, u32[]{:S(2)}) collective-permute-start(bf16[3,16,16,128]{3,2,1,0:T(8,128)(2,1)S(1)} %shard_map.55), channel_id=1, source_target_pairs={{2,0},{1,3},{0,1},{3,2},{6,4},{5,7},{4,5},{7,6},{10,8},{9,11},{8,9... | collective-permute-start | bytes 589832 | tf_op jit(solution)/shard_map/ppermute | solution.py:44
  38.9 5.8 %collective-permute-start.8 = (bf16[3,16,16,128]{3,2,1,0:T(8,128)(2,1)S(1)}, bf16[3,16,16,128]{3,2,1,0:T(8,128)(2,1)S(1)}, u32[]{:S(2)}, u32[]{:S(2)}) collective-permute-start(bf16[3,16,16,128]{3,2,1,0:T(8,128)(2,1)S(1)} %get-tuple-element.35.e_ref), channel_id=1, source_target_pairs={{0,2},{3,1},{1,0},{2,3},{4,6},{7,5},{5,4},{6,7},{8,10},{11,9},{9,8... | collective-permute-start | bytes 589832 | tf_op jit(solution)/shard_map/ppermute | solution.py:44
  39.4 5.9 %collective-permute-start.10 = (bf16[3,16,16,128]{3,2,1,0:T(8,128)(2,1)S(1)}, bf16[3,16,16,128]{3,2,1,0:T(8,128)(2,1)S(1)}, u32[]{:S(2)}, u32[]{:S(2)}) collective-permute-start(bf16[3,16,16,128]{3,2,1,0:T(8,128)(2,1)S(1)} %get-tuple-element.40), channel_id=1, source_target_pairs={{1,2},{2,1},{0,0},{3,3},{5,6},{6,5},{4,4},{7,7},{9,10},{10,9},{8,8... | collective-permute-start | bytes 589832 | tf_op jit(solution)/shard_map/ppermute | solution.py:44
  40.1 13.1 %collective-permute-start.9 = (bf16[3,16,16,128]{3,2,1,0:T(8,128)(2,1)S(1)}, bf16[3,16,16,128]{3,2,1,0:T(8,128)(2,1)S(1)}, u32[]{:S(2)}, u32[]{:S(2)}) collective-permute-start(bf16[3,16,16,128]{3,2,1,0:T(8,128)(2,1)S(1)} %get-tuple-element.40), channel_id=1, source_target_pairs={{1,3},{2,0},{0,1},{3,2},{5,7},{6,4},{4,5},{7,6},{9,11},{10,8},{8,9... | collective-permute-start | bytes 589832 | tf_op jit(solution)/shard_map/ppermute | solution.py:44
  44.7 9.5 %collective-permute-start.11 = (bf16[3,16,16,128]{3,2,1,0:T(8,128)(2,1)S(1)}, bf16[3,16,16,128]{3,2,1,0:T(8,128)(2,1)S(1)}, u32[]{:S(2)}, u32[]{:S(2)}) collective-permute-start(bf16[3,16,16,128]{3,2,1,0:T(8,128)(2,1)S(1)} %collective-permute-done.8.refs_0_), channel_id=1, source_target_pairs={{2,3},{1,0},{0,1},{3,2},{6,7},{5,4},{4,5},{7,6},{10,11},{9,8},{8,9... | collective-permute-start | bytes 589832 | tf_op jit(solution)/shard_map/ppermute | solution.py:44
  58.7 6.4 %collective-permute-start.13 = (bf16[64,1024]{1,0:T(8,128)(2,1)S(1)}, bf16[64,1024]{1,0:T(8,128)(2,1)S(1)}, u32[]{:S(2)}, u32[]{:S(2)}) collective-permute-start(bf16[64,1024]{1,0:T(8,128)(2,1)S(1)} %get-tuple-element.44), channel_id=1, source_target_pairs={{0,8},{4,12},{8,0},{12,4},{16,24},{20,28},{24,16},{28,20},{1,9},{5... | collective-permute-start | bytes 393224 | tf_op jit(solution)/shard_map/ppermute | solution.py:44
  60.3 8.4 %collective-permute-start.14 = (bf16[64,1024]{1,0:T(8,128)(2,1)S(1)}, bf16[64,1024]{1,0:T(8,128)(2,1)S(1)}, u32[]{:S(2)}, u32[]{:S(2)}) collective-permute-start(bf16[64,1024]{1,0:T(8,128)(2,1)S(1)} %get-tuple-element.45), channel_id=1, source_target_pairs={{0,16},{4,20},{8,24},{12,28},{16,0},{20,4},{24,8},{28,12},{1,17},{... | collective-permute-start | bytes 393224 | tf_op jit(solution)/shard_map/ppermute | solution.py:44
  61.8 6.9 %collective-permute-start.15 = (bf16[64,1024]{1,0:T(8,128)(2,1)S(1)}, bf16[64,1024]{1,0:T(8,128)(2,1)S(1)}, u32[]{:S(2)}, u32[]{:S(2)}) collective-permute-start(bf16[64,1024]{1,0:T(8,128)(2,1)S(1)} %get-tuple-element.46), channel_id=1, source_target_pairs={{0,24},{4,28},{8,16},{12,20},{16,8},{20,12},{24,0},{28,4},{1,25},{... | collective-permute-start | bytes 393224 | tf_op jit(solution)/shard_map/ppermute | solution.py:44
  68.9 7.2 %collective-permute-start.18 = (bf16[64,1024]{1,0:T(8,128)(2,1)S(1)}, bf16[64,1024]{1,0:T(8,128)(2,1)S(1)}, u32[]{:S(2)}, u32[]{:S(2)}) collective-permute-start(bf16[64,1024]{1,0:T(8,128)(2,1)S(1)} %get-tuple-element.48.own), channel_id=1, source_target_pairs={{0,24},{4,28},{8,16},{12,20},{16,8},{20,12},{24,0},{28,4},{1,25},{... | collective-permute-start | bytes 393224 | tf_op jit(solution)/shard_map/ppermute | solution.py:44
  70.4 6.9 %collective-permute-start.17 = (bf16[64,1024]{1,0:T(8,128)(2,1)S(1)}, bf16[64,1024]{1,0:T(8,128)(2,1)S(1)}, u32[]{:S(2)}, u32[]{:S(2)}) collective-permute-start(bf16[64,1024]{1,0:T(8,128)(2,1)S(1)} %get-tuple-element.48.own), channel_id=1, source_target_pairs={{0,16},{4,20},{8,24},{12,28},{16,0},{20,4},{24,8},{28,12},{1,17},{... | collective-permute-start | bytes 393224 | tf_op jit(solution)/shard_map/ppermute | solution.py:44
  71.6 5.9 %collective-permute-start.16 = (bf16[64,1024]{1,0:T(8,128)(2,1)S(1)}, bf16[64,1024]{1,0:T(8,128)(2,1)S(1)}, u32[]{:S(2)}, u32[]{:S(2)}) collective-permute-start(bf16[64,1024]{1,0:T(8,128)(2,1)S(1)} %get-tuple-element.48.own), channel_id=1, source_target_pairs={{0,8},{4,12},{8,0},{12,4},{16,24},{20,28},{24,16},{28,20},{1,9},{5... | collective-permute-start | bytes 393224 | tf_op jit(solution)/shard_map/ppermute | solution.py:44
  77.5 15.3 %collective-permute-start.19 = (bf16[256,1024]{1,0:T(8,128)(2,1)S(1)}, bf16[256,1024]{1,0:T(8,128)(2,1)S(1)}, u32[]{:S(2)}, u32[]{:S(2)}) collective-permute-start(bf16[256,1024]{1,0:T(8,128)(2,1)S(1)} %shard_map.62.mine), channel_id=1, source_target_pairs={{0,4},{4,0},{8,12},{12,8},{16,20},{20,16},{24,28},{28,24},{1,5},{5... | collective-permute-start | bytes 1572872 | tf_op jit(solution)/shard_map/ppermute | solution.py:44
  77.6 4.6 %collective-permute-start.22 = (f32[8,128]{1,0:T(8,128)S(1)}, f32[8,128]{1,0:T(8,128)S(1)}, u32[]{:S(2)}, u32[]{:S(2)}) collective-permute-start(f32[8,128]{1,0:T(8,128)S(1)} %get-tuple-element.49.refs_0_), channel_id=1, source_target_pairs={{0,24},{4,28},{8,16},{12,20},{16,8},{20,12},{24,0},{28,4},{1,25},{... | collective-permute-start | bytes 12296 | tf_op jit(solution)/shard_map/ppermute | solution.py:44
  79.1 3.6 %collective-permute-start.21 = (f32[8,128]{1,0:T(8,128)S(1)}, f32[8,128]{1,0:T(8,128)S(1)}, u32[]{:S(2)}, u32[]{:S(2)}) collective-permute-start(f32[8,128]{1,0:T(8,128)S(1)} %get-tuple-element.49.refs_0_), channel_id=1, source_target_pairs={{0,16},{4,20},{8,24},{12,28},{16,0},{20,4},{24,8},{28,12},{1,17},{... | collective-permute-start | bytes 12296 | tf_op jit(solution)/shard_map/ppermute | solution.py:44
  80.6 3.6 %collective-permute-start.20 = (f32[8,128]{1,0:T(8,128)S(1)}, f32[8,128]{1,0:T(8,128)S(1)}, u32[]{:S(2)}, u32[]{:S(2)}) collective-permute-start(f32[8,128]{1,0:T(8,128)S(1)} %get-tuple-element.49.refs_0_), channel_id=1, source_target_pairs={{0,8},{4,12},{8,0},{12,4},{16,24},{20,28},{24,16},{28,20},{1,9},{5... | collective-permute-start | bytes 12296 | tf_op jit(solution)/shard_map/ppermute | solution.py:44
  87.5 4.5 %collective-permute-start.25 = (f32[8,128]{1,0:T(8,128)S(1)}, f32[8,128]{1,0:T(8,128)S(1)}, u32[]{:S(2)}, u32[]{:S(2)}) collective-permute-start(f32[8,128]{1,0:T(8,128)S(1)} %shard_map.64.refs_0_), channel_id=1, source_target_pairs={{0,2},{1,3},{2,0},{3,1},{4,6},{5,7},{6,4},{7,5},{8,10},{9,11},{10,... | collective-permute-start | bytes 12296 | tf_op jit(solution)/shard_map/ppermute | solution.py:44
  87.5 5.4 %collective-permute-start.24 = (f32[8,128]{1,0:T(8,128)S(1)}, f32[8,128]{1,0:T(8,128)S(1)}, u32[]{:S(2)}, u32[]{:S(2)}) collective-permute-start(f32[8,128]{1,0:T(8,128)S(1)} %shard_map.64.refs_0_), channel_id=1, source_target_pairs={{0,1},{1,2},{2,3},{3,0},{4,5},{5,6},{6,7},{7,4},{8,9},{9,10},{10,1... | collective-permute-start | bytes 12296 | tf_op jit(solution)/shard_map/ppermute | solution.py:44
  (6 other events, 13.1 us)

commit v6 on v5

--- a/solution.py
+++ b/solution.py
@@ -451,10 +451,14 @@
         return kernel_call(sum_body, (line,), n_in=len(values), flops=mac // 64)(*values)[0]
 
     across = [flips(n_dp, 2 * x) for x in range(1, chips)]
-    told = in_turn([tally] * (chips - 1), "dp", across)
     others = in_turn([mine] * (chips - 1), "dp", across)
-    tally = add_up(tally, *told)
-    tally = add_up(tally, send(tally, "dp", flips(n_dp, 1)))
+    flip = 2
+    while flip < n_dp:
+        told = send(tally, "dp", flips(n_dp, flip))
+        tally = add_up(tally, told)
+        flip *= 2
+    told = send(tally, "dp", flips(n_dp, 1))
+    tally = add_up(tally, told)
     tallies = in_turn([tally] * (n_tile - 1), "tile", [ring(n_tile, s) for s in range(1, n_tile)])
     tally = add_up(tally)
     (mine_half,) = kernel_call(

time: 94.5 us -> 95.3 us (level)
  waiting for transfers between devices: 40.3 us -> 41.7 us
    ppermute x27 -> x26, waiting for transfers between devices: 40.3 us -> 41.7 us  [send(): return lax.ppermute(value, axis, pairs)]
    ppermute x27 -> x26, starting transfers between devices: 36.7 us -> 36.1 us  [send(): return lax.ppermute(value, axis, pairs)]
  transfers between devices with their start and end apart: 27 -> 26, of which waited for: 20 -> 19; matrix products, arithmetic and copies ran while one was open for 1% -> 1% of each run, Pallas kernels for 8% -> 8%
where the time goes in v6:
time: 95.3 us; the launch traced here: 95 us
  waiting for transfers between devices  41.7 us (44%)
  starting transfers between devices  36.1 us (38%)
  Pallas kernels  13.4 us (14%)
  local copies, waits for them, and re-layouts  2.33 us (2%)
    ppermute x26, waiting for transfers between devices, send(): return lax.ppermute(value, axis, pairs)  41.7 us
    ppermute x26, starting transfers between devices, send(): return lax.ppermute(value, axis, pairs)  36.1 us
    pallas_call x1, Pallas kernels, local(): kernel_call(expand_body, (sds((UNITS, 3 * PLANE), BF), sds((4, 3 * QUAD,...  3.48 us
    pallas_call x1, Pallas kernels, local(): kernel_call(away_body, (sds(half, BF), sds((3, SPAN, SPAN, 2 * batch), BF...  2.27 us
    unnamed x6, local copies, waits for them, and re-layouts  2.15 us
    pallas_call x1, Pallas kernels, local(): kernel_call(home_body, (sds(half, F32),), work, n_in=6, flops=2 * mac)  2.02 us
  transfers between devices with their start and end apart: 26, of which 19 were waited for; matrix products, arithmetic and copies ran while one was open for 1% of the time, Pallas kernels for 8%

profile of v6, /device:TPU:0, one launch (start us, length us, event | category | flops | bytes accessed | tf_op | source)
XLA Modules:
  0.0 95.0 jit_solution(3868627985629939509)
XLA Ops:
  0.6 4.1 %collective-permute-start = (bf16[3,16,16,128]{3,2,1,0:T(8,128)(2,1)}, bf16[3,16,16,128]{3,2,1,0:T(8,128)(2,1)S(1)}, u32[]{:S(2)}, u32[]{:S(2)}) collective-permute-start(bf16[3,16,16,128]{3,2,1,0:T(8,128)(2,1)} %bitcast.5), channel_id=1, source_target_pairs={{0,2},{3,1},{1,0},{2,3},{4,6},{7,5},{5,4},{6,7},{8,10},{11,9},{9,8... | collective-permute-start | bytes 589832 | tf_op jit(solution)/shard_map/ppermute | solution.py:44
  4.7 1.6 %collective-permute-start.2 = (bf16[3,16,16,128]{3,2,1,0:T(8,128)(2,1)}, bf16[3,16,16,128]{3,2,1,0:T(8,128)(2,1)S(1)}, u32[]{:S(2)}, u32[]{:S(2)}) collective-permute-start(bf16[3,16,16,128]{3,2,1,0:T(8,128)(2,1)} %bitcast.6), channel_id=1, source_target_pairs={{1,2},{2,1},{0,0},{3,3},{5,6},{6,5},{4,4},{7,7},{9,10},{10,9},{8,8... | collective-permute-start | bytes 589832 | tf_op jit(solution)/shard_map/ppermute | solution.py:44
  6.3 2.5 %collective-permute-start.1 = (bf16[3,16,16,128]{3,2,1,0:T(8,128)(2,1)}, bf16[3,16,16,128]{3,2,1,0:T(8,128)(2,1)S(1)}, u32[]{:S(2)}, u32[]{:S(2)}) collective-permute-start(bf16[3,16,16,128]{3,2,1,0:T(8,128)(2,1)} %bitcast.7), channel_id=1, source_target_pairs={{1,3},{2,0},{0,1},{3,2},{5,7},{6,4},{4,5},{7,6},{9,11},{10,8},{8,9... | collective-permute-start | bytes 589832 | tf_op jit(solution)/shard_map/ppermute | solution.py:44
  9.9 2.4 %collective-permute-start.3 = (bf16[3,16,16,128]{3,2,1,0:T(8,128)(2,1)S(1)}, bf16[3,16,16,128]{3,2,1,0:T(8,128)(2,1)S(1)}, u32[]{:S(2)}, u32[]{:S(2)}) collective-permute-start(bf16[3,16,16,128]{3,2,1,0:T(8,128)(2,1)S(1)} %collective-permute-done.refs_0_), channel_id=1, source_target_pairs={{2,3},{1,0},{0,1},{3,2},{6,7},{5,4},{4,5},{7,6},{10,11},{9,8},{8,9... | collective-permute-start | bytes 589832 | tf_op jit(solution)/shard_map/ppermute | solution.py:44
  16.2 3.5 %shard_map.51 = (bf16[512,3072]{1,0:T(8,128)(2,1)S(1)}, bf16[4,768,512]{2,1,0:T(8,128)(2,1)S(1)}, bf16[3,640,512]{2,1,0:T(8,128)(2,1)S(1)}) custom-call(bf16[512,1024]{1,0:T(8,128)(2,1)S(1)} %get-tuple-element.27.wp_ref, f32[512,3]{1,0:T(8,128)S(1)} %bitcast.12), custom_call_target="tpu_custom_call" | custom-call | flops 1610612736 | bytes 6291456 | tf_op jit(solution)/shard_map/pallas_call | solution.py:380
  20.2 1.7 %shard_map.52 = (f32[512,128]{1,0:T(8,128)S(1)}, bf16[3,16,16,128]{3,2,1,0:T(8,128)(2,1)S(1)}) custom-call(bf16[3,16,16,128]{3,2,1,0:T(8,128)(2,1)S(1)} %bitcast.9, bf16[3,16,16,128]{3,2,1,0:T(8,128)(2,1)S(1)} %collective-permute-done.refs_0_, bf16[3,16,16,128]{3,2,1,0:T(8,128)(2,1)S(1)} %collective-permute-done.1.refs_1_, ...), custom_call_target="tpu_custom_call" | custom-call | flops 402653184 | bytes 1572864 | tf_op jit(solution)/shard_map/pallas_call | solution.py:387
  21.9 1.8 %collective-permute-start.6 = (bf16[3,16,16,128]{3,2,1,0:T(8,128)(2,1)S(1)}, bf16[3,16,16,128]{3,2,1,0:T(8,128)(2,1)S(1)}, u32[]{:S(2)}, u32[]{:S(2)}) collective-permute-start(bf16[3,16,16,128]{3,2,1,0:T(8,128)(2,1)S(1)} %get-tuple-element.33), channel_id=1, source_target_pairs={{0,1},{3,2},{4,5},{7,6},{8,9},{11,10},{12,13},{15,14},{16,17},{19,... | collective-permute-start | bytes 589832 | tf_op jit(solution)/shard_map/ppermute | solution.py:44
  24.7 2.1 %collective-permute-start.5 = (bf16[3,16,16,128]{3,2,1,0:T(8,128)(2,1)S(1)}, bf16[3,16,16,128]{3,2,1,0:T(8,128)(2,1)S(1)}, u32[]{:S(2)}, u32[]{:S(2)}) collective-permute-start(bf16[3,16,16,128]{3,2,1,0:T(8,128)(2,1)S(1)} %shard_map.54), channel_id=1, source_target_pairs={{3,1},{0,2},{1,0},{2,3},{7,5},{4,6},{5,4},{6,7},{11,9},{8,10},{9,8... | collective-permute-start | bytes 589832 | tf_op jit(solution)/shard_map/ppermute | solution.py:44
  28.4 2.5 %collective-permute-start.7 = (bf16[3,16,16,128]{3,2,1,0:T(8,128)(2,1)S(1)}, bf16[3,16,16,128]{3,2,1,0:T(8,128)(2,1)S(1)}, u32[]{:S(2)}, u32[]{:S(2)}) collective-permute-start(bf16[3,16,16,128]{3,2,1,0:T(8,128)(2,1)S(1)} %shard_map.55), channel_id=1, source_target_pairs={{2,0},{1,3},{0,1},{3,2},{6,4},{5,7},{4,5},{7,6},{10,8},{9,11},{8,9... | collective-permute-start | bytes 589832 | tf_op jit(solution)/shard_map/ppermute | solution.py:44
  31.0 1.7 %collective-permute-done.5.refs_1_ = bf16[3,16,16,128]{3,2,1,0:T(8,128)(2,1)S(1)} collective-permute-done((bf16[3,16,16,128]{3,2,1,0:T(8,128)(2,1)S(1)}, bf16[3,16,16,128]{3,2,1,0:T(8,128)(2,1)S(1)}, u32[]{:S(2)}, u32[]{:S(2)}) %collective-permute-start.5) | collective-permute-done | bytes 196640 | tf_op jit(solution)/shard_map/ppermute | solution.py:44
  32.7 6.1 %collective-permute-done.7.refs_2_ = bf16[3,16,16,128]{3,2,1,0:T(8,128)(2,1)S(1)} collective-permute-done((bf16[3,16,16,128]{3,2,1,0:T(8,128)(2,1)S(1)}, bf16[3,16,16,128]{3,2,1,0:T(8,128)(2,1)S(1)}, u32[]{:S(2)}, u32[]{:S(2)}) %collective-permute-start.7) | collective-permute-done | bytes 196640 | tf_op jit(solution)/shard_map/ppermute | solution.py:44
  40.1 4.0 %collective-permute-start.9 = (bf16[3,16,16,128]{3,2,1,0:T(8,128)(2,1)S(1)}, bf16[3,16,16,128]{3,2,1,0:T(8,128)(2,1)S(1)}, u32[]{:S(2)}, u32[]{:S(2)}) collective-permute-start(bf16[3,16,16,128]{3,2,1,0:T(8,128)(2,1)S(1)} %get-tuple-element.40), channel_id=1, source_target_pairs={{1,3},{2,0},{0,1},{3,2},{5,7},{6,4},{4,5},{7,6},{9,11},{10,8},{8,9... | collective-permute-start | bytes 589832 | tf_op jit(solution)/shard_map/ppermute | solution.py:44
  45.3 7.9 %collective-permute-done.9.refs_1_ = bf16[3,16,16,128]{3,2,1,0:T(8,128)(2,1)S(1)} collective-permute-done((bf16[3,16,16,128]{3,2,1,0:T(8,128)(2,1)S(1)}, bf16[3,16,16,128]{3,2,1,0:T(8,128)(2,1)S(1)}, u32[]{:S(2)}, u32[]{:S(2)}) %collective-permute-start.9) | collective-permute-done | bytes 196640 | tf_op jit(solution)/shard_map/ppermute | solution.py:44
  54.2 2.3 %shard_map.58 = (bf16[256,1024]{1,0:T(8,128)(2,1)S(1)}, bf16[3,32,32,256]{3,2,1,0:T(8,128)(2,1)S(1)}) custom-call(bf16[512,3072]{1,0:T(8,128)(2,1)S(1)} %get-tuple-element.28.refs_4_.wd_ref, bf16[512,128]{1,0:T(8,128)(2,1)S(1)} %get-tuple-element.36.left_ref, f32[512,128]{1,0:T(8,128)S(1)} %get-tuple-element.37.pull_ref, f32[512,3]{1,0:T(8,128)S(1)} %bitcast.13, ...), custom_call_target="tpu_custom_call" | custom-call | flops 805306368 | bytes 3145728 | tf_op jit(solution)/shard_map/pallas_call | solution.py:425
  56.5 2.0 %shard_map.59.keep = f32[256,1024]{1,0:T(8,128)S(1)} custom-call(bf16[512,3072]{1,0:T(8,128)(2,1)S(1)} %get-tuple-element.28.refs_4_.wd_ref, bf16[512,128]{1,0:T(8,128)(2,1)S(1)} %get-tuple-element.36.left_ref, f32[512,128]{1,0:T(8,128)S(1)} %get-tuple-element.37.pull_ref, f32[512,3]{1,0:T(8,128)S(1)} %bitcast.14, ...), custom_call_target="tpu_custom_call" | custom-call | flops 805306368 | bytes 3145728 | tf_op jit(solution)/shard_map/pallas_call | solution.py:432
  58.7 1.6 %collective-permute-start.13 = (bf16[64,1024]{1,0:T(8,128)(2,1)S(1)}, bf16[64,1024]{1,0:T(8,128)(2,1)S(1)}, u32[]{:S(2)}, u32[]{:S(2)}) collective-permute-start(bf16[64,1024]{1,0:T(8,128)(2,1)S(1)} %get-tuple-element.44), channel_id=1, source_target_pairs={{0,8},{4,12},{8,0},{12,4},{16,24},{20,28},{24,16},{28,20},{1,9},{5... | collective-permute-start | bytes 393224 | tf_op jit(solution)/shard_map/ppermute | solution.py:44
  60.3 1.5 %collective-permute-start.14 = (bf16[64,1024]{1,0:T(8,128)(2,1)S(1)}, bf16[64,1024]{1,0:T(8,128)(2,1)S(1)}, u32[]{:S(2)}, u32[]{:S(2)}) collective-permute-start(bf16[64,1024]{1,0:T(8,128)(2,1)S(1)} %get-tuple-element.45), channel_id=1, source_target_pairs={{0,16},{4,20},{8,24},{12,28},{16,0},{20,4},{24,8},{28,12},{1,17},{... | collective-permute-start | bytes 393224 | tf_op jit(solution)/shard_map/ppermute | solution.py:44
  62.3 2.8 %collective-permute-done.13.refs_0_ = bf16[64,1024]{1,0:T(8,128)(2,1)S(1)} collective-permute-done((bf16[64,1024]{1,0:T(8,128)(2,1)S(1)}, bf16[64,1024]{1,0:T(8,128)(2,1)S(1)}, u32[]{:S(2)}, u32[]{:S(2)}) %collective-permute-start.13) | collective-permute-done | bytes 131104 | tf_op jit(solution)/shard_map/ppermute | solution.py:44
  65.1 3.6 %collective-permute-done.14.refs_1_ = bf16[64,1024]{1,0:T(8,128)(2,1)S(1)} collective-permute-done((bf16[64,1024]{1,0:T(8,128)(2,1)S(1)}, bf16[64,1024]{1,0:T(8,128)(2,1)S(1)}, u32[]{:S(2)}, u32[]{:S(2)}) %collective-permute-start.14) | collective-permute-done | bytes 131104 | tf_op jit(solution)/shard_map/ppermute | solution.py:44
  72.4 3.7 %collective-permute-done.18.refs_2_ = bf16[64,1024]{1,0:T(8,128)(2,1)S(1)} collective-permute-done((bf16[64,1024]{1,0:T(8,128)(2,1)S(1)}, bf16[64,1024]{1,0:T(8,128)(2,1)S(1)}, u32[]{:S(2)}, u32[]{:S(2)}) %collective-permute-start.18) | collective-permute-done | bytes 131104 | tf_op jit(solution)/shard_map/ppermute | solution.py:44
  79.1 2.2 %collective-permute-done.20.refs_1_ = f32[8,128]{1,0:T(8,128)S(1)} collective-permute-done((f32[8,128]{1,0:T(8,128)S(1)}, f32[8,128]{1,0:T(8,128)S(1)}, u32[]{:S(2)}, u32[]{:S(2)}) %collective-permute-start.20) | collective-permute-done | bytes 4128 | tf_op jit(solution)/shard_map/ppermute | solution.py:44
  82.7 2.2 %collective-permute-done.21.refs_1_ = f32[8,128]{1,0:T(8,128)S(1)} collective-permute-done((f32[8,128]{1,0:T(8,128)S(1)}, f32[8,128]{1,0:T(8,128)S(1)}, u32[]{:S(2)}, u32[]{:S(2)}) %collective-permute-start.21) | collective-permute-done | bytes 4128 | tf_op jit(solution)/shard_map/ppermute | solution.py:44
  86.1 2.1 %collective-permute-start.25 = (f32[8,128]{1,0:T(8,128)S(1)}, f32[8,128]{1,0:T(8,128)S(1)}, u32[]{:S(2)}, u32[]{:S(2)}) collective-permute-start(f32[8,128]{1,0:T(8,128)S(1)} %shard_map.65.refs_0_), channel_id=1, source_target_pairs={{0,3},{1,0},{2,1},{3,2},{4,7},{5,4},{6,5},{7,6},{8,11},{9,8},{10,9... | collective-permute-start | bytes 12296 | tf_op jit(solution)/shard_map/ppermute | solution.py:44
  89.7 3.0 %collective-permute-done.24.refs_2_ = f32[8,128]{1,0:T(8,128)S(1)} collective-permute-done((f32[8,128]{1,0:T(8,128)S(1)}, f32[8,128]{1,0:T(8,128)S(1)}, u32[]{:S(2)}, u32[]{:S(2)}) %collective-permute-start.24) | collective-permute-done | bytes 4128 | tf_op jit(solution)/shard_map/ppermute | solution.py:44
  (54 shorter events, 25.2 us)
Async XLA Ops:
  0.6 9.3 %collective-permute-start = (bf16[3,16,16,128]{3,2,1,0:T(8,128)(2,1)}, bf16[3,16,16,128]{3,2,1,0:T(8,128)(2,1)S(1)}, u32[]{:S(2)}, u32[]{:S(2)}) collective-permute-start(bf16[3,16,16,128]{3,2,1,0:T(8,128)(2,1)} %bitcast.5), channel_id=1, source_target_pairs={{0,2},{3,1},{1,0},{2,3},{4,6},{7,5},{5,4},{6,7},{8,10},{11,9},{9,8... | collective-permute-start | bytes 589832 | tf_op jit(solution)/shard_map/ppermute | solution.py:44
  4.7 14.9 %collective-permute-start.2 = (bf16[3,16,16,128]{3,2,1,0:T(8,128)(2,1)}, bf16[3,16,16,128]{3,2,1,0:T(8,128)(2,1)S(1)}, u32[]{:S(2)}, u32[]{:S(2)}) collective-permute-start(bf16[3,16,16,128]{3,2,1,0:T(8,128)(2,1)} %bitcast.6), channel_id=1, source_target_pairs={{1,2},{2,1},{0,0},{3,3},{5,6},{6,5},{4,4},{7,7},{9,10},{10,9},{8,8... | collective-permute-start | bytes 589832 | tf_op jit(solution)/shard_map/ppermute | solution.py:44
  6.3 13.3 %collective-permute-start.1 = (bf16[3,16,16,128]{3,2,1,0:T(8,128)(2,1)}, bf16[3,16,16,128]{3,2,1,0:T(8,128)(2,1)S(1)}, u32[]{:S(2)}, u32[]{:S(2)}) collective-permute-start(bf16[3,16,16,128]{3,2,1,0:T(8,128)(2,1)} %bitcast.7), channel_id=1, source_target_pairs={{1,3},{2,0},{0,1},{3,2},{5,7},{6,4},{4,5},{7,6},{9,11},{10,8},{8,9... | collective-permute-start | bytes 589832 | tf_op jit(solution)/shard_map/ppermute | solution.py:44
  9.9 10.3 %collective-permute-start.3 = (bf16[3,16,16,128]{3,2,1,0:T(8,128)(2,1)S(1)}, bf16[3,16,16,128]{3,2,1,0:T(8,128)(2,1)S(1)}, u32[]{:S(2)}, u32[]{:S(2)}) collective-permute-start(bf16[3,16,16,128]{3,2,1,0:T(8,128)(2,1)S(1)} %collective-permute-done.refs_0_), channel_id=1, source_target_pairs={{2,3},{1,0},{0,1},{3,2},{6,7},{5,4},{4,5},{7,6},{10,11},{9,8},{8,9... | collective-permute-start | bytes 589832 | tf_op jit(solution)/shard_map/ppermute | solution.py:44
  21.9 6.5 %collective-permute-start.6 = (bf16[3,16,16,128]{3,2,1,0:T(8,128)(2,1)S(1)}, bf16[3,16,16,128]{3,2,1,0:T(8,128)(2,1)S(1)}, u32[]{:S(2)}, u32[]{:S(2)}) collective-permute-start(bf16[3,16,16,128]{3,2,1,0:T(8,128)(2,1)S(1)} %get-tuple-element.33), channel_id=1, source_target_pairs={{0,1},{3,2},{4,5},{7,6},{8,9},{11,10},{12,13},{15,14},{16,17},{19,... | collective-permute-start | bytes 589832 | tf_op jit(solution)/shard_map/ppermute | solution.py:44
  23.7 9.0 %collective-permute-start.4 = (bf16[3,16,16,128]{3,2,1,0:T(8,128)(2,1)S(1)}, bf16[3,16,16,128]{3,2,1,0:T(8,128)(2,1)S(1)}, u32[]{:S(2)}, u32[]{:S(2)}) collective-permute-start(bf16[3,16,16,128]{3,2,1,0:T(8,128)(2,1)S(1)} %get-tuple-element.33), channel_id=1, source_target_pairs={{1,2},{2,1},{5,6},{6,5},{9,10},{10,9},{13,14},{14,13},{17,18},{18,... | collective-permute-start | bytes 589832 | tf_op jit(solution)/shard_map/ppermute | solution.py:44
  24.7 7.9 %collective-permute-start.5 = (bf16[3,16,16,128]{3,2,1,0:T(8,128)(2,1)S(1)}, bf16[3,16,16,128]{3,2,1,0:T(8,128)(2,1)S(1)}, u32[]{:S(2)}, u32[]{:S(2)}) collective-permute-start(bf16[3,16,16,128]{3,2,1,0:T(8,128)(2,1)S(1)} %shard_map.54), channel_id=1, source_target_pairs={{3,1},{0,2},{1,0},{2,3},{7,5},{4,6},{5,4},{6,7},{11,9},{8,10},{9,8... | collective-permute-start | bytes 589832 | tf_op jit(solution)/shard_map/ppermute | solution.py:44
  28.4 10.3 %collective-permute-start.7 = (bf16[3,16,16,128]{3,2,1,0:T(8,128)(2,1)S(1)}, bf16[3,16,16,128]{3,2,1,0:T(8,128)(2,1)S(1)}, u32[]{:S(2)}, u32[]{:S(2)}) collective-permute-start(bf16[3,16,16,128]{3,2,1,0:T(8,128)(2,1)S(1)} %shard_map.55), channel_id=1, source_target_pairs={{2,0},{1,3},{0,1},{3,2},{6,4},{5,7},{4,5},{7,6},{10,8},{9,11},{8,9... | collective-permute-start | bytes 589832 | tf_op jit(solution)/shard_map/ppermute | solution.py:44
  38.9 5.8 %collective-permute-start.8 = (bf16[3,16,16,128]{3,2,1,0:T(8,128)(2,1)S(1)}, bf16[3,16,16,128]{3,2,1,0:T(8,128)(2,1)S(1)}, u32[]{:S(2)}, u32[]{:S(2)}) collective-permute-start(bf16[3,16,16,128]{3,2,1,0:T(8,128)(2,1)S(1)} %get-tuple-element.35.e_ref), channel_id=1, source_target_pairs={{0,2},{3,1},{1,0},{2,3},{4,6},{7,5},{5,4},{6,7},{8,10},{11,9},{9,8... | collective-permute-start | bytes 589832 | tf_op jit(solution)/shard_map/ppermute | solution.py:44
  39.4 5.9 %collective-permute-start.10 = (bf16[3,16,16,128]{3,2,1,0:T(8,128)(2,1)S(1)}, bf16[3,16,16,128]{3,2,1,0:T(8,128)(2,1)S(1)}, u32[]{:S(2)}, u32[]{:S(2)}) collective-permute-start(bf16[3,16,16,128]{3,2,1,0:T(8,128)(2,1)S(1)} %get-tuple-element.40), channel_id=1, source_target_pairs={{1,2},{2,1},{0,0},{3,3},{5,6},{6,5},{4,4},{7,7},{9,10},{10,9},{8,8... | collective-permute-start | bytes 589832 | tf_op jit(solution)/shard_map/ppermute | solution.py:44
  40.1 13.1 %collective-permute-start.9 = (bf16[3,16,16,128]{3,2,1,0:T(8,128)(2,1)S(1)}, bf16[3,16,16,128]{3,2,1,0:T(8,128)(2,1)S(1)}, u32[]{:S(2)}, u32[]{:S(2)}) collective-permute-start(bf16[3,16,16,128]{3,2,1,0:T(8,128)(2,1)S(1)} %get-tuple-element.40), channel_id=1, source_target_pairs={{1,3},{2,0},{0,1},{3,2},{5,7},{6,4},{4,5},{7,6},{9,11},{10,8},{8,9... | collective-permute-start | bytes 589832 | tf_op jit(solution)/shard_map/ppermute | solution.py:44
  44.7 9.5 %collective-permute-start.11 = (bf16[3,16,16,128]{3,2,1,0:T(8,128)(2,1)S(1)}, bf16[3,16,16,128]{3,2,1,0:T(8,128)(2,1)S(1)}, u32[]{:S(2)}, u32[]{:S(2)}) collective-permute-start(bf16[3,16,16,128]{3,2,1,0:T(8,128)(2,1)S(1)} %collective-permute-done.8.refs_0_), channel_id=1, source_target_pairs={{2,3},{1,0},{0,1},{3,2},{6,7},{5,4},{4,5},{7,6},{10,11},{9,8},{8,9... | collective-permute-start | bytes 589832 | tf_op jit(solution)/shard_map/ppermute | solution.py:44
  58.7 6.4 %collective-permute-start.13 = (bf16[64,1024]{1,0:T(8,128)(2,1)S(1)}, bf16[64,1024]{1,0:T(8,128)(2,1)S(1)}, u32[]{:S(2)}, u32[]{:S(2)}) collective-permute-start(bf16[64,1024]{1,0:T(8,128)(2,1)S(1)} %get-tuple-element.44), channel_id=1, source_target_pairs={{0,8},{4,12},{8,0},{12,4},{16,24},{20,28},{24,16},{28,20},{1,9},{5... | collective-permute-start | bytes 393224 | tf_op jit(solution)/shard_map/ppermute | solution.py:44
  60.3 8.4 %collective-permute-start.14 = (bf16[64,1024]{1,0:T(8,128)(2,1)S(1)}, bf16[64,1024]{1,0:T(8,128)(2,1)S(1)}, u32[]{:S(2)}, u32[]{:S(2)}) collective-permute-start(bf16[64,1024]{1,0:T(8,128)(2,1)S(1)} %get-tuple-element.45), channel_id=1, source_target_pairs={{0,16},{4,20},{8,24},{12,28},{16,0},{20,4},{24,8},{28,12},{1,17},{... | collective-permute-start | bytes 393224 | tf_op jit(solution)/shard_map/ppermute | solution.py:44
  61.8 6.9 %collective-permute-start.15 = (bf16[64,1024]{1,0:T(8,128)(2,1)S(1)}, bf16[64,1024]{1,0:T(8,128)(2,1)S(1)}, u32[]{:S(2)}, u32[]{:S(2)}) collective-permute-start(bf16[64,1024]{1,0:T(8,128)(2,1)S(1)} %get-tuple-element.46), channel_id=1, source_target_pairs={{0,24},{4,28},{8,16},{12,20},{16,8},{20,12},{24,0},{28,4},{1,25},{... | collective-permute-start | bytes 393224 | tf_op jit(solution)/shard_map/ppermute | solution.py:44
  68.9 7.2 %collective-permute-start.18 = (bf16[64,1024]{1,0:T(8,128)(2,1)S(1)}, bf16[64,1024]{1,0:T(8,128)(2,1)S(1)}, u32[]{:S(2)}, u32[]{:S(2)}) collective-permute-start(bf16[64,1024]{1,0:T(8,128)(2,1)S(1)} %get-tuple-element.48.own), channel_id=1, source_target_pairs={{0,24},{4,28},{8,16},{12,20},{16,8},{20,12},{24,0},{28,4},{1,25},{... | collective-permute-start | bytes 393224 | tf_op jit(solution)/shard_map/ppermute | solution.py:44
  70.4 6.9 %collective-permute-start.17 = (bf16[64,1024]{1,0:T(8,128)(2,1)S(1)}, bf16[64,1024]{1,0:T(8,128)(2,1)S(1)}, u32[]{:S(2)}, u32[]{:S(2)}) collective-permute-start(bf16[64,1024]{1,0:T(8,128)(2,1)S(1)} %get-tuple-element.48.own), channel_id=1, source_target_pairs={{0,16},{4,20},{8,24},{12,28},{16,0},{20,4},{24,8},{28,12},{1,17},{... | collective-permute-start | bytes 393224 | tf_op jit(solution)/shard_map/ppermute | solution.py:44
  71.6 5.9 %collective-permute-start.16 = (bf16[64,1024]{1,0:T(8,128)(2,1)S(1)}, bf16[64,1024]{1,0:T(8,128)(2,1)S(1)}, u32[]{:S(2)}, u32[]{:S(2)}) collective-permute-start(bf16[64,1024]{1,0:T(8,128)(2,1)S(1)} %get-tuple-element.48.own), channel_id=1, source_target_pairs={{0,8},{4,12},{8,0},{12,4},{16,24},{20,28},{24,16},{28,20},{1,9},{5... | collective-permute-start | bytes 393224 | tf_op jit(solution)/shard_map/ppermute | solution.py:44
  77.5 16.1 %collective-permute-start.19 = (bf16[256,1024]{1,0:T(8,128)(2,1)S(1)}, bf16[256,1024]{1,0:T(8,128)(2,1)S(1)}, u32[]{:S(2)}, u32[]{:S(2)}) collective-permute-start(bf16[256,1024]{1,0:T(8,128)(2,1)S(1)} %shard_map.62.mine), channel_id=1, source_target_pairs={{0,4},{4,0},{8,12},{12,8},{16,20},{20,16},{24,28},{28,24},{1,5},{5... | collective-permute-start | bytes 1572872 | tf_op jit(solution)/shard_map/ppermute | solution.py:44
  77.6 3.7 %collective-permute-start.20 = (f32[8,128]{1,0:T(8,128)S(1)}, f32[8,128]{1,0:T(8,128)S(1)}, u32[]{:S(2)}, u32[]{:S(2)}) collective-permute-start(f32[8,128]{1,0:T(8,128)S(1)} %get-tuple-element.49.refs_0_), channel_id=1, source_target_pairs={{0,8},{4,12},{8,0},{12,4},{16,24},{20,28},{24,16},{28,20},{1,9},{5... | collective-permute-start | bytes 12296 | tf_op jit(solution)/shard_map/ppermute | solution.py:44
  81.3 3.6 %collective-permute-start.21 = (f32[8,128]{1,0:T(8,128)S(1)}, f32[8,128]{1,0:T(8,128)S(1)}, u32[]{:S(2)}, u32[]{:S(2)}) collective-permute-start(f32[8,128]{1,0:T(8,128)S(1)} %shard_map.63.refs_0_), channel_id=1, source_target_pairs={{0,16},{4,20},{8,24},{12,28},{16,0},{20,4},{24,8},{28,12},{1,17},{... | collective-permute-start | bytes 12296 | tf_op jit(solution)/shard_map/ppermute | solution.py:44
  86.1 3.6 %collective-permute-start.25 = (f32[8,128]{1,0:T(8,128)S(1)}, f32[8,128]{1,0:T(8,128)S(1)}, u32[]{:S(2)}, u32[]{:S(2)}) collective-permute-start(f32[8,128]{1,0:T(8,128)S(1)} %shard_map.65.refs_0_), channel_id=1, source_target_pairs={{0,3},{1,0},{2,1},{3,2},{4,7},{5,4},{6,5},{7,6},{8,11},{9,8},{10,9... | collective-permute-start | bytes 12296 | tf_op jit(solution)/shard_map/ppermute | solution.py:44
  88.2 4.5 %collective-permute-start.24 = (f32[8,128]{1,0:T(8,128)S(1)}, f32[8,128]{1,0:T(8,128)S(1)}, u32[]{:S(2)}, u32[]{:S(2)}) collective-permute-start(f32[8,128]{1,0:T(8,128)S(1)} %shard_map.65.refs_0_), channel_id=1, source_target_pairs={{0,2},{1,3},{2,0},{3,1},{4,6},{5,7},{6,4},{7,5},{8,10},{9,11},{10,... | collective-permute-start | bytes 12296 | tf_op jit(solution)/shard_map/ppermute | solution.py:44
  88.2 5.4 %collective-permute-start.23 = (f32[8,128]{1,0:T(8,128)S(1)}, f32[8,128]{1,0:T(8,128)S(1)}, u32[]{:S(2)}, u32[]{:S(2)}) collective-permute-start(f32[8,128]{1,0:T(8,128)S(1)} %shard_map.65.refs_0_), channel_id=1, source_target_pairs={{0,1},{1,2},{2,3},{3,0},{4,5},{5,6},{6,7},{7,4},{8,9},{9,10},{10,1... | collective-permute-start | bytes 12296 | tf_op jit(solution)/shard_map/ppermute | solution.py:44
  (5 other events, 9.4 us)
